TPU v7x, 256 devices: a whole 4x4x8 slice. The times are simulated.
256 devices in a mesh: rows: 32 (over x_lo, z, core), freq: 8 (over y, x_hi).
Axes of the slice: x: 4 (x_hi: 2, x_lo: 2; x = x_hi * 2 + x_lo), y: 4, z: 8, core: 2. Of those that a mesh axis runs over, the one named last changes fastest.
Arguments:
- design: float32 [256, 65536], P('rows'), may hold values from 0.05 to 0.95
- passive: int32 [256, 65536], P('rows'), may hold values 0 or 1
- state: bfloat16 [2, 8, 256, 65536], P(None, 'freq', 'rows'), may hold values from -36 to 36
- adjoint: bfloat16 [2, 8, 256, 65536], P(None, 'freq', 'rows'), may hold values from -36 to 36
- omega_sq: float32 [8], replicated, may hold values from 0.05 to 2
- assign: int32 [8], P('freq'), may hold values from 0 to 7, each once
Outputs:
- gradient: float32 [256, 65536], P('rows')
Inputs may be any that keep to these rules, and one draw needn't show every extreme that they name: `assign`: each of 0 .. 7 appears once.
All inputs are finite; a program needn't handle non-finite values. No bound on the sum of `passive` on one device may be relied on, other than what follows from the above.
Results may differ from a plain program's by a relative error of at most 0.0003.
Values may be sent and summed in bfloat16 or wider, within the bound.
No kernel may reach another device: no remote copies, remote signals or barrier semaphores. Data moves between devices by JAX's collectives and lax.ppermute only.
A program may use at most 128 MiB of HBM per device.

v0:
```python
import jax
import jax.numpy as jnp
from jax import lax
from jax.sharding import PartitionSpec as P

RADIUS = 8


sharpness = 8.0
threshold = 0.5
exponent = 3.0
soft_floor = 0.001
loss_factor = 0.2
epsilon = 1e-06
stiff_table = [
    [4.0 / 6, -1.0 / 6, -1.0 / 6, -2.0 / 6],
    [-1.0 / 6, 4.0 / 6, -2.0 / 6, -1.0 / 6],
    [-1.0 / 6, -2.0 / 6, 4.0 / 6, -1.0 / 6],
    [-2.0 / 6, -1.0 / 6, -1.0 / 6, 4.0 / 6],
]
mass_table = [
    [4.0 / 36, 2.0 / 36, 2.0 / 36, 1.0 / 36],
    [2.0 / 36, 4.0 / 36, 1.0 / 36, 2.0 / 36],
    [2.0 / 36, 1.0 / 36, 4.0 / 36, 2.0 / 36],
    [1.0 / 36, 2.0 / 36, 2.0 / 36, 4.0 / 36],
]


def extended(block, sides, width):
    for axis, dim in sides:
        count = lax.axis_size(axis)
        forward = [(i, i + 1) for i in range(count - 1)]
        backward = [(target, source) for source, target in forward]
        low = lax.ppermute(
            lax.slice_in_dim(block, block.shape[dim] - width, None, axis=dim), axis, forward
        )
        high = lax.ppermute(lax.slice_in_dim(block, 0, width, axis=dim), axis, backward)
        block = jnp.concatenate([low, block, high], axis=dim)
    return block


def from_behind(block, axis, distance):
    devices = range(lax.axis_size(axis))
    route = [(i - distance, i) for i in devices if i - distance in devices]
    return lax.ppermute(block, axis, route)


def in_blocks(shard, dim, peers):
    lengths = shard.shape
    blocks = shard.reshape(*lengths[:dim], peers, lengths[dim] // peers, *lengths[dim + 1 :])
    return jnp.moveaxis(blocks, dim, 0)


def sent_and_summed(shard, axis, dim):
    peers = lax.axis_size(axis)
    blocks = lax.all_to_all(in_blocks(shard, dim, peers), axis, 0, 0, tiled=True)
    return jnp.sum(blocks, axis=0)


def from_everyone(shard, axis):
    peers = lax.axis_size(axis)
    return lax.all_to_all(
        jnp.broadcast_to(shard[None], (peers, *shard.shape)), axis, 0, 0, tiled=True
    )


def in_order(blocks, dim):
    blocks = jnp.moveaxis(blocks, 0, dim)
    lengths = blocks.shape
    return blocks.reshape(*lengths[:dim], lengths[dim] * lengths[dim + 1], *lengths[dim + 2 :])


def gathered_copies(shard, axis, dim):
    blocks = from_everyone(shard, axis)
    return in_order(blocks, dim)


def of_everyone(shard, axis):
    everything = from_everyone(shard, axis)
    return jnp.sum(everything, axis=0)


def tap_list():
    return [float(RADIUS + 1 - abs(offset)) for offset in range(-RADIUS, RADIUS + 1)]


def row_pass(padded, count):
    taps = tap_list()
    total = taps[0] * padded[0:count]
    for offset in range(1, 2 * RADIUS + 1):
        total = total + taps[offset] * padded[offset : offset + count]
    return total


def col_pass(field):
    taps = tap_list()
    count = field.shape[1]
    padded = jnp.pad(field, ((0, 0), (RADIUS, RADIUS)))
    total = taps[0] * padded[:, 0:count]
    for offset in range(1, 2 * RADIUS + 1):
        total = total + taps[offset] * padded[:, offset : offset + count]
    return total


def edge_sums(start, count, whole):
    positions = start + jnp.arange(count, dtype=jnp.int32)
    total = jnp.zeros((count,), jnp.float32)
    for offset in range(-RADIUS, RADIUS + 1):
        inside = ((positions + offset >= 0) & (positions + offset < whole)).astype(jnp.float32)
        total = total + float(RADIUS + 1 - abs(offset)) * inside
    return total


def project(tilde, passive):
    bottom = jnp.tanh(sharpness * threshold) + jnp.tanh(sharpness * (1.0 - threshold))
    steep = jnp.tanh(sharpness * (tilde - threshold))
    value = (jnp.tanh(sharpness * threshold) + steep) / bottom
    slope = sharpness * (1.0 - steep * steep) / bottom
    solid = passive > 0
    density = jnp.where(solid, 1.0, value)
    slope = jnp.where(solid, 0.0, slope)
    stiffness = exponent * density * density * (1.0 - soft_floor)
    return (stiffness, slope)


def bilinear(table, left, right):
    total = None
    for row_pos in range(4):
        inner = table[row_pos][0] * right[0]
        for col_pos in range(1, 4):
            inner = inner + table[row_pos][col_pos] * right[col_pos]
        term = left[row_pos] * inner
        total = term if total is None else total + term
    return total


def corners(nodes, below):
    stacked = jnp.concatenate([nodes, below], axis=0)
    right_col = jnp.zeros((stacked.shape[0], 1), stacked.dtype)
    shifted = jnp.concatenate([stacked[:, 1:], right_col], axis=1)
    return (stacked[:-1], shifted[:-1], stacked[1:], shifted[1:])


def element_terms(fields, fields_below, duals, duals_below, stiffness, omega):
    state_real = corners(fields[0], fields_below[0])
    state_imag = corners(fields[1], fields_below[1])
    adjoint_real = corners(duals[0], duals_below[0])
    adjoint_imag = corners(duals[1], duals_below[1])
    elastic = bilinear(stiff_table, adjoint_real, state_real) - bilinear(
        stiff_table, adjoint_imag, state_imag
    )
    damped = bilinear(stiff_table, adjoint_real, state_imag) + bilinear(
        stiff_table, adjoint_imag, state_real
    )
    inertia = bilinear(mass_table, adjoint_real, state_real) - bilinear(
        mass_table, adjoint_imag, state_imag
    )
    return stiffness * (elastic - loss_factor * damped) - omega * inertia


def shards(design, passive, state, adjoint, omega_sq, assign):
    slab_rows, width = design.shape
    whole_rows = slab_rows * lax.axis_size("rows")
    top = lax.axis_index("rows") * slab_rows
    weight_sum = (
        edge_sums(top, slab_rows, whole_rows)[:, None] * edge_sums(0, width, width)[None, :]
    )
    padded = extended(design, (("rows", 0),), RADIUS)
    tilde = col_pass(row_pass(padded, slab_rows)) / weight_sum
    stiffness, slope = project(tilde, passive)
    factor = slope / weight_sum
    below_state, below_adjoint = from_behind((state[:, :, :1, :], adjoint[:, :, :1, :]), "rows", -1)
    table = jnp.arange(omega_sq.shape[0], dtype=jnp.int32)
    picked = (assign[:, None] == table[None, :]).astype(jnp.float32)
    omegas = jnp.sum(picked * omega_sq[None, :], axis=1)

    def accumulate(slot, total):
        fields = lax.dynamic_index_in_dim(state, slot, 1, keepdims=False).astype(jnp.float32)
        duals = lax.dynamic_index_in_dim(adjoint, slot, 1, keepdims=False).astype(jnp.float32)
        fields_below = lax.dynamic_index_in_dim(below_state, slot, 1, keepdims=False).astype(
            jnp.float32
        )
        duals_below = lax.dynamic_index_in_dim(below_adjoint, slot, 1, keepdims=False).astype(
            jnp.float32
        )
        omega = lax.dynamic_index_in_dim(omegas, slot, 0, keepdims=False)
        return total + element_terms(fields, fields_below, duals, duals_below, stiffness, omega)

    local = lax.fori_loop(0, state.shape[1], accumulate, jnp.zeros((slab_rows, width), jnp.float32))
    share = sent_and_summed(local, "freq", 1)
    piece_cols = share.shape[1]
    start = lax.axis_index("freq") * piece_cols
    spread = share * lax.dynamic_slice_in_dim(factor, start, piece_cols, 1)
    padded_back = extended(spread, (("rows", 0),), RADIUS)
    rowed = row_pass(padded_back, slab_rows)
    joined = gathered_copies(rowed, "freq", 1)
    back = col_pass(joined)
    total = of_everyone(jnp.sum(back * back), "rows")
    return back * lax.rsqrt(total / (whole_rows * width) + epsilon)


def solution(mesh):
    return jax.shard_map(
        shards,
        mesh=mesh,
        in_specs=(
            P("rows", None),
            P("rows", None),
            P(None, "freq", "rows", None),
            P(None, "freq", "rows", None),
            P(),
            P("freq"),
        ),
        out_specs=P("rows", None),
        check_vma=False,
    )
```

profile of v0, /device:TPU:1, one launch (start us, length us, event | category | flops | bytes accessed | tf_op | source)
XLA Modules:
  0.0 214.9 jit_solution(5700033274319038545)
XLA Ops:
  0.0 5.0 %collective-permute-start = (f32[8,65536]{1,0:T(8,128)}, f32[8,65536]{1,0:T(8,128)}, u32[]{:S(2)}, u32[]{:S(2)}) collective-permute-start(f32[8,65536]{1,0:T(8,128)} %param.6), channel_id=1, source_target_pairs={{0,8},{8,16},{16,24},{24,32},{32,40},{40,48},{48,56},{56,64},{64,7... | collective-permute-start | bytes 6291464 | tf_op jit(solution)/shard_map/ppermute | solution.py:34
  5.1 2.8 %collective-permute-start.1 = (f32[8,65536]{1,0:T(8,128)}, f32[8,65536]{1,0:T(8,128)}, u32[]{:S(2)}, u32[]{:S(2)}) collective-permute-start(f32[8,65536]{1,0:T(8,128)} %param.6), channel_id=1, source_target_pairs={{8,0},{16,8},{24,16},{32,24},{40,32},{48,40},{56,48},{64,56},{72,6... | collective-permute-start | bytes 6291464 | tf_op jit(solution)/shard_map/ppermute | solution.py:37
  7.9 1.9 slice.352
  10.2 1.9 collective-permute-start.2
  12.1 1.9 slice.358
  14.4 2.1 collective-permute-start.3
  17.0 1.6 slice_bitcast_fusion.2
  18.6 2.2 %slice_bitcast_fusion.3 = (f32[8,65536]{1,0:T(8,128)}, f32[8,65536]{1,0:T(8,128)}) fusion(f32[2,1,8,65536]{3,2,1,0:T(8,128)S(1)} %convert_element_type.102), kind=kLoop, calls=%fused_computation.40 | loop fusion | bytes 8388608 | tf_op jit(solution)/shard_map/while/body/eval_jaxpr/squeeze | solution.py:147
  22.2 13.2 %collective-permute-done.2 = bf16[2,1,1,65536]{3,0,2,1:T(2,128)(2,1)S(1)} collective-permute-done((bf16[2,1,1,65536]{3,0,2,1:T(2,128)(2,1)S(1)}, bf16[2,1,1,65536]{3,0,2,1:T(2,128)(2,1)S(1)}, u32[]{:S(2)}, u32[]{:S(2)}) %collective-permute-start.2) | collective-permute-done | bytes 262176 | tf_op jit(solution)/shard_map/ppermute | solution.py:45
  36.0 2.3 %collective-permute-done.3 = bf16[2,1,1,65536]{3,0,2,1:T(2,128)(2,1)} collective-permute-done((bf16[2,1,1,65536]{3,0,2,1:T(2,128)(2,1)S(1)}, bf16[2,1,1,65536]{3,0,2,1:T(2,128)(2,1)}, u32[]{:S(2)}, u32[]{:S(2)}) %collective-permute-start.3) | collective-permute-done | bytes 262176 | tf_op jit(solution)/shard_map/ppermute | solution.py:45
  39.9 6.6 %slice_maximum_fusion = (f32[9,65535]{1,0:T(8,128)}, f32[9,65535]{1,0:T(8,128)}) fusion(f32[1,65536]{1,0:T(1,128)S(1)} %get-tuple-element.46, f32[8,65536]{1,0:T(8,128)} %get-tuple-element.36, f32[1,65536]{1,0:T(1,128)S(1)} %get-tuple-element.45, f32[8,65536]{1,0:T(8,128)S(1)} %copy-done.1), kind=kLoop, calls=%fused_computation | loop fusion | flops 1179630 | bytes 9437112 | tf_op jit(solution)/shard_map/while/body/eval_jaxpr/concatenate | solution.py:138
  46.5 4.8 %slice_maximum_fusion.1 = (f32[9,65535]{1,0:T(8,128)}, f32[9,65535]{1,0:T(8,128)}) fusion(f32[1,65536]{1,0:T(1,128)S(1)} %get-tuple-element.44, f32[8,65536]{1,0:T(8,128)S(1)} %copy-done, f32[1,65536]{1,0:T(1,128)S(1)} %get-tuple-element.43, f32[8,65536]{1,0:T(8,128)S(1)} %get-tuple-element.38), kind=kLoop, calls=%fused_computation.1 | loop fusion | flops 1179630 | bytes 9437112 | tf_op jit(solution)/shard_map/while/body/eval_jaxpr/concatenate | solution.py:138
  51.3 1.9 constant_dynamic-update-slice_fusion.1
  53.8 1.7 constant_dynamic-update-slice_fusion.2
  55.6 6.8 %fusion.4 = f32[8,65536]{1,0:T(8,128)} fusion(f32[8,65536]{1,0:T(8,128)} %collective-permute-done.1, f32[16,65536]{1,0:T(8,128)S(1)} %constant_dynamic-update-slice_fusion.2, f32[16,65536]{1,0:T(8,128)S(1)} %get-tuple-element.41, f32[8,65536]{1,0:T(8,128)} %collective-permute-done, f32[8,65536]{1,0:T(8,128)} %param.6), kind=kLoop, calls=%fused_computation.43 | loop fusion | flops 16252928 | bytes 37748736 | tf_op jit(solution)/shard_map/add | solution.py:91
  62.4 45.1 %fusion.2 = (f32[8,65536]{1,0:T(8,128)}, f32[8,65536]{1,0:T(8,128)}, pred[8,65536]{1,0:T(8,128)(4,1)}) fusion(f32[8,65536]{1,0:T(8,128)} %get-tuple-element.40, f32[8,65536]{1,0:T(8,128)} %get-tuple-element.36, f32[8,65536]{1,0:T(8,128)S(1)} %get-tuple-element.38, f32[8,65536]{1,0:T(8,128)} %get-tuple-element.26, f32[1,65536]{1,0:T(1,128)} %copy-done.6, ...), kind=kLoop, calls=%fused_computation.32 | loop fusion | flops 100663296 | bytes 28049300 | tf_op jit(solution)/shard_map/while/body/eval_jaxpr/sub | solution.py:158
  107.5 6.7 %all-to-all-start = ((f32[8,8,8192]{2,1,0:T(8,128)}), f32[8,8,8192]{2,1,0:T(8,128)S(1)}, u32[]{:S(2)}, u32[]{:S(2)}) async-start(f32[8,8,8192]{2,1,0:T(8,128)} %bitcast.24), calls=%async_computation | async-start | bytes 4194304 | tf_op jit(solution)/shard_map/all_to_all | solution.py:56
  115.7 16.0 %all-to-all-done = f32[8,8,8192]{2,1,0:T(8,128)S(1)} async-done(((f32[8,8,8192]{2,1,0:T(8,128)}), f32[8,8,8192]{2,1,0:T(8,128)S(1)}, u32[]{:S(2)}, u32[]{:S(2)}) %all-to-all-start) | async-done | bytes 2097184 | tf_op jit(solution)/shard_map/all_to_all | solution.py:56
  133.0 1.9 collective-permute-start.5
  134.9 13.5 %collective-permute-start.4 = (f32[8,8192]{1,0:T(8,128)S(1)}, f32[8,8192]{1,0:T(8,128)S(1)}, u32[]{:S(2)}, u32[]{:S(2)}) collective-permute-start(f32[8,8192]{1,0:T(8,128)S(1)} %fusion.136), channel_id=1, source_target_pairs={{0,8},{8,16},{16,24},{24,32},{32,40},{40,48},{48,56},{56,64},{64,7... | collective-permute-start | bytes 786440 | tf_op jit(solution)/shard_map/ppermute | solution.py:34
  148.4 2.2 %collective-permute-done.5 = f32[8,8192]{1,0:T(8,128)S(1)} collective-permute-done((f32[8,8192]{1,0:T(8,128)S(1)}, f32[8,8192]{1,0:T(8,128)S(1)}, u32[]{:S(2)}, u32[]{:S(2)}) %collective-permute-start.5) | collective-permute-done | bytes 262176 | tf_op jit(solution)/shard_map/ppermute | solution.py:37
  152.4 21.5 %all_to_all.16 = f32[8,8,8192]{2,1,0:T(8,128)S(1)} all-to-all(f32[8,8,8192]{2,1,0:T(8,128)S(1)} %broadcast_in_dim.13), channel_id=1, replica_groups=mesh['rows'=32,'freq'=8] {'freq'}, dimensions={0} | all-to-all | bytes 4194304 | tf_op jit(solution)/shard_map/all_to_all | solution.py:62
  174.0 9.5 %multiply_reduce_fusion = (f32[]{:T(128)}, f32[8,65536]{1,0:T(8,128)S(1)}) fusion(f32[8,65536]{1,0:T(8,128)S(1)} %bitcast.25), kind=kLoop, calls=%fused_computation.71 | loop fusion | flops 17301504 | bytes 4194308 | tf_op jit(solution)/shard_map/reduce_sum | solution.py:198
  184.1 28.0 %all_to_all.17 = f32[32,1,1]{2,1,0:T(1,128)S(1)} all-to-all(f32[32,1,1]{2,1,0:T(1,128)S(1)} %broadcast_in_dim.14), channel_id=1, replica_groups=mesh['rows'=32,'freq'=8] {'rows'}, dimensions={0} | all-to-all | bytes 256 | tf_op jit(solution)/shard_map/all_to_all | solution.py:62
  (38 shorter events, 12.2 us)
Async XLA Ops:
  0.0 16.4 %copy-start.3 = (bf16[2,1,8,65536]{3,2,1,0:T(8,128)(2,1)S(1)}, bf16[2,1,8,65536]{3,2,1,0:T(8,128)(2,1)}, u32[]{:S(2)}) copy-start(bf16[2,1,8,65536]{3,2,1,0:T(8,128)(2,1)} %param.8) | copy-start | bytes 6291460
  0.0 51.3 %collective-permute-start = (f32[8,65536]{1,0:T(8,128)}, f32[8,65536]{1,0:T(8,128)}, u32[]{:S(2)}, u32[]{:S(2)}) collective-permute-start(f32[8,65536]{1,0:T(8,128)} %param.6), channel_id=1, source_target_pairs={{0,8},{8,16},{16,24},{24,32},{32,40},{40,48},{48,56},{56,64},{64,7... | collective-permute-start | bytes 6291464 | tf_op jit(solution)/shard_map/ppermute | solution.py:34
  5.1 48.8 %collective-permute-start.1 = (f32[8,65536]{1,0:T(8,128)}, f32[8,65536]{1,0:T(8,128)}, u32[]{:S(2)}, u32[]{:S(2)}) collective-permute-start(f32[8,65536]{1,0:T(8,128)} %param.6), channel_id=1, source_target_pairs={{8,0},{16,8},{24,16},{32,24},{40,32},{48,40},{56,48},{64,56},{72,6... | collective-permute-start | bytes 6291464 | tf_op jit(solution)/shard_map/ppermute | solution.py:37
  10.2 25.3 %collective-permute-start.2 = (bf16[2,1,1,65536]{3,0,2,1:T(2,128)(2,1)S(1)}, bf16[2,1,1,65536]{3,0,2,1:T(2,128)(2,1)S(1)}, u32[]{:S(2)}, u32[]{:S(2)}) collective-permute-start(bf16[2,1,1,65536]{3,0,2,1:T(2,128)(2,1)S(1)} %copy.15), channel_id=1, source_target_pairs={{8,0},{16,8},{24,16},{32,24},{40,32},{48,40},{56,48},{64,56},{72,6... | collective-permute-start | bytes 786440 | tf_op jit(solution)/shard_map/ppermute | solution.py:45
  14.4 2.4 %copy-start.4 = (bf16[2,1,8,65536]{3,2,1,0:T(8,128)(2,1)S(1)}, bf16[2,1,8,65536]{3,2,1,0:T(8,128)(2,1)}, u32[]{:S(2)}) copy-start(bf16[2,1,8,65536]{3,2,1,0:T(8,128)(2,1)} %param.9) | copy-start | bytes 6291460
  14.4 24.0 %collective-permute-start.3 = (bf16[2,1,1,65536]{3,0,2,1:T(2,128)(2,1)S(1)}, bf16[2,1,1,65536]{3,0,2,1:T(2,128)(2,1)}, u32[]{:S(2)}, u32[]{:S(2)}) collective-permute-start(bf16[2,1,1,65536]{3,0,2,1:T(2,128)(2,1)S(1)} %copy.16), channel_id=1, source_target_pairs={{8,0},{16,8},{24,16},{32,24},{40,32},{48,40},{56,48},{64,56},{72,6... | collective-permute-start | bytes 786440 | tf_op jit(solution)/shard_map/ppermute | solution.py:45
  18.6 2.9 %copy-start.7 = (f32[8]{0:T(128)S(1)}, f32[8]{0:T(128)}, u32[]{:S(2)}) copy-start(f32[8]{0:T(128)} %param.10) | copy-start | bytes 100
  21.5 18.4 %copy-start.1 = (f32[8,65536]{1,0:T(8,128)S(1)}, f32[8,65536]{1,0:T(8,128)}, u32[]{:S(2)}) copy-start(f32[8,65536]{1,0:T(8,128)} %get-tuple-element.26) | copy-start | bytes 6291460
  39.9 6.6 %copy-start.5 = (f32[1,65536]{1,0:T(1,128)}, f32[1,65536]{1,0:T(1,128)S(1)}, u32[]{:S(2)}) copy-start(f32[1,65536]{1,0:T(1,128)S(1)} %get-tuple-element.45) | copy-start | bytes 786436
  39.9 6.6 %copy-start.6 = (f32[1,65536]{1,0:T(1,128)}, f32[1,65536]{1,0:T(1,128)S(1)}, u32[]{:S(2)}) copy-start(f32[1,65536]{1,0:T(1,128)S(1)} %get-tuple-element.46) | copy-start | bytes 786436
  39.9 6.6 %copy-start = (f32[8,65536]{1,0:T(8,128)S(1)}, f32[8,65536]{1,0:T(8,128)}, u32[]{:S(2)}) copy-start(f32[8,65536]{1,0:T(8,128)} %get-tuple-element.40) | copy-start | bytes 6291460
  51.3 2.2 %copy-start.2 = (f32[8,65536]{1,0:T(8,128)S(1)}, f32[8,65536]{1,0:T(8,128)}, u32[]{:S(2)}) copy-start(f32[8,65536]{1,0:T(8,128)} %param.6) | copy-start | bytes 6291460
  107.5 24.2 %all-to-all-start = ((f32[8,8,8192]{2,1,0:T(8,128)}), f32[8,8,8192]{2,1,0:T(8,128)S(1)}, u32[]{:S(2)}, u32[]{:S(2)}) async-start(f32[8,8,8192]{2,1,0:T(8,128)} %bitcast.24), calls=%async_computation | async-start | bytes 4194304 | tf_op jit(solution)/shard_map/all_to_all | solution.py:56
  133.0 17.6 %collective-permute-start.5 = (f32[8,8192]{1,0:T(8,128)S(1)}, f32[8,8192]{1,0:T(8,128)S(1)}, u32[]{:S(2)}, u32[]{:S(2)}) collective-permute-start(f32[8,8192]{1,0:T(8,128)S(1)} %fusion.136), channel_id=1, source_target_pairs={{8,0},{16,8},{24,16},{32,24},{40,32},{48,40},{56,48},{64,56},{72,6... | collective-permute-start | bytes 786440 | tf_op jit(solution)/shard_map/ppermute | solution.py:37
  134.9 16.6 %collective-permute-start.4 = (f32[8,8192]{1,0:T(8,128)S(1)}, f32[8,8192]{1,0:T(8,128)S(1)}, u32[]{:S(2)}, u32[]{:S(2)}) collective-permute-start(f32[8,8192]{1,0:T(8,128)S(1)} %fusion.136), channel_id=1, source_target_pairs={{0,8},{8,16},{16,24},{24,32},{32,40},{40,48},{48,56},{56,64},{64,7... | collective-permute-start | bytes 786440 | tf_op jit(solution)/shard_map/ppermute | solution.py:34
where the time goes:
time: 216 us; the launch traced here: 215 us
  other arithmetic  81.1 us (38%)
  blocking collectives  49.5 us (23%)
  waiting for transfers between devices  34.6 us (16%)
  starting transfers between devices  33.9 us (16%)
  local copies, waits for them, and re-layouts  14.2 us (7%)
    all_to_all x2, blocking collectives, from_everyone(): lax.all_to_all(jnp.broadcast_to(shard[None], (peers, *shard.shape)), axis...  49.5 us
    sub x1, other arithmetic, element_terms(): return stiffness * (elastic - loss_factor * damped) - omega * inertia  45.1 us
    ppermute x2, starting transfers between devices, extended(): lax.ppermute(lax.slice_in_dim(block, block.shape[dim] - width, None, axis...  18.5 us
    all_to_all x1, waiting for transfers between devices, sent_and_summed(): lax.all_to_all(in_blocks(shard, dim, peers), axis, 0, 0, tiled=True)  16 us
    ppermute x2, waiting for transfers between devices, from_behind(): return lax.ppermute(block, axis, route)  15.5 us
    concatenate x2, other arithmetic, corners(): stacked = jnp.concatenate([nodes, below], axis=0)  11.4 us
    reduce_sum x1, other arithmetic, shards(): total = of_everyone(jnp.sum(back * back), 'rows')  9.48 us
    add x2, other arithmetic, row_pass(): total = total + taps[offset] * padded[offset:offset + count]  7.71 us
  transfers between devices with their start and end apart: 7, of which 5 were waited for; matrix products, arithmetic and copies ran while one was open for 12% of the time, Pallas kernels for 0%

commit v1 on v0

v1 whole, which is shorter than its diff:
```python
import functools

import jax
import jax.numpy as jnp
from jax import lax
from jax.experimental import pallas as pl
from jax.experimental.pallas import tpu as pltpu
from jax.sharding import PartitionSpec as P

RADIUS = 8
LANES = 128
SHARPNESS = 8.0
THRESHOLD = 0.5
EXPONENT = 3.0
SOFT_FLOOR = 0.001
LOSS = 0.2
EPSILON = 1e-06
TANH_HALF = 0.999329299739067
DESIGN_STEPS = 32767.0
CODE_STEPS = 32700.0

f32 = jnp.float32
i16 = jnp.int16


def params(megabytes):
    return pltpu.CompilerParams(vmem_limit_bytes=megabytes * 1024 * 1024)


def vmem(count):
    return [pl.BlockSpec(memory_space=pltpu.VMEM)] * count


def cost(flops, moved):
    return pl.CostEstimate(flops=flops, bytes_accessed=moved, transcendentals=0)


def cols(index, width):
    return pl.ds(pl.multiple_of(index * width, width), width)


def row_ids(width):
    return lax.broadcasted_iota(jnp.int32, (8, width), 0)


def rows_up(block, count, ids):
    return jnp.where(ids < 8 - count, pltpu.roll(block, 8 - count, 0), 0.0)


def rows_down(block, count, ids):
    return jnp.where(ids >= count, pltpu.roll(block, count, 0), 0.0)


def row_filter(above, here, below):
    ids = row_ids(here.shape[1])
    upper = above - here
    lower = below - here
    for _ in range(2):
        for count in (1, 2, 4):
            upper = upper + rows_up(upper, count, ids)
            lower = lower + rows_down(lower, count, ids)
    total = here
    for count in (1, 2, 4):
        total = total + pltpu.roll(total, count, 0)
    return upper + lower + here + 10.0 * total


def cols_left(block, count):
    return pltpu.roll(block, block.shape[1] - count, 1)


def col_filter(block):
    for _ in range(2):
        first = block
        for count in (1, 2, 4):
            block = block + cols_left(block, count)
        block = block + cols_left(first, 8)
    return block


def moved_right(carry, block):
    joined = jnp.concatenate([carry, block], axis=1)
    return pltpu.roll(joined, RADIUS, 1)[:, LANES:]


def decode_scale(code):
    return jnp.exp2(code.astype(jnp.int32).astype(f32) * (1.0 / 256)) * (1.0 / CODE_STEPS)


def scale_code(largest):
    level = jnp.floor(jnp.log(jnp.maximum(largest, 1e-30)) * (256 * 1.4426950408889634)) + 1.0
    return level


def to_i16(values):
    return jnp.floor(values + 0.5).astype(jnp.int32).astype(i16)


def wide(tile, width):
    return jnp.concatenate([tile] * (width // LANES), axis=1)


def folded_max(block):
    parts = [block[:, i : i + LANES] for i in range(0, block.shape[1], LANES)]
    while len(parts) > 1:
        parts = [jnp.maximum(a, b) for a, b in zip(parts[::2], parts[1::2])]
    return parts[0]


def encode(source, target, count, width):
    largest = lax.fori_loop(
        0,
        count // width,
        lambda c, m: jnp.maximum(m, folded_max(jnp.abs(source[:, cols(c, width)]))),
        jnp.zeros((8, LANES), f32),
    )
    level = scale_code(largest)
    code = level.astype(jnp.int32).astype(i16)
    target[:, count : count + LANES] = code
    inverse = wide(1.0 / decode_scale(code), width)

    def step(c, none):
        target[:, cols(c, width)] = to_i16(source[:, cols(c, width)] * inverse)
        return none

    lax.fori_loop(0, count // width, step, 0)


def prepare_kernel(design, state, adjoint, edge, code, *, width):
    ids = row_ids(width)

    def step(c, none):
        at = cols(c, width)
        first = state[0, 0, :, at].astype(f32)
        rows = [state[1, 0, :, at], adjoint[0, 0, :, at], adjoint[1, 0, :, at]]
        for place, row in enumerate(rows):
            first = jnp.where(ids == place + 1, pltpu.roll(row.astype(f32), place + 1, 0), first)
        edge[:, at] = first[:4].astype(jnp.bfloat16)
        code[:, at] = to_i16(design[:, at] * DESIGN_STEPS)
        return none

    lax.fori_loop(0, design.shape[1] // width, step, 0)


def element_kernel(omega_sq, assign, state, adjoint, edge, elastic, inertia, *, width):
    omega = omega_sq[assign[0]]
    ids = row_ids(width)
    count = elastic.shape[1] // width
    whole = width + LANES

    def shifted(block, carry):
        return cols_left(jnp.concatenate([block, carry], axis=1), 1)[:, :width]

    def step(c, carries):
        at = cols(count - 1 - c, width)
        edges = edge[:, at].astype(f32)
        fields = [state[0, 0, :, at], state[1, 0, :, at], adjoint[0, 0, :, at], adjoint[1, 0, :, at]]
        kept = []
        parts = []
        for place, field in enumerate(fields):
            here = field.astype(f32)
            row = jnp.broadcast_to(edges[place : place + 1], here.shape)
            below = jnp.where(ids == 7, row, pltpu.roll(here, 7, 0))
            plus = here + below
            minus = here - below
            kept += [plus[:, :LANES], minus[:, :LANES]]
            plus_next = shifted(plus, carries[2 * place])
            minus_next = shifted(minus, carries[2 * place + 1])
            parts.append((plus + plus_next, plus - plus_next, minus + minus_next, minus - minus_next))
        sr, si, ar, ai = parts
        same = [ar[k] * sr[k] - ai[k] * si[k] for k in range(4)]
        cross = [ar[k] * si[k] + ai[k] * sr[k] for k in range(1, 4)]
        same_mixed = same[1] + same[2]
        cross_mixed = cross[0] + cross[1]
        stiff = 1.5 * (same_mixed - LOSS * cross_mixed) + (same[3] - LOSS * cross[2])
        mass = 2.25 * same[0] + 0.75 * same_mixed + 0.25 * same[3]
        elastic[:, at] = stiff * (EXPONENT * (1.0 - SOFT_FLOOR) / 6.0)
        inertia[:, at] = mass * (omega * (1.0 / 36.0))
        return tuple(kept)

    lax.fori_loop(0, count, step, tuple(jnp.zeros((8, LANES), f32) for _ in range(8)))


def partial_kernel(place, design, above, below, passive, elastic, inertia, inverse, *refs, width):
    outs, (rowed, spread, blocks) = refs[:-3], refs[-3:]
    count = design.shape[1] // width
    peers = len(outs)
    piece = design.shape[1] // peers
    zeros = jnp.zeros((8, LANES), f32)

    def filter_rows(c, carry):
        at = cols(c, width)
        upper = above[:, at].astype(jnp.int32).astype(f32) * (1.0 / DESIGN_STEPS)
        lower = below[:, at].astype(jnp.int32).astype(f32) * (1.0 / DESIGN_STEPS)
        block = row_filter(upper, design[:, at], lower)
        rowed[:, at] = moved_right(carry, block)
        return block[:, width - LANES :]

    last = lax.fori_loop(0, count, filter_rows, zeros)
    rowed[:, count * width :] = moved_right(last, zeros)

    def scale(c, carry):
        at = cols(c, width)
        window = rowed[:, pl.ds(pl.multiple_of(c * width, width), width + LANES)]
        weights = inverse[:, at]
        tilde = col_filter(window)[:, :width] * weights
        steep = jnp.tanh(SHARPNESS * (tilde - THRESHOLD))
        solid = passive[:, at] > 0
        density = jnp.where(solid, 1.0, (TANH_HALF + steep) * (0.5 / TANH_HALF))
        slope = jnp.where(solid, 0.0, (1.0 - steep * steep) * (SHARPNESS * 0.5 / TANH_HALF))
        block = (density * density * elastic[:, at] - inertia[:, at]) * (slope * weights)
        spread[:, at] = moved_right(carry, block)
        return block[:, width - LANES :]

    last = lax.fori_loop(0, count, scale, zeros)
    spread[:, count * width :] = moved_right(last, zeros)

    for shift in range(peers):
        start = lax.rem(place[0] + shift, peers) * piece

        def filter_cols(c, none):
            at = pl.ds(pl.multiple_of(start + c * width, width), width + LANES)
            blocks[:, cols(c, width)] = col_filter(spread[:, at])[:, :width]
            return none

        lax.fori_loop(0, piece // width, filter_cols, 0)
        encode(blocks, outs[shift], piece, width)


def sum_kernel(*refs, width):
    coded, out = refs[:-1], refs[-1]
    piece = out.shape[1]
    scales = [decode_scale(ref[:, piece:]) for ref in coded]

    def step(c, none):
        at = cols(c, width)
        total = None
        for ref, scale in zip(coded, scales):
            term = ref[:, at].astype(jnp.int32).astype(f32) * wide(scale, width)
            total = term if total is None else total + term
        out[:, at] = total
        return none

    lax.fori_loop(0, piece // width, step, 0)


def back_kernel(above, here, below, out, blocks, *, width):
    piece = here.shape[1]

    def step(c, none):
        at = cols(c, width)
        blocks[:, at] = row_filter(above[:, at], here[:, at], below[:, at])
        return none

    lax.fori_loop(0, piece // width, step, 0)
    encode(blocks, out, piece, width)


def decode_kernel(place, *refs, width):
    coded, out, squares = refs[:-2], refs[-2], refs[-1]
    peers = len(coded)
    piece = out.shape[1] // peers
    total = jnp.zeros((8, LANES), f32)
    for shift, ref in enumerate(coded):
        start = lax.rem(place[0] + peers - shift, peers) * piece
        scale = wide(decode_scale(ref[:, piece:]), width)

        def step(c, total):
            block = ref[:, cols(c, width)].astype(jnp.int32).astype(f32) * scale
            out[:, pl.ds(pl.multiple_of(start + c * width, width), width)] = block
            square = block * block
            parts = [square[:, i : i + LANES] for i in range(0, width, LANES)]
            while len(parts) > 1:
                parts = [a + b for a, b in zip(parts[::2], parts[1::2])]
            return total + parts[0]

        total = lax.fori_loop(0, piece // width, step, total)
    squares[...] = jnp.broadcast_to(total[None], squares.shape)


def scale_kernel(back, squares, out, *, width, elements):
    mean = jnp.sum(jnp.sum(squares[...], axis=0), keepdims=True) * (1.0 / elements) + EPSILON
    root = lax.rsqrt(mean)
    root = root * (1.5 - 0.5 * mean * root * root)

    def step(c, none):
        at = cols(c, width)
        out[:, at] = back[:, at] * root
        return none

    lax.fori_loop(0, out.shape[1] // width, step, 0)


def edge_weights(positions, whole):
    near = jnp.maximum(RADIUS - positions, 0)
    far = jnp.maximum(RADIUS - (whole - 1 - positions), 0)
    missing = near * (near + 1) // 2 + far * (far + 1) // 2
    return ((RADIUS + 1) ** 2 - missing).astype(f32)


def shards(design, passive, state, adjoint, omega_sq, assign):
    slab_rows, width = design.shape
    rows = lax.axis_size("rows")
    peers = lax.axis_size("freq")
    whole_rows = slab_rows * rows
    piece = width // peers
    up = [(i, i + 1) for i in range(rows - 1)]
    down = [(target, source) for source, target in up]
    place = lax.axis_index("freq").astype(jnp.int32).reshape(1)
    smem = pl.BlockSpec(memory_space=pltpu.SMEM)

    edge, code = pl.pallas_call(
        functools.partial(prepare_kernel, width=512),
        out_shape=[
            jax.ShapeDtypeStruct((4, width), jnp.bfloat16),
            jax.ShapeDtypeStruct((slab_rows, width), i16),
        ],
        in_specs=vmem(3),
        out_specs=vmem(2),
        compiler_params=params(16),
        name="prepare",
    )(design, state, adjoint)
    edge_below = lax.ppermute(edge, "rows", down)
    code_below = lax.ppermute(code, "rows", down)
    code_above = lax.ppermute(code, "rows", up)

    top = lax.axis_index("rows") * slab_rows
    inverse = 1.0 / (
        edge_weights(top + jnp.arange(slab_rows, dtype=jnp.int32), whole_rows)[:, None]
        * edge_weights(jnp.arange(width, dtype=jnp.int32), width)[None, :]
    )

    slab = jax.ShapeDtypeStruct((slab_rows, width), f32)
    elastic, inertia = pl.pallas_call(
        functools.partial(element_kernel, width=256),
        out_shape=[slab, slab],
        in_specs=[smem, smem] + vmem(3),
        out_specs=vmem(2),
        compiler_params=params(20),
        cost_estimate=cost(80 * slab_rows * width, 8 * 1024 * 1024),
        name="element",
    )(omega_sq, assign, state, adjoint, edge_below)

    coded_piece = jax.ShapeDtypeStruct((slab_rows, piece + LANES), i16)
    sent = pl.pallas_call(
        functools.partial(partial_kernel, width=1024),
        out_shape=[coded_piece] * peers,
        in_specs=[smem] + vmem(7),
        out_specs=vmem(peers),
        scratch_shapes=[
            pltpu.VMEM((slab_rows, width + LANES), f32),
            pltpu.VMEM((slab_rows, width + LANES), f32),
            pltpu.VMEM((slab_rows, piece), f32),
        ],
        compiler_params=params(32),
        cost_estimate=cost(150 * slab_rows * width, 14 * 1024 * 1024),
        name="partial",
    )(place, design, code_above, code_below, passive, elastic, inertia, inverse)

    received = [sent[0]]
    for shift in range(1, peers):
        route = [(i, (i + shift) % peers) for i in range(peers)]
        received.append(lax.ppermute(sent[shift], "freq", route))

    spread = pl.pallas_call(
        functools.partial(sum_kernel, width=1024),
        out_shape=jax.ShapeDtypeStruct((slab_rows, piece), f32),
        in_specs=vmem(peers),
        out_specs=vmem(1)[0],
        compiler_params=params(8),
        name="total",
    )(*received)
    spread_below = lax.ppermute(spread, "rows", down)
    spread_above = lax.ppermute(spread, "rows", up)

    result = pl.pallas_call(
        functools.partial(back_kernel, width=1024),
        out_shape=coded_piece,
        in_specs=vmem(3),
        out_specs=vmem(1)[0],
        scratch_shapes=[pltpu.VMEM((slab_rows, piece), f32)],
        compiler_params=params(8),
        name="back",
    )(spread_above, spread, spread_below)

    pieces = [result]
    for shift in range(1, peers):
        route = [(i, (i + shift) % peers) for i in range(peers)]
        pieces.append(lax.ppermute(result, "freq", route))

    back, squares = pl.pallas_call(
        functools.partial(decode_kernel, width=1024),
        out_shape=[slab, jax.ShapeDtypeStruct((rows, 8, LANES), f32)],
        in_specs=[smem] + vmem(peers),
        out_specs=vmem(2),
        compiler_params=params(16),
        name="decode",
    )(place, *pieces)
    squares = lax.all_to_all(squares, "rows", 0, 0, tiled=True)

    return pl.pallas_call(
        functools.partial(scale_kernel, width=1024, elements=float(whole_rows * width)),
        out_shape=slab,
        in_specs=vmem(2),
        out_specs=vmem(1)[0],
        compiler_params=params(16),
        name="scale",
    )(back, squares)


def solution(mesh):
    return jax.shard_map(
        shards,
        mesh=mesh,
        in_specs=(
            P("rows", None),
            P("rows", None),
            P(None, "freq", "rows", None),
            P(None, "freq", "rows", None),
            P(),
            P("freq"),
        ),
        out_specs=P("rows", None),
        check_vma=False,
    )
```

time: 216 us -> 213 us (0.986)
  Pallas kernels: 0 us -> 108 us
  other arithmetic: 81.1 us -> 1.7 us
  blocking collectives: 49.5 us -> 23.7 us
  starting transfers between devices: 33.9 us -> 43.3 us
  waiting for transfers between devices: 34.6 us -> 27.3 us
  local copies, waits for them, and re-layouts: 14.2 us -> 7.96 us
    pallas_call x0 -> x7, Pallas kernels: none -> 108 us  [the longest x1 72.4 us: shards(): pl.pallas_call(functools.partial(partial_kernel, width=1024), out_shape=[...]
    sub x1 -> x0, other arithmetic: 45.1 us -> none  [element_terms(): return stiffness * (elastic - loss_factor * damped) - omega * inertia]
    all_to_all x2 -> x1, blocking collectives: 49.5 us -> 23.7 us  [shards(): squares = lax.all_to_all(squares, 'rows', 0, 0, tiled=True)]
    ppermute x6 -> x19, starting transfers between devices: 27.2 us -> 43.3 us  [the longest x7 13.2 us: shards(): received.append(lax.ppermute(sent[shift], 'freq', route))]
    all_to_all x1 -> x0, waiting for transfers between devices: 16 us -> none  [sent_and_summed(): lax.all_to_all(in_blocks(shard, dim, peers), axis, 0, 0, tiled=True)]
    concatenate x2 -> x0, other arithmetic: 11.4 us -> none  [corners(): stacked = jnp.concatenate([nodes, below], axis=0)]
    reduce_sum x3 -> x0, other arithmetic: 10.2 us -> none  [the longest x1 9.48 us: shards(): total = of_everyone(jnp.sum(back * back), 'rows')]
    ppermute x6 -> x19, waiting for transfers between devices: 18.6 us -> 27.3 us  [the longest x1 10.6 us: shards(): edge_below = lax.ppermute(edge, 'rows', down)]
  transfers between devices with their start and end apart: 7 -> 19, of which waited for: 5 -> 10; matrix products, arithmetic and copies ran while one was open for 12% -> 1% of each run, Pallas kernels for 0% -> 13%
where the time goes in v1:
time: 213 us
  Pallas kernels  108 us (51%)
  starting transfers between devices  43.3 us (20%)
  waiting for transfers between devices  27.3 us (13%)
  blocking collectives  23.7 us (11%)
  local copies, waits for them, and re-layouts  7.96 us (4%)
    pallas_call x1, Pallas kernels, shards(): pl.pallas_call(functools.partial(partial_kernel, width=1024), out_shape=[...  72.4 us
    pallas_call x1, Pallas kernels, shards(): pl.pallas_call(functools.partial(element_kernel, width=256), out_shape=[s...  28.7 us
    all_to_all x1, blocking collectives, shards(): squares = lax.all_to_all(squares, 'rows', 0, 0, tiled=True)  23.7 us
    ppermute x7, starting transfers between devices, shards(): received.append(lax.ppermute(sent[shift], 'freq', route))  13.2 us
    ppermute x7, starting transfers between devices, shards(): pieces.append(lax.ppermute(result, 'freq', route))  11.6 us
    ppermute x1, waiting for transfers between devices, shards(): edge_below = lax.ppermute(edge, 'rows', down)  10.6 us
    ppermute x7, waiting for transfers between devices, shards(): pieces.append(lax.ppermute(result, 'freq', route))  8.09 us
    unnamed x18, local copies, waits for them, and re-layouts  7.96 us
  transfers between devices with their start and end apart: 19, of which 10 were waited for; matrix products, arithmetic and copies ran while one was open for 1% of the time, Pallas kernels for 13%

profile of v1, /device:TPU:1, one launch (start us, length us, event | category | flops | bytes accessed | tf_op | source)
XLA Modules:
  0.0 212.7 jit_solution(5930685272001754676)
XLA Ops:
  4.8 3.2 %prepare.1 = (bf16[4,65536]{1,0:T(4,128)(2,1)}, s16[8,65536]{1,0:T(8,128)(2,1)}) custom-call(f32[8,65536]{1,0:T(8,128)S(1)} %copy-done.4, bf16[2,1,8,65536]{3,2,1,0:T(8,128)(2,1)S(1)} %copy-done, bf16[2,1,8,65536]{3,2,1,0:T(8,128)(2,1)S(1)} %copy-done.2), custom_call_target="tpu_custom_call" | custom-call | tf_op jit(solution)/shard_map/prepare/pallas_call | solution.py:312
  7.9 5.2 %collective-permute-start.1 = (s16[8,65536]{1,0:T(8,128)(2,1)}, s16[8,65536]{1,0:T(8,128)(2,1)S(1)}, u32[]{:S(2)}, u32[]{:S(2)}) collective-permute-start(s16[8,65536]{1,0:T(8,128)(2,1)} %get-tuple-element.19), channel_id=1, source_target_pairs={{8,0},{16,8},{24,16},{32,24},{40,32},{48,40},{56,48},{64,56},{72,6... | collective-permute-start | bytes 3145736 | tf_op jit(solution)/shard_map/ppermute | solution.py:324
  13.2 1.9 collective-permute-start
  15.1 3.4 %collective-permute-start.2 = (bf16[4,65536]{1,0:T(4,128)(2,1)}, bf16[4,65536]{1,0:T(4,128)(2,1)}, u32[]{:S(2)}, u32[]{:S(2)}) collective-permute-start(bf16[4,65536]{1,0:T(4,128)(2,1)} %get-tuple-element.20), channel_id=1, source_target_pairs={{8,0},{16,8},{24,16},{32,24},{40,32},{48,40},{56,48},{64,56},{72,6... | collective-permute-start | bytes 1572872 | tf_op jit(solution)/shard_map/ppermute | solution.py:323
  18.5 1.7 multiply_divide_fusion.inverse
  20.9 10.6 %collective-permute-done.2.edge = bf16[4,65536]{1,0:T(4,128)(2,1)} collective-permute-done((bf16[4,65536]{1,0:T(4,128)(2,1)}, bf16[4,65536]{1,0:T(4,128)(2,1)}, u32[]{:S(2)}, u32[]{:S(2)}) %collective-permute-start.2) | collective-permute-done | bytes 524320 | tf_op jit(solution)/shard_map/ppermute | solution.py:323
  31.4 1.6 copy-done.3
  33.0 28.7 %element.1 = (f32[8,65536]{1,0:T(8,128)S(1)}, f32[8,65536]{1,0:T(8,128)S(1)}) custom-call(f32[8]{0:T(128)S(1)} %copy-done.8, s32[1]{0:T(128)S(6)} %copy.7.assign, bf16[2,1,8,65536]{3,2,1,0:T(8,128)(2,1)S(1)} %copy-done.1, bf16[2,1,8,65536]{3,2,1,0:T(8,128)(2,1)S(1)} %copy-done.3, bf16[4,65536]{1,0:T(4,128)(2,1)} %collective-permute-done.2.edge), custom_call_target="tpu_custom_call" | custom-call | flops 41943040 | bytes 8388608 | tf_op jit(solution)/shard_map/element/pallas_call | solution.py:334
  63.3 72.4 %partial.1 = (s16[8,8320]{1,0:T(8,128)(2,1)S(1)}, s16[8,8320]{1,0:T(8,128)(2,1)S(1)}, s16[8,8320]{1,0:T(8,128)(2,1)S(1)}, s16[8,8320]{1,0:T(8,128)(2,1)S(1)}, s1...) custom-call(s32[1]{0:T(128)} %bitcast.place, ...), custom_call_target="tpu_custom_call" | custom-call | flops 78643200 | bytes 14680064 | tf_op jit(solution)/shard_map/partial/pallas_call | solution.py:345
  135.7 2.8 %collective-permute-start.3 = (s16[8,8320]{1,0:T(8,128)(2,1)S(1)}, s16[8,8320]{1,0:T(8,128)(2,1)S(1)}, u32[]{:S(2)}, u32[]{:S(2)}) collective-permute-start(s16[8,8320]{1,0:T(8,128)(2,1)S(1)} %get-tuple-element.24), channel_id=1, source_target_pairs={{0,1},{1,2},{2,3},{3,4},{4,5},{5,6},{6,7},{7,0},{8,9},{9,10},{10,1... | collective-permute-start | bytes 399368 | tf_op jit(solution)/shard_map/ppermute | solution.py:363
  139.8 2.0 collective-permute-start.5
  143.4 4.5 %collective-permute-start.7 = (s16[8,8320]{1,0:T(8,128)(2,1)S(1)}, s16[8,8320]{1,0:T(8,128)(2,1)S(1)}, u32[]{:S(2)}, u32[]{:S(2)}) collective-permute-start(s16[8,8320]{1,0:T(8,128)(2,1)S(1)} %get-tuple-element.28), channel_id=1, source_target_pairs={{0,5},{1,6},{2,7},{3,0},{4,1},{5,2},{6,3},{7,4},{8,13},{9,14},{10,... | collective-permute-start | bytes 399368 | tf_op jit(solution)/shard_map/ppermute | solution.py:363
  149.8 1.9 collective-permute-done.8.refs_6_
  151.7 2.6 %collective-permute-done.9.refs_7_ = s16[8,8320]{1,0:T(8,128)(2,1)S(1)} collective-permute-done((s16[8,8320]{1,0:T(8,128)(2,1)S(1)}, s16[8,8320]{1,0:T(8,128)(2,1)S(1)}, u32[]{:S(2)}, u32[]{:S(2)}) %collective-permute-start.9) | collective-permute-done | bytes 133152 | tf_op jit(solution)/shard_map/ppermute | solution.py:363
  154.6 1.9 collective-permute-start.11
  156.5 6.1 %collective-permute-start.10 = (f32[8,8192]{1,0:T(8,128)S(1)}, f32[8,8192]{1,0:T(8,128)S(1)}, u32[]{:S(2)}, u32[]{:S(2)}) collective-permute-start(f32[8,8192]{1,0:T(8,128)S(1)} %total.1.here), channel_id=1, source_target_pairs={{0,8},{8,16},{16,24},{24,32},{32,40},{40,48},{48,56},{56,64},{64,7... | collective-permute-start | bytes 786440 | tf_op jit(solution)/shard_map/ppermute | solution.py:374
  162.6 2.1 collective-permute-done.11.below
  166.6 4.7 %collective-permute-start.18 = (s16[8,8320]{1,0:T(8,128)(2,1)S(1)}, s16[8,8320]{1,0:T(8,128)(2,1)S(1)}, u32[]{:S(2)}, u32[]{:S(2)}) collective-permute-start(s16[8,8320]{1,0:T(8,128)(2,1)S(1)} %back.1.refs_0_), channel_id=1, source_target_pairs={{0,7},{1,0},{2,1},{3,2},{4,3},{5,4},{6,5},{7,6},{8,15},{9,8},{10,9... | collective-permute-start | bytes 399368 | tf_op jit(solution)/shard_map/ppermute | solution.py:389
  171.6 2.9 %collective-permute-start.15 = (s16[8,8320]{1,0:T(8,128)(2,1)S(1)}, s16[8,8320]{1,0:T(8,128)(2,1)S(1)}, u32[]{:S(2)}, u32[]{:S(2)}) collective-permute-start(s16[8,8320]{1,0:T(8,128)(2,1)S(1)} %back.1.refs_0_), channel_id=1, source_target_pairs={{0,4},{1,5},{2,6},{3,7},{4,0},{5,1},{6,2},{7,3},{8,12},{9,13},{10,... | collective-permute-start | bytes 399368 | tf_op jit(solution)/shard_map/ppermute | solution.py:389
  176.7 2.6 %collective-permute-start.12 = (s16[8,8320]{1,0:T(8,128)(2,1)S(1)}, s16[8,8320]{1,0:T(8,128)(2,1)S(1)}, u32[]{:S(2)}, u32[]{:S(2)}) collective-permute-start(s16[8,8320]{1,0:T(8,128)(2,1)S(1)} %back.1.refs_0_), channel_id=1, source_target_pairs={{0,1},{1,2},{2,3},{3,4},{4,5},{5,6},{6,7},{7,0},{8,9},{9,10},{10,1... | collective-permute-start | bytes 399368 | tf_op jit(solution)/shard_map/ppermute | solution.py:389
  179.6 3.8 %collective-permute-done.14.refs_3_ = s16[8,8320]{1,0:T(8,128)(2,1)S(1)} collective-permute-done((s16[8,8320]{1,0:T(8,128)(2,1)S(1)}, s16[8,8320]{1,0:T(8,128)(2,1)S(1)}, u32[]{:S(2)}, u32[]{:S(2)}) %collective-permute-start.14) | collective-permute-done | bytes 133152 | tf_op jit(solution)/shard_map/ppermute | solution.py:389
  183.5 2.9 %collective-permute-done.13.refs_2_ = s16[8,8320]{1,0:T(8,128)(2,1)S(1)} collective-permute-done((s16[8,8320]{1,0:T(8,128)(2,1)S(1)}, s16[8,8320]{1,0:T(8,128)(2,1)S(1)}, u32[]{:S(2)}, u32[]{:S(2)}) %collective-permute-start.13) | collective-permute-done | bytes 133152 | tf_op jit(solution)/shard_map/ppermute | solution.py:389
  187.2 23.7 %all_to_all.5.squares = f32[32,8,128]{2,1,0:T(8,128)S(1)} all-to-all(f32[32,8,128]{2,1,0:T(8,128)S(1)} %get-tuple-element.32), channel_id=1, replica_groups=mesh['rows'=32,'freq'=8] {'rows'}, dimensions={0} | all-to-all | bytes 262144 | tf_op jit(solution)/shard_map/all_to_all | solution.py:399
  210.9 1.9 scale.1
  (43 shorter events, 17.0 us)
Async XLA Ops:
  7.9 23.5 %copy-start.1 = (bf16[2,1,8,65536]{3,2,1,0:T(8,128)(2,1)S(1)}, bf16[2,1,8,65536]{3,2,1,0:T(8,128)(2,1)}, u32[]{:S(2)}) copy-start(bf16[2,1,8,65536]{3,2,1,0:T(8,128)(2,1)} %state.3) | copy-start | bytes 6291460
  7.9 23.5 %copy-start.8 = (f32[8]{0:T(128)S(1)}, f32[8]{0:T(128)}, u32[]{:S(2)}) copy-start(f32[8]{0:T(128)} %omega_sq.1) | copy-start | bytes 100
  7.9 53.7 %collective-permute-start.1 = (s16[8,65536]{1,0:T(8,128)(2,1)}, s16[8,65536]{1,0:T(8,128)(2,1)S(1)}, u32[]{:S(2)}, u32[]{:S(2)}) collective-permute-start(s16[8,65536]{1,0:T(8,128)(2,1)} %get-tuple-element.19), channel_id=1, source_target_pairs={{8,0},{16,8},{24,16},{32,24},{40,32},{48,40},{56,48},{64,56},{72,6... | collective-permute-start | bytes 3145736 | tf_op jit(solution)/shard_map/ppermute | solution.py:324
  13.2 48.5 %collective-permute-start = (s16[8,65536]{1,0:T(8,128)(2,1)}, s16[8,65536]{1,0:T(8,128)(2,1)}, u32[]{:S(2)}, u32[]{:S(2)}) collective-permute-start(s16[8,65536]{1,0:T(8,128)(2,1)} %get-tuple-element.19), channel_id=1, source_target_pairs={{0,8},{8,16},{16,24},{24,32},{32,40},{40,48},{48,56},{56,64},{64,7... | collective-permute-start | bytes 3145736 | tf_op jit(solution)/shard_map/ppermute | solution.py:325
  15.1 16.3 %collective-permute-start.2 = (bf16[4,65536]{1,0:T(4,128)(2,1)}, bf16[4,65536]{1,0:T(4,128)(2,1)}, u32[]{:S(2)}, u32[]{:S(2)}) collective-permute-start(bf16[4,65536]{1,0:T(4,128)(2,1)} %get-tuple-element.20), channel_id=1, source_target_pairs={{8,0},{16,8},{24,16},{32,24},{40,32},{48,40},{56,48},{64,56},{72,6... | collective-permute-start | bytes 1572872 | tf_op jit(solution)/shard_map/ppermute | solution.py:323
  33.0 28.7 %copy-start.5 = (f32[8,65536]{1,0:T(8,128)S(1)}, f32[8,65536]{1,0:T(8,128)}, u32[]{:S(2)}) copy-start(f32[8,65536]{1,0:T(8,128)} %design.3) | copy-start | bytes 6291460
  33.0 28.7 %copy-start.6 = (f32[8,65536]{1,0:T(8,128)S(1)}, f32[8,65536]{1,0:T(8,128)}, u32[]{:S(2)}) copy-start(f32[8,65536]{1,0:T(8,128)} %multiply_divide_fusion.inverse) | copy-start | bytes 6291460
  61.7 1.6 copy-start.7
  135.7 12.1 %collective-permute-start.3 = (s16[8,8320]{1,0:T(8,128)(2,1)S(1)}, s16[8,8320]{1,0:T(8,128)(2,1)S(1)}, u32[]{:S(2)}, u32[]{:S(2)}) collective-permute-start(s16[8,8320]{1,0:T(8,128)(2,1)S(1)} %get-tuple-element.24), channel_id=1, source_target_pairs={{0,1},{1,2},{2,3},{3,4},{4,5},{5,6},{6,7},{7,0},{8,9},{9,10},{10,1... | collective-permute-start | bytes 399368 | tf_op jit(solution)/shard_map/ppermute | solution.py:363
  138.5 10.4 %collective-permute-start.4 = (s16[8,8320]{1,0:T(8,128)(2,1)S(1)}, s16[8,8320]{1,0:T(8,128)(2,1)S(1)}, u32[]{:S(2)}, u32[]{:S(2)}) collective-permute-start(s16[8,8320]{1,0:T(8,128)(2,1)S(1)} %get-tuple-element.25), channel_id=1, source_target_pairs={{0,2},{1,3},{2,4},{3,5},{4,6},{5,7},{6,0},{7,1},{8,10},{9,11},{10,... | collective-permute-start | bytes 399368 | tf_op jit(solution)/shard_map/ppermute | solution.py:363
  139.8 9.1 %collective-permute-start.5 = (s16[8,8320]{1,0:T(8,128)(2,1)S(1)}, s16[8,8320]{1,0:T(8,128)(2,1)S(1)}, u32[]{:S(2)}, u32[]{:S(2)}) collective-permute-start(s16[8,8320]{1,0:T(8,128)(2,1)S(1)} %get-tuple-element.26), channel_id=1, source_target_pairs={{0,3},{1,4},{2,5},{3,6},{4,7},{5,0},{6,1},{7,2},{8,11},{9,12},{10,... | collective-permute-start | bytes 399368 | tf_op jit(solution)/shard_map/ppermute | solution.py:363
  141.8 7.1 %collective-permute-start.6 = (s16[8,8320]{1,0:T(8,128)(2,1)S(1)}, s16[8,8320]{1,0:T(8,128)(2,1)S(1)}, u32[]{:S(2)}, u32[]{:S(2)}) collective-permute-start(s16[8,8320]{1,0:T(8,128)(2,1)S(1)} %get-tuple-element.27), channel_id=1, source_target_pairs={{0,4},{1,5},{2,6},{3,7},{4,0},{5,1},{6,2},{7,3},{8,12},{9,13},{10,... | collective-permute-start | bytes 399368 | tf_op jit(solution)/shard_map/ppermute | solution.py:363
  143.4 6.4 %collective-permute-start.7 = (s16[8,8320]{1,0:T(8,128)(2,1)S(1)}, s16[8,8320]{1,0:T(8,128)(2,1)S(1)}, u32[]{:S(2)}, u32[]{:S(2)}) collective-permute-start(s16[8,8320]{1,0:T(8,128)(2,1)S(1)} %get-tuple-element.28), channel_id=1, source_target_pairs={{0,5},{1,6},{2,7},{3,0},{4,1},{5,2},{6,3},{7,4},{8,13},{9,14},{10,... | collective-permute-start | bytes 399368 | tf_op jit(solution)/shard_map/ppermute | solution.py:363
  147.8 3.8 %collective-permute-start.8 = (s16[8,8320]{1,0:T(8,128)(2,1)S(1)}, s16[8,8320]{1,0:T(8,128)(2,1)S(1)}, u32[]{:S(2)}, u32[]{:S(2)}) collective-permute-start(s16[8,8320]{1,0:T(8,128)(2,1)S(1)} %get-tuple-element.29), channel_id=1, source_target_pairs={{0,6},{1,7},{2,0},{3,1},{4,2},{5,3},{6,4},{7,5},{8,14},{9,15},{10,... | collective-permute-start | bytes 399368 | tf_op jit(solution)/shard_map/ppermute | solution.py:363
  148.9 5.3 %collective-permute-start.9 = (s16[8,8320]{1,0:T(8,128)(2,1)S(1)}, s16[8,8320]{1,0:T(8,128)(2,1)S(1)}, u32[]{:S(2)}, u32[]{:S(2)}) collective-permute-start(s16[8,8320]{1,0:T(8,128)(2,1)S(1)} %get-tuple-element.30), channel_id=1, source_target_pairs={{0,7},{1,0},{2,1},{3,2},{4,3},{5,4},{6,5},{7,6},{8,15},{9,8},{10,9... | collective-permute-start | bytes 399368 | tf_op jit(solution)/shard_map/ppermute | solution.py:363
  154.6 10.1 %collective-permute-start.11 = (f32[8,8192]{1,0:T(8,128)S(1)}, f32[8,8192]{1,0:T(8,128)S(1)}, u32[]{:S(2)}, u32[]{:S(2)}) collective-permute-start(f32[8,8192]{1,0:T(8,128)S(1)} %total.1.here), channel_id=1, source_target_pairs={{8,0},{16,8},{24,16},{32,24},{40,32},{48,40},{56,48},{64,56},{72,6... | collective-permute-start | bytes 786440 | tf_op jit(solution)/shard_map/ppermute | solution.py:373
  156.5 9.4 %collective-permute-start.10 = (f32[8,8192]{1,0:T(8,128)S(1)}, f32[8,8192]{1,0:T(8,128)S(1)}, u32[]{:S(2)}, u32[]{:S(2)}) collective-permute-start(f32[8,8192]{1,0:T(8,128)S(1)} %total.1.here), channel_id=1, source_target_pairs={{0,8},{8,16},{16,24},{24,32},{32,40},{40,48},{48,56},{56,64},{64,7... | collective-permute-start | bytes 786440 | tf_op jit(solution)/shard_map/ppermute | solution.py:374
  166.6 9.7 %collective-permute-start.18 = (s16[8,8320]{1,0:T(8,128)(2,1)S(1)}, s16[8,8320]{1,0:T(8,128)(2,1)S(1)}, u32[]{:S(2)}, u32[]{:S(2)}) collective-permute-start(s16[8,8320]{1,0:T(8,128)(2,1)S(1)} %back.1.refs_0_), channel_id=1, source_target_pairs={{0,7},{1,0},{2,1},{3,2},{4,3},{5,4},{6,5},{7,6},{8,15},{9,8},{10,9... | collective-permute-start | bytes 399368 | tf_op jit(solution)/shard_map/ppermute | solution.py:389
  171.3 5.4 %collective-permute-start.17 = (s16[8,8320]{1,0:T(8,128)(2,1)S(1)}, s16[8,8320]{1,0:T(8,128)(2,1)S(1)}, u32[]{:S(2)}, u32[]{:S(2)}) collective-permute-start(s16[8,8320]{1,0:T(8,128)(2,1)S(1)} %back.1.refs_0_), channel_id=1, source_target_pairs={{0,6},{1,7},{2,0},{3,1},{4,2},{5,3},{6,4},{7,5},{8,14},{9,15},{10,... | collective-permute-start | bytes 399368 | tf_op jit(solution)/shard_map/ppermute | solution.py:389
  171.3 8.0 %collective-permute-start.16 = (s16[8,8320]{1,0:T(8,128)(2,1)S(1)}, s16[8,8320]{1,0:T(8,128)(2,1)S(1)}, u32[]{:S(2)}, u32[]{:S(2)}) collective-permute-start(s16[8,8320]{1,0:T(8,128)(2,1)S(1)} %back.1.refs_0_), channel_id=1, source_target_pairs={{0,5},{1,6},{2,7},{3,0},{4,1},{5,2},{6,3},{7,4},{8,13},{9,14},{10,... | collective-permute-start | bytes 399368 | tf_op jit(solution)/shard_map/ppermute | solution.py:389
  171.6 8.0 %collective-permute-start.15 = (s16[8,8320]{1,0:T(8,128)(2,1)S(1)}, s16[8,8320]{1,0:T(8,128)(2,1)S(1)}, u32[]{:S(2)}, u32[]{:S(2)}) collective-permute-start(s16[8,8320]{1,0:T(8,128)(2,1)S(1)} %back.1.refs_0_), channel_id=1, source_target_pairs={{0,4},{1,5},{2,6},{3,7},{4,0},{5,1},{6,2},{7,3},{8,12},{9,13},{10,... | collective-permute-start | bytes 399368 | tf_op jit(solution)/shard_map/ppermute | solution.py:389
  174.6 8.9 %collective-permute-start.14 = (s16[8,8320]{1,0:T(8,128)(2,1)S(1)}, s16[8,8320]{1,0:T(8,128)(2,1)S(1)}, u32[]{:S(2)}, u32[]{:S(2)}) collective-permute-start(s16[8,8320]{1,0:T(8,128)(2,1)S(1)} %back.1.refs_0_), channel_id=1, source_target_pairs={{0,3},{1,4},{2,5},{3,6},{4,7},{5,0},{6,1},{7,2},{8,11},{9,12},{10,... | collective-permute-start | bytes 399368 | tf_op jit(solution)/shard_map/ppermute | solution.py:389
  176.3 10.0 %collective-permute-start.13 = (s16[8,8320]{1,0:T(8,128)(2,1)S(1)}, s16[8,8320]{1,0:T(8,128)(2,1)S(1)}, u32[]{:S(2)}, u32[]{:S(2)}) collective-permute-start(s16[8,8320]{1,0:T(8,128)(2,1)S(1)} %back.1.refs_0_), channel_id=1, source_target_pairs={{0,2},{1,3},{2,4},{3,5},{4,6},{5,7},{6,0},{7,1},{8,10},{9,11},{10,... | collective-permute-start | bytes 399368 | tf_op jit(solution)/shard_map/ppermute | solution.py:389
  176.7 9.6 %collective-permute-start.12 = (s16[8,8320]{1,0:T(8,128)(2,1)S(1)}, s16[8,8320]{1,0:T(8,128)(2,1)S(1)}, u32[]{:S(2)}, u32[]{:S(2)}) collective-permute-start(s16[8,8320]{1,0:T(8,128)(2,1)S(1)} %back.1.refs_0_), channel_id=1, source_target_pairs={{0,1},{1,2},{2,3},{3,4},{4,5},{5,6},{6,7},{7,0},{8,9},{9,10},{10,1... | collective-permute-start | bytes 399368 | tf_op jit(solution)/shard_map/ppermute | solution.py:389
  (4 other events, 6.4 us)

commit v2 on v1

--- a/solution.py
+++ b/solution.py
@@ -6,6 +6,7 @@
 from jax.experimental import pallas as pl
 from jax.experimental.pallas import tpu as pltpu
 from jax.sharding import PartitionSpec as P
+
 
 RADIUS = 8
 LANES = 128
@@ -65,22 +66,31 @@
     return upper + lower + here + 10.0 * total
 
 
-def cols_left(block, count):
-    return pltpu.roll(block, block.shape[1] - count, 1)
+def moved(block, count):
+    width = block.shape[1]
+    return pltpu.roll(block, (width - count) % width, 1)
 
 
 def col_filter(block):
-    for _ in range(2):
-        first = block
-        for count in (1, 2, 4):
-            block = block + cols_left(block, count)
-        block = block + cols_left(first, 8)
+    for step in (1, 3):
+        near = moved(block, step) + moved(block, -step)
+        far = moved(block, 2 * step) + moved(block, -2 * step)
+        block = 3.0 * block + 2.0 * near + far
     return block
 
 
-def moved_right(carry, block):
-    joined = jnp.concatenate([carry, block], axis=1)
-    return pltpu.roll(joined, RADIUS, 1)[:, LANES:]
+def padded_cols(index, width):
+    return pl.ds(pl.multiple_of(index * width, LANES), width + 2 * LANES)
+
+
+def inner_cols(index, width):
+    return pl.ds(pl.multiple_of(index * width + LANES, LANES), width)
+
+
+def clear_ends(ref):
+    count = ref.shape[1]
+    ref[:, :LANES] = jnp.zeros((8, LANES), f32)
+    ref[:, count - LANES :] = jnp.zeros((8, LANES), f32)
 
 
 def decode_scale(code):
@@ -93,7 +103,7 @@
 
 
 def to_i16(values):
-    return jnp.floor(values + 0.5).astype(jnp.int32).astype(i16)
+    return jnp.round(values).astype(jnp.int32).astype(i16)
 
 
 def wide(tile, width):
@@ -107,15 +117,9 @@
     return parts[0]
 
 
-def encode(source, target, count, width):
-    largest = lax.fori_loop(
-        0,
-        count // width,
-        lambda c, m: jnp.maximum(m, folded_max(jnp.abs(source[:, cols(c, width)]))),
-        jnp.zeros((8, LANES), f32),
-    )
-    level = scale_code(largest)
-    code = level.astype(jnp.int32).astype(i16)
+def encode(source, largest, target, width):
+    count = source.shape[1]
+    code = scale_code(largest).astype(jnp.int32).astype(i16)
     target[:, count : count + LANES] = code
     inverse = wide(1.0 / decode_scale(code), width)
 
@@ -126,7 +130,7 @@
     lax.fori_loop(0, count // width, step, 0)
 
 
-def prepare_kernel(design, state, adjoint, edge, code, *, width):
+def edge_kernel(state, adjoint, edge, *, width):
     ids = row_ids(width)
 
     def step(c, none):
@@ -136,37 +140,43 @@
         for place, row in enumerate(rows):
             first = jnp.where(ids == place + 1, pltpu.roll(row.astype(f32), place + 1, 0), first)
         edge[:, at] = first[:4].astype(jnp.bfloat16)
-        code[:, at] = to_i16(design[:, at] * DESIGN_STEPS)
-        return none
-
-    lax.fori_loop(0, design.shape[1] // width, step, 0)
+        return none
+
+    lax.fori_loop(0, edge.shape[1] // width, step, 0)
 
 
 def element_kernel(omega_sq, assign, state, adjoint, edge, elastic, inertia, *, width):
     omega = omega_sq[assign[0]]
     ids = row_ids(width)
     count = elastic.shape[1] // width
-    whole = width + LANES
 
     def shifted(block, carry):
-        return cols_left(jnp.concatenate([block, carry], axis=1), 1)[:, :width]
+        return moved(jnp.concatenate([block, carry], axis=1), 1)[:, :width]
 
     def step(c, carries):
         at = cols(count - 1 - c, width)
         edges = edge[:, at].astype(f32)
+        edges_next = shifted(edges, carries[4])
+        edges_plus = edges + edges_next
+        edges_minus = edges - edges_next
         fields = [state[0, 0, :, at], state[1, 0, :, at], adjoint[0, 0, :, at], adjoint[1, 0, :, at]]
         kept = []
         parts = []
         for place, field in enumerate(fields):
             here = field.astype(f32)
-            row = jnp.broadcast_to(edges[place : place + 1], here.shape)
-            below = jnp.where(ids == 7, row, pltpu.roll(here, 7, 0))
-            plus = here + below
-            minus = here - below
-            kept += [plus[:, :LANES], minus[:, :LANES]]
-            plus_next = shifted(plus, carries[2 * place])
-            minus_next = shifted(minus, carries[2 * place + 1])
-            parts.append((plus + plus_next, plus - plus_next, minus + minus_next, minus - minus_next))
+            kept.append(here[:, :LANES])
+            following = shifted(here, carries[place])
+            plus = here + following
+            minus = here - following
+
+            def below(block, edge_rows):
+                row = jnp.broadcast_to(edge_rows[place : place + 1], block.shape)
+                return jnp.where(ids == 7, row, pltpu.roll(block, 7, 0))
+
+            plus_below = below(plus, edges_plus)
+            minus_below = below(minus, edges_minus)
+            parts.append((plus + plus_below, minus + minus_below, plus - plus_below, minus - minus_below))
+        kept.append(edges[:, :LANES])
         sr, si, ar, ai = parts
         same = [ar[k] * sr[k] - ai[k] * si[k] for k in range(4)]
         cross = [ar[k] * si[k] + ai[k] * sr[k] for k in range(1, 4)]
@@ -178,53 +188,46 @@
         inertia[:, at] = mass * (omega * (1.0 / 36.0))
         return tuple(kept)
 
-    lax.fori_loop(0, count, step, tuple(jnp.zeros((8, LANES), f32) for _ in range(8)))
-
-
-def partial_kernel(place, design, above, below, passive, elastic, inertia, inverse, *refs, width):
+    zeros = jnp.zeros((8, LANES), f32)
+    lax.fori_loop(0, count, step, (zeros, zeros, zeros, zeros, zeros[:4]))
+
+
+def partial_kernel(place, design, above, below, passive, elastic, inertia, inverse, *refs):
     outs, (rowed, spread, blocks) = refs[:-3], refs[-3:]
-    count = design.shape[1] // width
     peers = len(outs)
     piece = design.shape[1] // peers
-    zeros = jnp.zeros((8, LANES), f32)
-
-    def filter_rows(c, carry):
-        at = cols(c, width)
+    narrow = 2048
+    clear_ends(rowed)
+    clear_ends(spread)
+
+    def filter_rows(c, none):
+        at = cols(c, narrow)
         upper = above[:, at].astype(jnp.int32).astype(f32) * (1.0 / DESIGN_STEPS)
         lower = below[:, at].astype(jnp.int32).astype(f32) * (1.0 / DESIGN_STEPS)
-        block = row_filter(upper, design[:, at], lower)
-        rowed[:, at] = moved_right(carry, block)
-        return block[:, width - LANES :]
-
-    last = lax.fori_loop(0, count, filter_rows, zeros)
-    rowed[:, count * width :] = moved_right(last, zeros)
-
-    def scale(c, carry):
-        at = cols(c, width)
-        window = rowed[:, pl.ds(pl.multiple_of(c * width, width), width + LANES)]
+        rowed[:, inner_cols(c, narrow)] = row_filter(upper, design[:, at], lower)
+        return none
+
+    lax.fori_loop(0, design.shape[1] // narrow, filter_rows, 0)
+
+    def scale(c, none):
+        at = cols(c, piece)
         weights = inverse[:, at]
-        tilde = col_filter(window)[:, :width] * weights
+        tilde = col_filter(rowed[:, padded_cols(c, piece)])[:, LANES : LANES + piece] * weights
         steep = jnp.tanh(SHARPNESS * (tilde - THRESHOLD))
         solid = passive[:, at] > 0
         density = jnp.where(solid, 1.0, (TANH_HALF + steep) * (0.5 / TANH_HALF))
         slope = jnp.where(solid, 0.0, (1.0 - steep * steep) * (SHARPNESS * 0.5 / TANH_HALF))
         block = (density * density * elastic[:, at] - inertia[:, at]) * (slope * weights)
-        spread[:, at] = moved_right(carry, block)
-        return block[:, width - LANES :]
-
-    last = lax.fori_loop(0, count, scale, zeros)
-    spread[:, count * width :] = moved_right(last, zeros)
+        spread[:, inner_cols(c, piece)] = block
+        return none
+
+    lax.fori_loop(0, peers, scale, 0)
 
     for shift in range(peers):
-        start = lax.rem(place[0] + shift, peers) * piece
-
-        def filter_cols(c, none):
-            at = pl.ds(pl.multiple_of(start + c * width, width), width + LANES)
-            blocks[:, cols(c, width)] = col_filter(spread[:, at])[:, :width]
-            return none
-
-        lax.fori_loop(0, piece // width, filter_cols, 0)
-        encode(blocks, outs[shift], piece, width)
+        source = lax.rem(place[0] + shift, peers)
+        block = col_filter(spread[:, padded_cols(source, piece)])[:, LANES : LANES + piece]
+        blocks[...] = block
+        encode(blocks, folded_max(jnp.abs(block)), outs[shift], narrow)
 
 
 def sum_kernel(*refs, width):
@@ -247,13 +250,14 @@
 def back_kernel(above, here, below, out, blocks, *, width):
     piece = here.shape[1]
 
-    def step(c, none):
+    def step(c, largest):
         at = cols(c, width)
-        blocks[:, at] = row_filter(above[:, at], here[:, at], below[:, at])
-        return none
-
-    lax.fori_loop(0, piece // width, step, 0)
-    encode(blocks, out, piece, width)
+        block = row_filter(above[:, at], here[:, at], below[:, at])
+        blocks[:, at] = block
+        return jnp.maximum(largest, folded_max(jnp.abs(block)))
+
+    largest = lax.fori_loop(0, piece // width, step, jnp.zeros((8, LANES), f32))
+    encode(blocks, largest, out, width)
 
 
 def decode_kernel(place, *refs, width):
@@ -298,7 +302,7 @@
     return ((RADIUS + 1) ** 2 - missing).astype(f32)
 
 
-def shards(design, passive, state, adjoint, omega_sq, assign):
+def layer(design, passive, state, adjoint, omega_sq, assign):
     slab_rows, width = design.shape
     rows = lax.axis_size("rows")
     peers = lax.axis_size("freq")
@@ -309,18 +313,20 @@
     place = lax.axis_index("freq").astype(jnp.int32).reshape(1)
     smem = pl.BlockSpec(memory_space=pltpu.SMEM)
 
-    edge, code = pl.pallas_call(
-        functools.partial(prepare_kernel, width=512),
-        out_shape=[
-            jax.ShapeDtypeStruct((4, width), jnp.bfloat16),
-            jax.ShapeDtypeStruct((slab_rows, width), i16),
-        ],
-        in_specs=vmem(3),
-        out_specs=vmem(2),
-        compiler_params=params(16),
-        name="prepare",
-    )(design, state, adjoint)
+    edge_width = 8192
+    field_block = pl.BlockSpec((2, 1, slab_rows, edge_width), lambda c: (0, 0, 0, c))
+    edge = pl.pallas_call(
+        functools.partial(edge_kernel, width=1024),
+        grid=(width // edge_width,),
+        out_shape=jax.ShapeDtypeStruct((4, width), jnp.bfloat16),
+        in_specs=[field_block, field_block],
+        out_specs=pl.BlockSpec((4, edge_width), lambda c: (0, c)),
+        compiler_params=params(8),
+        cost_estimate=cost(8 * slab_rows * width, 4 * 1024 * 1024),
+        name="edge",
+    )(state, adjoint)
     edge_below = lax.ppermute(edge, "rows", down)
+    code = jnp.round(design * DESIGN_STEPS).astype(i16)
     code_below = lax.ppermute(code, "rows", down)
     code_above = lax.ppermute(code, "rows", up)
 
@@ -332,7 +338,7 @@
 
     slab = jax.ShapeDtypeStruct((slab_rows, width), f32)
     elastic, inertia = pl.pallas_call(
-        functools.partial(element_kernel, width=256),
+        functools.partial(element_kernel, width=2048),
         out_shape=[slab, slab],
         in_specs=[smem, smem] + vmem(3),
         out_specs=vmem(2),
@@ -343,13 +349,13 @@
 
     coded_piece = jax.ShapeDtypeStruct((slab_rows, piece + LANES), i16)
     sent = pl.pallas_call(
-        functools.partial(partial_kernel, width=1024),
+        partial_kernel,
         out_shape=[coded_piece] * peers,
         in_specs=[smem] + vmem(7),
         out_specs=vmem(peers),
         scratch_shapes=[
-            pltpu.VMEM((slab_rows, width + LANES), f32),
-            pltpu.VMEM((slab_rows, width + LANES), f32),
+            pltpu.VMEM((slab_rows, width + 2 * LANES), f32),
+            pltpu.VMEM((slab_rows, width + 2 * LANES), f32),
             pltpu.VMEM((slab_rows, piece), f32),
         ],
         compiler_params=params(32),
@@ -410,7 +416,7 @@
 
 def solution(mesh):
     return jax.shard_map(
-        shards,
+        layer,
         mesh=mesh,
         in_specs=(
             P("rows", None),

time: 213 us -> 135 us (0.63)
  Pallas kernels: 108 us -> 35.3 us
  local copies, waits for them, and re-layouts: 7.96 us -> 4.79 us
  waiting for transfers between devices: 27.3 us -> 25 us
    pallas_call x7, Pallas kernels: 108 us -> 35.3 us  [the longest x1 17.2 us: layer(): pl.pallas_call(partial_kernel, out_shape=[coded_piece] * peers, in_specs=...]
    unnamed x18 -> x14, local copies, waits for them, and re-layouts: 7.96 us -> 4.79 us
    convert_element_type x0 -> x1, other arithmetic: none -> 3.02 us  [layer(): code = jnp.round(design * DESIGN_STEPS).astype(i16)]
    ppermute x19, waiting for transfers between devices: 27.3 us -> 25 us  [the longest x7 9.85 us: layer(): pieces.append(lax.ppermute(result, 'freq', route))]
  transfers between devices with their start and end apart: 19 -> 19, of which waited for: 10 -> 11; matrix products, arithmetic and copies ran while one was open for 1% -> 0% of each run, Pallas kernels for 13% -> 11%
where the time goes in v2:
time: 135 us; the launch traced here: 134 us
  starting transfers between devices  41.9 us (31%)
  Pallas kernels  35.3 us (26%)
  waiting for transfers between devices  25 us (19%)
  blocking collectives  23.1 us (17%)
  local copies, waits for them, and re-layouts  4.79 us (4%)
  other arithmetic  3.51 us (3%)
    all_to_all x1, blocking collectives, layer(): squares = lax.all_to_all(squares, 'rows', 0, 0, tiled=True)  23.1 us
    pallas_call x1, Pallas kernels, layer(): pl.pallas_call(partial_kernel, out_shape=[coded_piece] * peers, in_specs=...  17.2 us
    ppermute x7, starting transfers between devices, layer(): received.append(lax.ppermute(sent[shift], 'freq', route))  13.2 us
    pallas_call x1, Pallas kernels, layer(): pl.pallas_call(functools.partial(element_kernel, width=2048), out_shape=[...  11 us
    ppermute x7, starting transfers between devices, layer(): pieces.append(lax.ppermute(result, 'freq', route))  10.2 us
    ppermute x7, waiting for transfers between devices, layer(): pieces.append(lax.ppermute(result, 'freq', route))  9.85 us
    ppermute x1, waiting for transfers between devices, layer(): edge_below = lax.ppermute(edge, 'rows', down)  6.5 us
    ppermute x1, starting transfers between devices, layer(): spread_above = lax.ppermute(spread, 'rows', up)  6.09 us
  transfers between devices with their start and end apart: 19, of which 11 were waited for; matrix products, arithmetic and copies ran while one was open for 0% of the time, Pallas kernels for 11%

profile of v2, /device:TPU:1, one launch (start us, length us, event | category | flops | bytes accessed | tf_op | source)
XLA Modules:
  0.0 134.4 jit_solution(14336692181614872407)
XLA Ops:
  0.0 3.0 %round-nearest-even_convert_fusion = s16[8,65536]{1,0:T(8,128)(2,1)} fusion(f32[8,65536]{1,0:T(8,128)} %design.1), kind=kLoop, calls=%fused_computation.1 | loop fusion | flops 1572864 | bytes 3145728 | tf_op jit(solution)/shard_map/convert_element_type | solution.py:329
  3.0 5.1 %collective-permute-start.1 = (s16[8,65536]{1,0:T(8,128)(2,1)}, s16[8,65536]{1,0:T(8,128)(2,1)S(1)}, u32[]{:S(2)}, u32[]{:S(2)}) collective-permute-start(s16[8,65536]{1,0:T(8,128)(2,1)} %round-nearest-even_convert_fusion), channel_id=1, source_target_pairs={{8,0},{16,8},{24,16},{32,24},{40,32},{48,40},{56,48},{64,56},{72,6... | collective-permute-start | bytes 3145736 | tf_op jit(solution)/shard_map/ppermute | solution.py:330
  8.1 1.9 %collective-permute-start = (s16[8,65536]{1,0:T(8,128)(2,1)}, s16[8,65536]{1,0:T(8,128)(2,1)}, u32[]{:S(2)}, u32[]{:S(2)}) collective-permute-start(s16[8,65536]{1,0:T(8,128)(2,1)} %round-nearest-even_convert_fusion), channel_id=1, source_target_pairs={{0,8},{8,16},{16,24},{24,32},{32,40},{40,48},{48,56},{56,64},{64,7... | collective-permute-start | bytes 3145736 | tf_op jit(solution)/shard_map/ppermute | solution.py:331
  11.7 3.5 %edge.1 = bf16[4,65536]{1,0:T(4,128)(2,1)} custom-call(bf16[2,1,8,65536]{3,2,1,0:T(8,128)(2,1)S(1)} %copy-done.1, bf16[2,1,8,65536]{3,2,1,0:T(8,128)(2,1)S(1)} %copy-done.3), custom_call_target="tpu_custom_call" | custom-call | flops 4194304 | bytes 4194304 | tf_op jit(solution)/shard_map/edge/pallas_call | solution.py:318
  15.1 3.5 %collective-permute-start.2 = (bf16[4,65536]{1,0:T(4,128)(2,1)}, bf16[4,65536]{1,0:T(4,128)(2,1)}, u32[]{:S(2)}, u32[]{:S(2)}) collective-permute-start(bf16[4,65536]{1,0:T(4,128)(2,1)} %edge.1), channel_id=1, source_target_pairs={{8,0},{16,8},{24,16},{32,24},{40,32},{48,40},{56,48},{64,56},{72,6... | collective-permute-start | bytes 1572872 | tf_op jit(solution)/shard_map/ppermute | solution.py:328
  19.8 6.5 %collective-permute-done.2.edge = bf16[4,65536]{1,0:T(4,128)(2,1)} collective-permute-done((bf16[4,65536]{1,0:T(4,128)(2,1)}, bf16[4,65536]{1,0:T(4,128)(2,1)}, u32[]{:S(2)}, u32[]{:S(2)}) %collective-permute-start.2) | collective-permute-done | bytes 524320 | tf_op jit(solution)/shard_map/ppermute | solution.py:328
  26.3 1.6 %copy-done.2 = bf16[2,1,8,65536]{3,2,1,0:T(8,128)(2,1)S(1)} copy-done((bf16[2,1,8,65536]{3,2,1,0:T(8,128)(2,1)S(1)}, bf16[2,1,8,65536]{3,2,1,0:T(8,128)(2,1)}, u32[]{:S(2)}) %copy-start.2) | copy-done | bytes 2097176
  29.5 11.0 %element.1 = (f32[8,65536]{1,0:T(8,128)S(1)}, f32[8,65536]{1,0:T(8,128)S(1)}) custom-call(f32[8]{0:T(128)S(1)} %copy-done.6, s32[1]{0:T(128)S(6)} %copy.7.assign, bf16[2,1,8,65536]{3,2,1,0:T(8,128)(2,1)S(1)} %copy-done.2, bf16[2,1,8,65536]{3,2,1,0:T(8,128)(2,1)S(1)} %copy-done.4, bf16[4,65536]{1,0:T(4,128)(2,1)} %collective-permute-done.2.edge), custom_call_target="tpu_custom_call" | custom-call | flops 41943040 | bytes 8388608 | tf_op jit(solution)/shard_map/element/pallas_call | solution.py:340
  40.6 17.2 %partial.1 = (s16[8,8320]{1,0:T(8,128)(2,1)S(1)}, s16[8,8320]{1,0:T(8,128)(2,1)S(1)}, s16[8,8320]{1,0:T(8,128)(2,1)S(1)}, s16[8,8320]{1,0:T(8,128)(2,1)S(1)}, s1...) custom-call(s32[1]{0:T(128)} %bitcast.place, ...), custom_call_target="tpu_custom_call" | custom-call | flops 78643200 | bytes 14680064 | tf_op jit(solution)/shard_map/partial/pallas_call | solution.py:351
  57.8 2.8 %collective-permute-start.3 = (s16[8,8320]{1,0:T(8,128)(2,1)S(1)}, s16[8,8320]{1,0:T(8,128)(2,1)S(1)}, u32[]{:S(2)}, u32[]{:S(2)}) collective-permute-start(s16[8,8320]{1,0:T(8,128)(2,1)S(1)} %get-tuple-element.20), channel_id=1, source_target_pairs={{0,1},{1,2},{2,3},{3,4},{4,5},{5,6},{6,7},{7,0},{8,9},{9,10},{10,1... | collective-permute-start | bytes 399368 | tf_op jit(solution)/shard_map/ppermute | solution.py:369
  61.9 2.0 %collective-permute-start.5 = (s16[8,8320]{1,0:T(8,128)(2,1)S(1)}, s16[8,8320]{1,0:T(8,128)(2,1)S(1)}, u32[]{:S(2)}, u32[]{:S(2)}) collective-permute-start(s16[8,8320]{1,0:T(8,128)(2,1)S(1)} %get-tuple-element.22), channel_id=1, source_target_pairs={{0,3},{1,4},{2,5},{3,6},{4,7},{5,0},{6,1},{7,2},{8,11},{9,12},{10,... | collective-permute-start | bytes 399368 | tf_op jit(solution)/shard_map/ppermute | solution.py:369
  65.4 4.5 %collective-permute-start.7 = (s16[8,8320]{1,0:T(8,128)(2,1)S(1)}, s16[8,8320]{1,0:T(8,128)(2,1)S(1)}, u32[]{:S(2)}, u32[]{:S(2)}) collective-permute-start(s16[8,8320]{1,0:T(8,128)(2,1)S(1)} %get-tuple-element.24), channel_id=1, source_target_pairs={{0,5},{1,6},{2,7},{3,0},{4,1},{5,2},{6,3},{7,4},{8,13},{9,14},{10,... | collective-permute-start | bytes 399368 | tf_op jit(solution)/shard_map/ppermute | solution.py:369
  71.1 1.8 %collective-permute-done.7.refs_5_ = s16[8,8320]{1,0:T(8,128)(2,1)S(1)} collective-permute-done((s16[8,8320]{1,0:T(8,128)(2,1)S(1)}, s16[8,8320]{1,0:T(8,128)(2,1)S(1)}, u32[]{:S(2)}, u32[]{:S(2)}) %collective-permute-start.7) | collective-permute-done | bytes 133152 | tf_op jit(solution)/shard_map/ppermute | solution.py:369
  74.4 1.9 %collective-permute-done.9.refs_7_ = s16[8,8320]{1,0:T(8,128)(2,1)S(1)} collective-permute-done((s16[8,8320]{1,0:T(8,128)(2,1)S(1)}, s16[8,8320]{1,0:T(8,128)(2,1)S(1)}, u32[]{:S(2)}, u32[]{:S(2)}) %collective-permute-start.9) | collective-permute-done | bytes 133152 | tf_op jit(solution)/shard_map/ppermute | solution.py:369
  76.6 1.9 %collective-permute-start.11 = (f32[8,8192]{1,0:T(8,128)S(1)}, f32[8,8192]{1,0:T(8,128)S(1)}, u32[]{:S(2)}, u32[]{:S(2)}) collective-permute-start(f32[8,8192]{1,0:T(8,128)S(1)} %total.1.here), channel_id=1, source_target_pairs={{8,0},{16,8},{24,16},{32,24},{40,32},{48,40},{56,48},{64,56},{72,6... | collective-permute-start | bytes 786440 | tf_op jit(solution)/shard_map/ppermute | solution.py:379
  78.6 6.1 %collective-permute-start.10 = (f32[8,8192]{1,0:T(8,128)S(1)}, f32[8,8192]{1,0:T(8,128)S(1)}, u32[]{:S(2)}, u32[]{:S(2)}) collective-permute-start(f32[8,8192]{1,0:T(8,128)S(1)} %total.1.here), channel_id=1, source_target_pairs={{0,8},{8,16},{16,24},{24,32},{32,40},{40,48},{48,56},{56,64},{64,7... | collective-permute-start | bytes 786440 | tf_op jit(solution)/shard_map/ppermute | solution.py:380
  84.7 2.1 %collective-permute-done.11.below = f32[8,8192]{1,0:T(8,128)S(1)} collective-permute-done((f32[8,8192]{1,0:T(8,128)S(1)}, f32[8,8192]{1,0:T(8,128)S(1)}, u32[]{:S(2)}, u32[]{:S(2)}) %collective-permute-start.11) | collective-permute-done | bytes 262176 | tf_op jit(solution)/shard_map/ppermute | solution.py:379
  88.5 4.9 %collective-permute-start.18 = (s16[8,8320]{1,0:T(8,128)(2,1)S(1)}, s16[8,8320]{1,0:T(8,128)(2,1)S(1)}, u32[]{:S(2)}, u32[]{:S(2)}) collective-permute-start(s16[8,8320]{1,0:T(8,128)(2,1)S(1)} %back.1.refs_0_), channel_id=1, source_target_pairs={{0,7},{1,0},{2,1},{3,2},{4,3},{5,4},{6,5},{7,6},{8,15},{9,8},{10,9... | collective-permute-start | bytes 399368 | tf_op jit(solution)/shard_map/ppermute | solution.py:395
  93.7 2.9 %collective-permute-start.15 = (s16[8,8320]{1,0:T(8,128)(2,1)S(1)}, s16[8,8320]{1,0:T(8,128)(2,1)S(1)}, u32[]{:S(2)}, u32[]{:S(2)}) collective-permute-start(s16[8,8320]{1,0:T(8,128)(2,1)S(1)} %back.1.refs_0_), channel_id=1, source_target_pairs={{0,4},{1,5},{2,6},{3,7},{4,0},{5,1},{6,2},{7,3},{8,12},{9,13},{10,... | collective-permute-start | bytes 399368 | tf_op jit(solution)/shard_map/ppermute | solution.py:395
  97.3 1.9 %collective-permute-done.18.refs_7_ = s16[8,8320]{1,0:T(8,128)(2,1)S(1)} collective-permute-done((s16[8,8320]{1,0:T(8,128)(2,1)S(1)}, s16[8,8320]{1,0:T(8,128)(2,1)S(1)}, u32[]{:S(2)}, u32[]{:S(2)}) %collective-permute-start.18) | collective-permute-done | bytes 133152 | tf_op jit(solution)/shard_map/ppermute | solution.py:395
  101.6 4.4 %collective-permute-done.14.refs_3_ = s16[8,8320]{1,0:T(8,128)(2,1)S(1)} collective-permute-done((s16[8,8320]{1,0:T(8,128)(2,1)S(1)}, s16[8,8320]{1,0:T(8,128)(2,1)S(1)}, u32[]{:S(2)}, u32[]{:S(2)}) %collective-permute-start.14) | collective-permute-done | bytes 133152 | tf_op jit(solution)/shard_map/ppermute | solution.py:395
  106.0 2.5 %collective-permute-done.13.refs_2_ = s16[8,8320]{1,0:T(8,128)(2,1)S(1)} collective-permute-done((s16[8,8320]{1,0:T(8,128)(2,1)S(1)}, s16[8,8320]{1,0:T(8,128)(2,1)S(1)}, u32[]{:S(2)}, u32[]{:S(2)}) %collective-permute-start.13) | collective-permute-done | bytes 133152 | tf_op jit(solution)/shard_map/ppermute | solution.py:395
  109.4 23.1 %all_to_all.5.squares = f32[32,8,128]{2,1,0:T(8,128)S(1)} all-to-all(f32[32,8,128]{2,1,0:T(8,128)S(1)} %get-tuple-element.28), channel_id=1, replica_groups=mesh['rows'=32,'freq'=8] {'rows'}, dimensions={0} | all-to-all | bytes 262144 | tf_op jit(solution)/shard_map/all_to_all | solution.py:405
  132.5 1.9 %scale.1 = f32[8,65536]{1,0:T(8,128)} custom-call(f32[8,65536]{1,0:T(8,128)S(1)} %get-tuple-element.27.back, f32[32,8,128]{2,1,0:T(8,128)S(1)} %all_to_all.5.squares), custom_call_target="tpu_custom_call" | custom-call | tf_op jit(solution)/shard_map/scale/pallas_call | solution.py:407
  (40 shorter events, 15.5 us)
Async XLA Ops:
  0.0 10.1 %copy-start.1 = (bf16[2,1,8,65536]{3,2,1,0:T(8,128)(2,1)S(1)}, bf16[2,1,8,65536]{3,2,1,0:T(8,128)(2,1)}, u32[]{:S(2)}) copy-start(bf16[2,1,8,65536]{3,2,1,0:T(8,128)(2,1)} %state.3) | copy-start | bytes 6291460
  3.0 37.5 %collective-permute-start.1 = (s16[8,65536]{1,0:T(8,128)(2,1)}, s16[8,65536]{1,0:T(8,128)(2,1)S(1)}, u32[]{:S(2)}, u32[]{:S(2)}) collective-permute-start(s16[8,65536]{1,0:T(8,128)(2,1)} %round-nearest-even_convert_fusion), channel_id=1, source_target_pairs={{8,0},{16,8},{24,16},{32,24},{40,32},{48,40},{56,48},{64,56},{72,6... | collective-permute-start | bytes 3145736 | tf_op jit(solution)/shard_map/ppermute | solution.py:330
  8.1 32.4 %collective-permute-start = (s16[8,65536]{1,0:T(8,128)(2,1)}, s16[8,65536]{1,0:T(8,128)(2,1)}, u32[]{:S(2)}, u32[]{:S(2)}) collective-permute-start(s16[8,65536]{1,0:T(8,128)(2,1)} %round-nearest-even_convert_fusion), channel_id=1, source_target_pairs={{0,8},{8,16},{16,24},{24,32},{32,40},{40,48},{48,56},{56,64},{64,7... | collective-permute-start | bytes 3145736 | tf_op jit(solution)/shard_map/ppermute | solution.py:331
  10.1 1.6 %copy-start.3 = (bf16[2,1,8,65536]{3,2,1,0:T(8,128)(2,1)S(1)}, bf16[2,1,8,65536]{3,2,1,0:T(8,128)(2,1)}, u32[]{:S(2)}) copy-start(bf16[2,1,8,65536]{3,2,1,0:T(8,128)(2,1)} %adjoint.3) | copy-start | bytes 6291460
  15.1 11.2 %copy-start.6 = (f32[8]{0:T(128)S(1)}, f32[8]{0:T(128)}, u32[]{:S(2)}) copy-start(f32[8]{0:T(128)} %omega_sq.1) | copy-start | bytes 100
  15.1 11.2 %collective-permute-start.2 = (bf16[4,65536]{1,0:T(4,128)(2,1)}, bf16[4,65536]{1,0:T(4,128)(2,1)}, u32[]{:S(2)}, u32[]{:S(2)}) collective-permute-start(bf16[4,65536]{1,0:T(4,128)(2,1)} %edge.1), channel_id=1, source_target_pairs={{8,0},{16,8},{24,16},{32,24},{40,32},{48,40},{56,48},{64,56},{72,6... | collective-permute-start | bytes 1572872 | tf_op jit(solution)/shard_map/ppermute | solution.py:328
  19.8 20.8 %copy-start = (f32[8,65536]{1,0:T(8,128)S(1)}, f32[8,65536]{1,0:T(8,128)}, u32[]{:S(2)}) copy-start(f32[8,65536]{1,0:T(8,128)} %design.1) | copy-start | bytes 6291460
  29.5 11.1 %copy-start.5 = (s32[8,65536]{1,0:T(8,128)S(1)}, s32[8,65536]{1,0:T(8,128)}, u32[]{:S(2)}) copy-start(s32[8,65536]{1,0:T(8,128)} %passive.1) | copy-start | bytes 6291460
  57.8 12.1 %collective-permute-start.3 = (s16[8,8320]{1,0:T(8,128)(2,1)S(1)}, s16[8,8320]{1,0:T(8,128)(2,1)S(1)}, u32[]{:S(2)}, u32[]{:S(2)}) collective-permute-start(s16[8,8320]{1,0:T(8,128)(2,1)S(1)} %get-tuple-element.20), channel_id=1, source_target_pairs={{0,1},{1,2},{2,3},{3,4},{4,5},{5,6},{6,7},{7,0},{8,9},{9,10},{10,1... | collective-permute-start | bytes 399368 | tf_op jit(solution)/shard_map/ppermute | solution.py:369
  60.6 10.4 %collective-permute-start.4 = (s16[8,8320]{1,0:T(8,128)(2,1)S(1)}, s16[8,8320]{1,0:T(8,128)(2,1)S(1)}, u32[]{:S(2)}, u32[]{:S(2)}) collective-permute-start(s16[8,8320]{1,0:T(8,128)(2,1)S(1)} %get-tuple-element.21), channel_id=1, source_target_pairs={{0,2},{1,3},{2,4},{3,5},{4,6},{5,7},{6,0},{7,1},{8,10},{9,11},{10,... | collective-permute-start | bytes 399368 | tf_op jit(solution)/shard_map/ppermute | solution.py:369
  61.9 9.1 %collective-permute-start.5 = (s16[8,8320]{1,0:T(8,128)(2,1)S(1)}, s16[8,8320]{1,0:T(8,128)(2,1)S(1)}, u32[]{:S(2)}, u32[]{:S(2)}) collective-permute-start(s16[8,8320]{1,0:T(8,128)(2,1)S(1)} %get-tuple-element.22), channel_id=1, source_target_pairs={{0,3},{1,4},{2,5},{3,6},{4,7},{5,0},{6,1},{7,2},{8,11},{9,12},{10,... | collective-permute-start | bytes 399368 | tf_op jit(solution)/shard_map/ppermute | solution.py:369
  63.8 7.3 %collective-permute-start.6 = (s16[8,8320]{1,0:T(8,128)(2,1)S(1)}, s16[8,8320]{1,0:T(8,128)(2,1)S(1)}, u32[]{:S(2)}, u32[]{:S(2)}) collective-permute-start(s16[8,8320]{1,0:T(8,128)(2,1)S(1)} %get-tuple-element.23), channel_id=1, source_target_pairs={{0,4},{1,5},{2,6},{3,7},{4,0},{5,1},{6,2},{7,3},{8,12},{9,13},{10,... | collective-permute-start | bytes 399368 | tf_op jit(solution)/shard_map/ppermute | solution.py:369
  65.4 7.6 %collective-permute-start.7 = (s16[8,8320]{1,0:T(8,128)(2,1)S(1)}, s16[8,8320]{1,0:T(8,128)(2,1)S(1)}, u32[]{:S(2)}, u32[]{:S(2)}) collective-permute-start(s16[8,8320]{1,0:T(8,128)(2,1)S(1)} %get-tuple-element.24), channel_id=1, source_target_pairs={{0,5},{1,6},{2,7},{3,0},{4,1},{5,2},{6,3},{7,4},{8,13},{9,14},{10,... | collective-permute-start | bytes 399368 | tf_op jit(solution)/shard_map/ppermute | solution.py:369
  69.9 4.5 %collective-permute-start.8 = (s16[8,8320]{1,0:T(8,128)(2,1)S(1)}, s16[8,8320]{1,0:T(8,128)(2,1)S(1)}, u32[]{:S(2)}, u32[]{:S(2)}) collective-permute-start(s16[8,8320]{1,0:T(8,128)(2,1)S(1)} %get-tuple-element.25), channel_id=1, source_target_pairs={{0,6},{1,7},{2,0},{3,1},{4,2},{5,3},{6,4},{7,5},{8,14},{9,15},{10,... | collective-permute-start | bytes 399368 | tf_op jit(solution)/shard_map/ppermute | solution.py:369
  70.9 5.3 %collective-permute-start.9 = (s16[8,8320]{1,0:T(8,128)(2,1)S(1)}, s16[8,8320]{1,0:T(8,128)(2,1)S(1)}, u32[]{:S(2)}, u32[]{:S(2)}) collective-permute-start(s16[8,8320]{1,0:T(8,128)(2,1)S(1)} %get-tuple-element.26), channel_id=1, source_target_pairs={{0,7},{1,0},{2,1},{3,2},{4,3},{5,4},{6,5},{7,6},{8,15},{9,8},{10,9... | collective-permute-start | bytes 399368 | tf_op jit(solution)/shard_map/ppermute | solution.py:369
  76.6 10.1 %collective-permute-start.11 = (f32[8,8192]{1,0:T(8,128)S(1)}, f32[8,8192]{1,0:T(8,128)S(1)}, u32[]{:S(2)}, u32[]{:S(2)}) collective-permute-start(f32[8,8192]{1,0:T(8,128)S(1)} %total.1.here), channel_id=1, source_target_pairs={{8,0},{16,8},{24,16},{32,24},{40,32},{48,40},{56,48},{64,56},{72,6... | collective-permute-start | bytes 786440 | tf_op jit(solution)/shard_map/ppermute | solution.py:379
  78.6 9.4 %collective-permute-start.10 = (f32[8,8192]{1,0:T(8,128)S(1)}, f32[8,8192]{1,0:T(8,128)S(1)}, u32[]{:S(2)}, u32[]{:S(2)}) collective-permute-start(f32[8,8192]{1,0:T(8,128)S(1)} %total.1.here), channel_id=1, source_target_pairs={{0,8},{8,16},{16,24},{24,32},{32,40},{40,48},{48,56},{56,64},{64,7... | collective-permute-start | bytes 786440 | tf_op jit(solution)/shard_map/ppermute | solution.py:380
  88.5 10.7 %collective-permute-start.18 = (s16[8,8320]{1,0:T(8,128)(2,1)S(1)}, s16[8,8320]{1,0:T(8,128)(2,1)S(1)}, u32[]{:S(2)}, u32[]{:S(2)}) collective-permute-start(s16[8,8320]{1,0:T(8,128)(2,1)S(1)} %back.1.refs_0_), channel_id=1, source_target_pairs={{0,7},{1,0},{2,1},{3,2},{4,3},{5,4},{6,5},{7,6},{8,15},{9,8},{10,9... | collective-permute-start | bytes 399368 | tf_op jit(solution)/shard_map/ppermute | solution.py:395
  93.4 5.8 %collective-permute-start.17 = (s16[8,8320]{1,0:T(8,128)(2,1)S(1)}, s16[8,8320]{1,0:T(8,128)(2,1)S(1)}, u32[]{:S(2)}, u32[]{:S(2)}) collective-permute-start(s16[8,8320]{1,0:T(8,128)(2,1)S(1)} %back.1.refs_0_), channel_id=1, source_target_pairs={{0,6},{1,7},{2,0},{3,1},{4,2},{5,3},{6,4},{7,5},{8,14},{9,15},{10,... | collective-permute-start | bytes 399368 | tf_op jit(solution)/shard_map/ppermute | solution.py:395
  93.4 8.2 %collective-permute-start.16 = (s16[8,8320]{1,0:T(8,128)(2,1)S(1)}, s16[8,8320]{1,0:T(8,128)(2,1)S(1)}, u32[]{:S(2)}, u32[]{:S(2)}) collective-permute-start(s16[8,8320]{1,0:T(8,128)(2,1)S(1)} %back.1.refs_0_), channel_id=1, source_target_pairs={{0,5},{1,6},{2,7},{3,0},{4,1},{5,2},{6,3},{7,4},{8,13},{9,14},{10,... | collective-permute-start | bytes 399368 | tf_op jit(solution)/shard_map/ppermute | solution.py:395
  93.7 7.9 %collective-permute-start.15 = (s16[8,8320]{1,0:T(8,128)(2,1)S(1)}, s16[8,8320]{1,0:T(8,128)(2,1)S(1)}, u32[]{:S(2)}, u32[]{:S(2)}) collective-permute-start(s16[8,8320]{1,0:T(8,128)(2,1)S(1)} %back.1.refs_0_), channel_id=1, source_target_pairs={{0,4},{1,5},{2,6},{3,7},{4,0},{5,1},{6,2},{7,3},{8,12},{9,13},{10,... | collective-permute-start | bytes 399368 | tf_op jit(solution)/shard_map/ppermute | solution.py:395
  96.7 9.3 %collective-permute-start.14 = (s16[8,8320]{1,0:T(8,128)(2,1)S(1)}, s16[8,8320]{1,0:T(8,128)(2,1)S(1)}, u32[]{:S(2)}, u32[]{:S(2)}) collective-permute-start(s16[8,8320]{1,0:T(8,128)(2,1)S(1)} %back.1.refs_0_), channel_id=1, source_target_pairs={{0,3},{1,4},{2,5},{3,6},{4,7},{5,0},{6,1},{7,2},{8,11},{9,12},{10,... | collective-permute-start | bytes 399368 | tf_op jit(solution)/shard_map/ppermute | solution.py:395
  99.2 9.3 %collective-permute-start.13 = (s16[8,8320]{1,0:T(8,128)(2,1)S(1)}, s16[8,8320]{1,0:T(8,128)(2,1)S(1)}, u32[]{:S(2)}, u32[]{:S(2)}) collective-permute-start(s16[8,8320]{1,0:T(8,128)(2,1)S(1)} %back.1.refs_0_), channel_id=1, source_target_pairs={{0,2},{1,3},{2,4},{3,5},{4,6},{5,7},{6,0},{7,1},{8,10},{9,11},{10,... | collective-permute-start | bytes 399368 | tf_op jit(solution)/shard_map/ppermute | solution.py:395
  99.2 9.3 %collective-permute-start.12 = (s16[8,8320]{1,0:T(8,128)(2,1)S(1)}, s16[8,8320]{1,0:T(8,128)(2,1)S(1)}, u32[]{:S(2)}, u32[]{:S(2)}) collective-permute-start(s16[8,8320]{1,0:T(8,128)(2,1)S(1)} %back.1.refs_0_), channel_id=1, source_target_pairs={{0,1},{1,2},{2,3},{3,4},{4,5},{5,6},{6,7},{7,0},{8,9},{9,10},{10,1... | collective-permute-start | bytes 399368 | tf_op jit(solution)/shard_map/ppermute | solution.py:395
  (2 other events, 3.2 us)

commit v3 on v2

--- a/solution.py
+++ b/solution.py
@@ -117,66 +117,106 @@
     return parts[0]
 
 
-def encode(source, largest, target, width):
+def encode(source, largest, targets, width):
     count = source.shape[1]
     code = scale_code(largest).astype(jnp.int32).astype(i16)
-    target[:, count : count + LANES] = code
+    for target in targets:
+        target[:, count : count + LANES] = code
     inverse = wide(1.0 / decode_scale(code), width)
 
     def step(c, none):
-        target[:, cols(c, width)] = to_i16(source[:, cols(c, width)] * inverse)
+        values = to_i16(source[:, cols(c, width)] * inverse)
+        for target in targets:
+            target[:, cols(c, width)] = values
         return none
 
     lax.fori_loop(0, count // width, step, 0)
 
 
-def edge_kernel(state, adjoint, edge, *, width):
+def field_copies(sources, kept, arrived, stage, span):
+    at = pl.ds(stage * span, span)
+    whole = lambda ref: (slice(None),) * (len(ref.shape) - 1) + (at,)
+    return [
+        pltpu.make_async_copy(source.at[whole(source)], target.at[whole(target)], arrived.at[stage, place])
+        for place, (source, target) in enumerate(zip(sources, kept))
+    ]
+
+
+def edge_kernel(state_far, adjoint_far, edge, state, adjoint, arrived, *, width, stages):
     ids = row_ids(width)
-
-    def step(c, none):
-        at = cols(c, width)
-        first = state[0, 0, :, at].astype(f32)
-        rows = [state[1, 0, :, at], adjoint[0, 0, :, at], adjoint[1, 0, :, at]]
-        for place, row in enumerate(rows):
-            first = jnp.where(ids == place + 1, pltpu.roll(row.astype(f32), place + 1, 0), first)
-        edge[:, at] = first[:4].astype(jnp.bfloat16)
-        return none
-
-    lax.fori_loop(0, edge.shape[1] // width, step, 0)
-
-
-def element_kernel(omega_sq, assign, state, adjoint, edge, elastic, inertia, *, width):
+    span = edge.shape[1] // stages
+    copies = functools.partial(
+        field_copies, (state_far, adjoint_far), (state, adjoint), arrived, span=span
+    )
+    for stage in range(stages):
+        for copy in copies(stage):
+            copy.start()
+
+    for stage in range(stages):
+        for copy in copies(stage):
+            copy.wait()
+
+        def step(c, none):
+            at = cols(stage * (span // width) + c, width)
+            first = state[0, 0, :, at].astype(f32)
+            rows = [state[1, 0, :, at], adjoint[0, 0, :, at], adjoint[1, 0, :, at]]
+            for place, row in enumerate(rows):
+                first = jnp.where(ids == place + 1, pltpu.roll(row.astype(f32), place + 1, 0), first)
+            edge[:, at] = first[:4].astype(jnp.bfloat16)
+            return none
+
+        lax.fori_loop(0, span // width, step, 0)
+
+
+def element_kernel(
+    omega_sq,
+    assign,
+    state_far,
+    adjoint_far,
+    edge_far,
+    elastic_far,
+    inertia_far,
+    state,
+    adjoint,
+    edge,
+    elastic,
+    inertia,
+    arrived,
+    left,
+    *,
+    width,
+    stages,
+):
     omega = omega_sq[assign[0]]
     ids = row_ids(width)
-    count = elastic.shape[1] // width
+    span = elastic.shape[1] // stages
+    count = span // width
+    copies = functools.partial(
+        field_copies, (state_far, adjoint_far, edge_far), (state, adjoint, edge), arrived, span=span
+    )
+    for stage in reversed(range(stages)):
+        for copy in copies(stage):
+            copy.start()
 
     def shifted(block, carry):
         return moved(jnp.concatenate([block, carry], axis=1), 1)[:, :width]
 
-    def step(c, carries):
-        at = cols(count - 1 - c, width)
+    def step(stage, c, carries):
+        at = cols((stage + 1) * count - 1 - c, width)
         edges = edge[:, at].astype(f32)
-        edges_next = shifted(edges, carries[4])
-        edges_plus = edges + edges_next
-        edges_minus = edges - edges_next
         fields = [state[0, 0, :, at], state[1, 0, :, at], adjoint[0, 0, :, at], adjoint[1, 0, :, at]]
         kept = []
         parts = []
         for place, field in enumerate(fields):
             here = field.astype(f32)
-            kept.append(here[:, :LANES])
-            following = shifted(here, carries[place])
-            plus = here + following
-            minus = here - following
-
-            def below(block, edge_rows):
-                row = jnp.broadcast_to(edge_rows[place : place + 1], block.shape)
-                return jnp.where(ids == 7, row, pltpu.roll(block, 7, 0))
-
-            plus_below = below(plus, edges_plus)
-            minus_below = below(minus, edges_minus)
-            parts.append((plus + plus_below, minus + minus_below, plus - plus_below, minus - minus_below))
-        kept.append(edges[:, :LANES])
+            row = jnp.broadcast_to(edges[place : place + 1], here.shape)
+            below = jnp.where(ids == 7, row, pltpu.roll(here, 7, 0))
+            plus = here + below
+            minus = here - below
+            kept += [plus[:, :LANES], minus[:, :LANES]]
+            plus_next = shifted(plus, carries[2 * place])
+            minus_next = shifted(minus, carries[2 * place + 1])
+            parts.append((plus + plus_next, plus - plus_next, minus + minus_next, minus - minus_next))
         sr, si, ar, ai = parts
         same = [ar[k] * sr[k] - ai[k] * si[k] for k in range(4)]
         cross = [ar[k] * si[k] + ai[k] * sr[k] for k in range(1, 4)]
@@ -188,15 +228,47 @@
         inertia[:, at] = mass * (omega * (1.0 / 36.0))
         return tuple(kept)
 
-    zeros = jnp.zeros((8, LANES), f32)
-    lax.fori_loop(0, count, step, (zeros, zeros, zeros, zeros, zeros[:4]))
-
-
-def partial_kernel(place, design, above, below, passive, elastic, inertia, inverse, *refs):
-    outs, (rowed, spread, blocks) = refs[:-3], refs[-3:]
-    peers = len(outs)
+    def results(stage):
+        at = pl.ds(stage * span, span)
+        return [
+            pltpu.make_async_copy(source.at[:, at], target.at[:, at], left.at[stage, place])
+            for place, (source, target) in enumerate(((elastic, elastic_far), (inertia, inertia_far)))
+        ]
+
+    carries = (jnp.zeros((8, LANES), f32),) * 8
+    for stage in reversed(range(stages)):
+        for copy in copies(stage):
+            copy.wait()
+        carries = lax.fori_loop(0, count, functools.partial(step, stage), carries)
+        for copy in results(stage):
+            copy.start()
+    for stage in reversed(range(stages)):
+        for copy in results(stage):
+            copy.wait()
+
+
+def partial_kernel(*refs, stages):
+    sources, out_far, kept = refs[:7], refs[7], refs[8:15]
+    rowed, spread, blocks, out, arrived, left = refs[15:]
+    design, above, below, passive, elastic, inertia, inverse = kept
+    peers = out.shape[0]
     piece = design.shape[1] // peers
     narrow = 2048
+    span = design.shape[1] // stages
+
+    def early(stage):
+        at = pl.ds(stage * span, span)
+        return [
+            pltpu.make_async_copy(sources[k].at[:, at], kept[k].at[:, at], arrived.at[stage, k])
+            for k in range(3)
+        ]
+
+    late = [pltpu.make_async_copy(sources[k], kept[k], arrived.at[0, k]) for k in range(3, 7)]
+    for stage in range(stages):
+        for copy in early(stage):
+            copy.start()
+    for copy in late:
+        copy.start()
     clear_ends(rowed)
     clear_ends(spread)
 
@@ -207,7 +279,13 @@
         rowed[:, inner_cols(c, narrow)] = row_filter(upper, design[:, at], lower)
         return none
 
-    lax.fori_loop(0, design.shape[1] // narrow, filter_rows, 0)
+    for stage in range(stages):
+        for copy in early(stage):
+            copy.wait()
+        first = stage * (span // narrow)
+        lax.fori_loop(first, first + span // narrow, filter_rows, 0)
+    for copy in late:
+        copy.wait()
 
     def scale(c, none):
         at = cols(c, piece)
@@ -223,23 +301,27 @@
 
     lax.fori_loop(0, peers, scale, 0)
 
-    for shift in range(peers):
-        source = lax.rem(place[0] + shift, peers)
-        block = col_filter(spread[:, padded_cols(source, piece)])[:, LANES : LANES + piece]
+    def send(peer, none):
+        block = col_filter(spread[:, padded_cols(peer, piece)])[:, LANES : LANES + piece]
         blocks[...] = block
-        encode(blocks, folded_max(jnp.abs(block)), outs[shift], narrow)
-
-
-def sum_kernel(*refs, width):
-    coded, out = refs[:-1], refs[-1]
-    piece = out.shape[1]
-    scales = [decode_scale(ref[:, piece:]) for ref in coded]
+        encode(blocks, folded_max(jnp.abs(block)), [out.at[peer]], narrow)
+        pltpu.make_async_copy(out.at[peer], out_far.at[peer], left.at[peer]).start()
+        return none
+
+    lax.fori_loop(0, peers, send, 0)
+    for peer in range(peers):
+        pltpu.make_async_copy(out.at[peer], out_far.at[peer], left.at[peer]).wait()
+
+
+def sum_kernel(coded, out, *, width):
+    peers, piece = coded.shape[0], out.shape[1]
+    scales = [wide(decode_scale(coded[peer, :, piece:]), width) for peer in range(peers)]
 
     def step(c, none):
         at = cols(c, width)
         total = None
-        for ref, scale in zip(coded, scales):
-            term = ref[:, at].astype(jnp.int32).astype(f32) * wide(scale, width)
+        for peer in range(peers):
+            term = coded[peer, :, at].astype(jnp.int32).astype(f32) * scales[peer]
             total = term if total is None else total + term
         out[:, at] = total
         return none
@@ -257,21 +339,19 @@
         return jnp.maximum(largest, folded_max(jnp.abs(block)))
 
     largest = lax.fori_loop(0, piece // width, step, jnp.zeros((8, LANES), f32))
-    encode(blocks, largest, out, width)
-
-
-def decode_kernel(place, *refs, width):
-    coded, out, squares = refs[:-2], refs[-2], refs[-1]
-    peers = len(coded)
+    encode(blocks, largest, [out.at[peer] for peer in range(out.shape[0])], width)
+
+
+def decode_kernel(coded, out, squares, *, width):
+    peers = coded.shape[0]
     piece = out.shape[1] // peers
     total = jnp.zeros((8, LANES), f32)
-    for shift, ref in enumerate(coded):
-        start = lax.rem(place[0] + peers - shift, peers) * piece
-        scale = wide(decode_scale(ref[:, piece:]), width)
+    for peer in range(peers):
+        scale = wide(decode_scale(coded[peer, :, piece:]), width)
 
         def step(c, total):
-            block = ref[:, cols(c, width)].astype(jnp.int32).astype(f32) * scale
-            out[:, pl.ds(pl.multiple_of(start + c * width, width), width)] = block
+            block = coded[peer, :, cols(c, width)].astype(jnp.int32).astype(f32) * scale
+            out[:, cols(peer * (piece // width) + c, width)] = block
             square = block * block
             parts = [square[:, i : i + LANES] for i in range(0, width, LANES)]
             while len(parts) > 1:
@@ -310,18 +390,22 @@
     piece = width // peers
     up = [(i, i + 1) for i in range(rows - 1)]
     down = [(target, source) for source, target in up]
-    place = lax.axis_index("freq").astype(jnp.int32).reshape(1)
     smem = pl.BlockSpec(memory_space=pltpu.SMEM)
 
-    edge_width = 8192
-    field_block = pl.BlockSpec((2, 1, slab_rows, edge_width), lambda c: (0, 0, 0, c))
+    in_place = pl.BlockSpec(memory_space=pltpu.HBM)
+    stages = 4
+    field_scratch = [
+        pltpu.VMEM(state.shape, state.dtype),
+        pltpu.VMEM(adjoint.shape, adjoint.dtype),
+        pltpu.SemaphoreType.DMA((stages, 2)),
+    ]
     edge = pl.pallas_call(
-        functools.partial(edge_kernel, width=1024),
-        grid=(width // edge_width,),
+        functools.partial(edge_kernel, width=2048, stages=stages),
         out_shape=jax.ShapeDtypeStruct((4, width), jnp.bfloat16),
-        in_specs=[field_block, field_block],
-        out_specs=pl.BlockSpec((4, edge_width), lambda c: (0, c)),
-        compiler_params=params(8),
+        in_specs=[in_place, in_place],
+        out_specs=vmem(1)[0],
+        scratch_shapes=field_scratch,
+        compiler_params=params(63),
         cost_estimate=cost(8 * slab_rows * width, 4 * 1024 * 1024),
         name="edge",
     )(state, adjoint)
@@ -338,50 +422,56 @@
 
     slab = jax.ShapeDtypeStruct((slab_rows, width), f32)
     elastic, inertia = pl.pallas_call(
-        functools.partial(element_kernel, width=2048),
+        functools.partial(element_kernel, width=2048, stages=stages),
         out_shape=[slab, slab],
-        in_specs=[smem, smem] + vmem(3),
-        out_specs=vmem(2),
-        compiler_params=params(20),
+        in_specs=[smem, smem] + [in_place] * 3,
+        out_specs=[in_place, in_place],
+        scratch_shapes=field_scratch[:2]
+        + [pltpu.VMEM(edge.shape, edge.dtype)]
+        + [pltpu.VMEM((slab_rows, width), f32)] * 2
+        + [pltpu.SemaphoreType.DMA((stages, 3)), pltpu.SemaphoreType.DMA((stages, 2))],
+        compiler_params=params(63),
         cost_estimate=cost(80 * slab_rows * width, 8 * 1024 * 1024),
         name="element",
     )(omega_sq, assign, state, adjoint, edge_below)
 
-    coded_piece = jax.ShapeDtypeStruct((slab_rows, piece + LANES), i16)
+    coded = jax.ShapeDtypeStruct((peers, slab_rows, piece + LANES), i16)
+    operands = (design, code_above, code_below, passive, elastic, inertia, inverse)
     sent = pl.pallas_call(
-        partial_kernel,
-        out_shape=[coded_piece] * peers,
-        in_specs=[smem] + vmem(7),
-        out_specs=vmem(peers),
-        scratch_shapes=[
+        functools.partial(partial_kernel, stages=stages),
+        out_shape=coded,
+        in_specs=[in_place] * len(operands),
+        out_specs=in_place,
+        scratch_shapes=[pltpu.VMEM(operand.shape, operand.dtype) for operand in operands]
+        + [
             pltpu.VMEM((slab_rows, width + 2 * LANES), f32),
             pltpu.VMEM((slab_rows, width + 2 * LANES), f32),
             pltpu.VMEM((slab_rows, piece), f32),
+            pltpu.VMEM(coded.shape, coded.dtype),
+            pltpu.SemaphoreType.DMA((stages, len(operands))),
+            pltpu.SemaphoreType.DMA((peers,)),
         ],
-        compiler_params=params(32),
+        compiler_params=params(63),
         cost_estimate=cost(150 * slab_rows * width, 14 * 1024 * 1024),
         name="partial",
-    )(place, design, code_above, code_below, passive, elastic, inertia, inverse)
-
-    received = [sent[0]]
-    for shift in range(1, peers):
-        route = [(i, (i + shift) % peers) for i in range(peers)]
-        received.append(lax.ppermute(sent[shift], "freq", route))
+    )(*operands)
+
+    received = lax.all_to_all(sent, "freq", 0, 0, tiled=True)
 
     spread = pl.pallas_call(
         functools.partial(sum_kernel, width=1024),
         out_shape=jax.ShapeDtypeStruct((slab_rows, piece), f32),
-        in_specs=vmem(peers),
+        in_specs=vmem(1),
         out_specs=vmem(1)[0],
         compiler_params=params(8),
         name="total",
-    )(*received)
+    )(received)
     spread_below = lax.ppermute(spread, "rows", down)
     spread_above = lax.ppermute(spread, "rows", up)
 
     result = pl.pallas_call(
         functools.partial(back_kernel, width=1024),
-        out_shape=coded_piece,
+        out_shape=coded,
         in_specs=vmem(3),
         out_specs=vmem(1)[0],
         scratch_shapes=[pltpu.VMEM((slab_rows, piece), f32)],
@@ -389,26 +479,26 @@
         name="back",
     )(spread_above, spread, spread_below)
 
-    pieces = [result]
-    for shift in range(1, peers):
-        route = [(i, (i + shift) % peers) for i in range(peers)]
-        pieces.append(lax.ppermute(result, "freq", route))
+    pieces = lax.all_to_all(result, "freq", 0, 0, tiled=True)
 
     back, squares = pl.pallas_call(
         functools.partial(decode_kernel, width=1024),
         out_shape=[slab, jax.ShapeDtypeStruct((rows, 8, LANES), f32)],
-        in_specs=[smem] + vmem(peers),
+        in_specs=vmem(1),
         out_specs=vmem(2),
         compiler_params=params(16),
         name="decode",
-    )(place, *pieces)
+    )(pieces)
     squares = lax.all_to_all(squares, "rows", 0, 0, tiled=True)
 
+    out_width = 16384
+    out_block = pl.BlockSpec((slab_rows, out_width), lambda c: (0, c))
     return pl.pallas_call(
-        functools.partial(scale_kernel, width=1024, elements=float(whole_rows * width)),
+        functools.partial(scale_kernel, width=2048, elements=float(whole_rows * width)),
+        grid=(width // out_width,),
         out_shape=slab,
-        in_specs=vmem(2),
-        out_specs=vmem(1)[0],
+        in_specs=[out_block, pl.BlockSpec((rows, 8, LANES), lambda c: (0, 0, 0))],
+        out_specs=out_block,
         compiler_params=params(16),
         name="scale",
     )(back, squares)

time: 135 us -> 134 us (level)
  blocking collectives: 23.1 us -> 58.9 us
  starting transfers between devices: 41.9 us -> 20.4 us
  waiting for transfers between devices: 25 us -> 10.4 us
  local copies, waits for them, and re-layouts: 4.79 us -> 0.78 us
  Pallas kernels: 35.3 us -> 37.3 us
    all_to_all x0 -> x2, blocking collectives: none -> 34.6 us  [the longest x1 18.8 us: layer(): received = lax.all_to_all(sent, 'freq', 0, 0, tiled=True)]
    ppermute x14 -> x0, starting transfers between devices: 23.3 us -> none  [the longest x7 13.2 us: layer(): received.append(lax.ppermute(sent[shift], 'freq', route))]
    ppermute x14 -> x0, waiting for transfers between devices: 15.2 us -> none  [the longest x7 9.85 us: layer(): pieces.append(lax.ppermute(result, 'freq', route))]
    unnamed x14 -> x2, local copies, waits for them, and re-layouts: 4.79 us -> 0.78 us
    ppermute x1, starting transfers between devices: 6.09 us -> 8.1 us  [layer(): spread_above = lax.ppermute(spread, 'rows', up)]
    pallas_call x4, Pallas kernels: 33.5 us -> 35.5 us  [the longest x1 18 us: layer(): pl.pallas_call(functools.partial(partial_kernel, stages=stages), out_shap...]
  transfers between devices with their start and end apart: 19 -> 5, of which waited for: 11 -> 3; matrix products, arithmetic and copies ran while one was open for 0% -> 1% of each run, Pallas kernels for 11% -> 11%
where the time goes in v3:
time: 134 us; the launch traced here: 133 us
  blocking collectives  58.9 us (44%)
  Pallas kernels  37.3 us (28%)
  starting transfers between devices  20.4 us (15%)
  waiting for transfers between devices  10.4 us (8%)
  other arithmetic  4.62 us (3%)
    all_to_all x1, blocking collectives, layer(): squares = lax.all_to_all(squares, 'rows', 0, 0, tiled=True)  24.3 us
    all_to_all x1, blocking collectives, layer(): received = lax.all_to_all(sent, 'freq', 0, 0, tiled=True)  18.8 us
    pallas_call x1, Pallas kernels, layer(): pl.pallas_call(functools.partial(partial_kernel, stages=stages), out_shap...  18 us
    all_to_all x1, blocking collectives, layer(): pieces = lax.all_to_all(result, 'freq', 0, 0, tiled=True)  15.7 us
    pallas_call x1, Pallas kernels, layer(): pl.pallas_call(functools.partial(element_kernel, width=2048, stages=stage...  11.9 us
    ppermute x1, starting transfers between devices, layer(): spread_above = lax.ppermute(spread, 'rows', up)  8.1 us
    ppermute x1, waiting for transfers between devices, layer(): edge_below = lax.ppermute(edge, 'rows', down)  7.13 us
    ppermute x1, starting transfers between devices, layer(): code_below = lax.ppermute(code, 'rows', down)  5.1 us
  transfers between devices with their start and end apart: 5, of which 3 were waited for; matrix products, arithmetic and copies ran while one was open for 1% of the time, Pallas kernels for 11%

profile of v3, /device:TPU:1, one launch (start us, length us, event | category | flops | bytes accessed | tf_op | source)
XLA Modules:
  0.0 133.3 jit_solution(869966849429809416)
XLA Ops:
  0.0 2.9 %round-nearest-even_convert_fusion = s16[8,65536]{1,0:T(8,128)(2,1)} fusion(f32[8,65536]{1,0:T(8,128)} %refs_0_.1), kind=kLoop, calls=%fused_computation.1 | loop fusion | flops 1572864 | bytes 3145728 | tf_op jit(solution)/shard_map/convert_element_type | solution.py:413
  2.9 5.1 %collective-permute-start.1 = (s16[8,65536]{1,0:T(8,128)(2,1)}, s16[8,65536]{1,0:T(8,128)(2,1)}, u32[]{:S(2)}, u32[]{:S(2)}) collective-permute-start(s16[8,65536]{1,0:T(8,128)(2,1)} %round-nearest-even_convert_fusion), channel_id=1, source_target_pairs={{8,0},{16,8},{24,16},{32,24},{40,32},{48,40},{56,48},{64,56},{72,6... | collective-permute-start | bytes 3145736 | tf_op jit(solution)/shard_map/ppermute | solution.py:414
  8.0 1.9 %collective-permute-start = (s16[8,65536]{1,0:T(8,128)(2,1)}, s16[8,65536]{1,0:T(8,128)(2,1)}, u32[]{:S(2)}, u32[]{:S(2)}) collective-permute-start(s16[8,65536]{1,0:T(8,128)(2,1)} %round-nearest-even_convert_fusion), channel_id=1, source_target_pairs={{0,8},{8,16},{16,24},{24,32},{32,40},{40,48},{48,56},{56,64},{64,7... | collective-permute-start | bytes 3145736 | tf_op jit(solution)/shard_map/ppermute | solution.py:415
  9.9 3.3 %edge.1 = bf16[4,65536]{1,0:T(4,128)(2,1)} custom-call(bf16[2,1,8,65536]{3,2,1,0:T(8,128)(2,1)} %state_far.3, bf16[2,1,8,65536]{3,2,1,0:T(8,128)(2,1)} %adjoint_far.3), custom_call_target="tpu_custom_call" | custom-call | flops 4194304 | bytes 4194304 | tf_op jit(solution)/shard_map/edge/pallas_call | solution.py:402
  13.2 3.4 %collective-permute-start.2 = (bf16[4,65536]{1,0:T(4,128)(2,1)}, bf16[4,65536]{1,0:T(4,128)(2,1)S(1)}, u32[]{:S(2)}, u32[]{:S(2)}) collective-permute-start(bf16[4,65536]{1,0:T(4,128)(2,1)} %edge.1), channel_id=1, source_target_pairs={{8,0},{16,8},{24,16},{32,24},{40,32},{48,40},{56,48},{64,56},{72,6... | collective-permute-start | bytes 1572872 | tf_op jit(solution)/shard_map/ppermute | solution.py:412
  16.6 1.7 %multiply_divide_fusion.refs_6_ = f32[8,65536]{1,0:T(8,128)} fusion(f32[65536]{0:T(1024)S(1)} %fusion.14, f32[8]{0:T(128)S(1)} %subtract_convert_fusion), kind=kLoop, calls=%fused_computation | loop fusion | flops 1048576 | bytes 2359328 | tf_op jit(solution)/shard_map/div | solution.py:418
  19.0 7.1 %collective-permute-done.2.edge_far = bf16[4,65536]{1,0:T(4,128)(2,1)S(1)} collective-permute-done((bf16[4,65536]{1,0:T(4,128)(2,1)}, bf16[4,65536]{1,0:T(4,128)(2,1)S(1)}, u32[]{:S(2)}, u32[]{:S(2)}) %collective-permute-start.2) | collective-permute-done | bytes 524320 | tf_op jit(solution)/shard_map/ppermute | solution.py:412
  26.1 0.0 copy-start
  26.1 0.8 copy-done
  26.9 11.9 %element.1 = (f32[8,65536]{1,0:T(8,128)}, f32[8,65536]{1,0:T(8,128)}) custom-call(f32[8]{0:T(128)} %omega_sq.1, s32[1]{0:T(128)S(6)} %copy.7.assign, bf16[2,1,8,65536]{3,2,1,0:T(8,128)(2,1)} %state_far.3, bf16[2,1,8,65536]{3,2,1,0:T(8,128)(2,1)} %adjoint_far.3, bf16[4,65536]{1,0:T(4,128)(2,1)} %copy-done), custom_call_target="tpu_custom_call" | custom-call | flops 41943040 | bytes 8388608 | tf_op jit(solution)/shard_map/element/pallas_call | solution.py:424
  38.8 0.0 collective-permute-done.1.refs_2_
  38.8 0.0 collective-permute-done.refs_1_
  38.9 18.0 %partial.1 = s16[8,8,8320]{2,1,0:T(8,128)(2,1)} custom-call(f32[8,65536]{1,0:T(8,128)} %refs_0_.1, s16[8,65536]{1,0:T(8,128)(2,1)} %collective-permute-done.refs_1_, s16[8,65536]{1,0:T(8,128)(2,1)} %collective-permute-done.1.refs_2_, s32[8,65536]{1,0:T(8,128)} %refs_3_.1, f32[8,65536]{1,0:T(8,128)} %get-tuple-element.9.refs_4_, ...), custom_call_target="tpu_custom_call" | custom-call | flops 78643200 | bytes 14680064 | tf_op jit(solution)/shard_map/partial/pallas_call | solution.py:440
  56.9 18.8 %all_to_all.15.coded = s16[8,8,8320]{2,1,0:T(8,128)(2,1)S(1)} all-to-all(s16[8,8,8320]{2,1,0:T(8,128)(2,1)} %partial.1), channel_id=1, replica_groups=mesh['rows'=32,'freq'=8] {'freq'}, dimensions={0} | all-to-all | bytes 2129920 | tf_op jit(solution)/shard_map/all_to_all | solution.py:459
  75.8 0.3 total.1.here
  76.1 1.9 %collective-permute-start.4 = (f32[8,8192]{1,0:T(8,128)S(1)}, f32[8,8192]{1,0:T(8,128)S(1)}, u32[]{:S(2)}, u32[]{:S(2)}) collective-permute-start(f32[8,8192]{1,0:T(8,128)S(1)} %total.1.here), channel_id=1, source_target_pairs={{8,0},{16,8},{24,16},{32,24},{40,32},{48,40},{56,48},{64,56},{72,6... | collective-permute-start | bytes 786440 | tf_op jit(solution)/shard_map/ppermute | solution.py:469
  78.0 8.1 %collective-permute-start.3 = (f32[8,8192]{1,0:T(8,128)S(1)}, f32[8,8192]{1,0:T(8,128)S(1)}, u32[]{:S(2)}, u32[]{:S(2)}) collective-permute-start(f32[8,8192]{1,0:T(8,128)S(1)} %total.1.here), channel_id=1, source_target_pairs={{0,8},{8,16},{16,24},{24,32},{32,40},{40,48},{48,56},{56,64},{64,7... | collective-permute-start | bytes 786440 | tf_op jit(solution)/shard_map/ppermute | solution.py:470
  86.1 2.2 %collective-permute-done.4.below = f32[8,8192]{1,0:T(8,128)S(1)} collective-permute-done((f32[8,8192]{1,0:T(8,128)S(1)}, f32[8,8192]{1,0:T(8,128)S(1)}, u32[]{:S(2)}, u32[]{:S(2)}) %collective-permute-start.4) | collective-permute-done | bytes 262176 | tf_op jit(solution)/shard_map/ppermute | solution.py:469
  88.3 1.1 collective-permute-done.3.above
  89.4 0.6 back.1
  90.1 15.7 %all_to_all.16.coded = s16[8,8,8320]{2,1,0:T(8,128)(2,1)S(1)} all-to-all(s16[8,8,8320]{2,1,0:T(8,128)(2,1)S(1)} %back.1), channel_id=1, replica_groups=mesh['rows'=32,'freq'=8] {'freq'}, dimensions={0} | all-to-all | bytes 2129920 | tf_op jit(solution)/shard_map/all_to_all | solution.py:482
  105.8 0.9 decode.1
  106.7 24.3 %all_to_all.17.squares = f32[32,8,128]{2,1,0:T(8,128)S(1)} all-to-all(f32[32,8,128]{2,1,0:T(8,128)S(1)} %get-tuple-element.12), channel_id=1, replica_groups=mesh['rows'=32,'freq'=8] {'rows'}, dimensions={0} | all-to-all | bytes 262144 | tf_op jit(solution)/shard_map/all_to_all | solution.py:492
  131.0 2.3 %scale.1 = f32[8,65536]{1,0:T(8,128)} custom-call(f32[8,65536]{1,0:T(8,128)S(1)} %get-tuple-element.11.back, f32[32,8,128]{2,1,0:T(8,128)S(1)} %all_to_all.17.squares), custom_call_target="tpu_custom_call" | custom-call | tf_op jit(solution)/shard_map/scale/pallas_call | solution.py:496
  (2 shorter events, 0.0 us)
Async XLA Ops:
  2.9 35.9 %collective-permute-start.1 = (s16[8,65536]{1,0:T(8,128)(2,1)}, s16[8,65536]{1,0:T(8,128)(2,1)}, u32[]{:S(2)}, u32[]{:S(2)}) collective-permute-start(s16[8,65536]{1,0:T(8,128)(2,1)} %round-nearest-even_convert_fusion), channel_id=1, source_target_pairs={{8,0},{16,8},{24,16},{32,24},{40,32},{48,40},{56,48},{64,56},{72,6... | collective-permute-start | bytes 3145736 | tf_op jit(solution)/shard_map/ppermute | solution.py:414
  8.0 30.8 %collective-permute-start = (s16[8,65536]{1,0:T(8,128)(2,1)}, s16[8,65536]{1,0:T(8,128)(2,1)}, u32[]{:S(2)}, u32[]{:S(2)}) collective-permute-start(s16[8,65536]{1,0:T(8,128)(2,1)} %round-nearest-even_convert_fusion), channel_id=1, source_target_pairs={{0,8},{8,16},{16,24},{24,32},{32,40},{40,48},{48,56},{56,64},{64,7... | collective-permute-start | bytes 3145736 | tf_op jit(solution)/shard_map/ppermute | solution.py:415
  13.2 12.9 %collective-permute-start.2 = (bf16[4,65536]{1,0:T(4,128)(2,1)}, bf16[4,65536]{1,0:T(4,128)(2,1)S(1)}, u32[]{:S(2)}, u32[]{:S(2)}) collective-permute-start(bf16[4,65536]{1,0:T(4,128)(2,1)} %edge.1), channel_id=1, source_target_pairs={{8,0},{16,8},{24,16},{32,24},{40,32},{48,40},{56,48},{64,56},{72,6... | collective-permute-start | bytes 1572872 | tf_op jit(solution)/shard_map/ppermute | solution.py:412
  26.1 0.8 copy-start
  76.1 12.2 %collective-permute-start.4 = (f32[8,8192]{1,0:T(8,128)S(1)}, f32[8,8192]{1,0:T(8,128)S(1)}, u32[]{:S(2)}, u32[]{:S(2)}) collective-permute-start(f32[8,8192]{1,0:T(8,128)S(1)} %total.1.here), channel_id=1, source_target_pairs={{8,0},{16,8},{24,16},{32,24},{40,32},{48,40},{56,48},{64,56},{72,6... | collective-permute-start | bytes 786440 | tf_op jit(solution)/shard_map/ppermute | solution.py:469
  78.0 11.4 %collective-permute-start.3 = (f32[8,8192]{1,0:T(8,128)S(1)}, f32[8,8192]{1,0:T(8,128)S(1)}, u32[]{:S(2)}, u32[]{:S(2)}) collective-permute-start(f32[8,8192]{1,0:T(8,128)S(1)} %total.1.here), channel_id=1, source_target_pairs={{0,8},{8,16},{16,24},{24,32},{32,40},{40,48},{48,56},{56,64},{64,7... | collective-permute-start | bytes 786440 | tf_op jit(solution)/shard_map/ppermute | solution.py:470

commit v4 on v3

--- a/solution.py
+++ b/solution.py
@@ -110,11 +110,15 @@
     return jnp.concatenate([tile] * (width // LANES), axis=1)
 
 
-def folded_max(block):
+def folded(block, join):
     parts = [block[:, i : i + LANES] for i in range(0, block.shape[1], LANES)]
     while len(parts) > 1:
-        parts = [jnp.maximum(a, b) for a, b in zip(parts[::2], parts[1::2])]
+        parts = [join(a, b) for a, b in zip(parts[::2], parts[1::2])]
     return parts[0]
+
+
+def folded_max(block):
+    return folded(jnp.abs(block), jnp.maximum)
 
 
 def encode(source, largest, targets, width):
@@ -166,6 +170,33 @@
             return none
 
         lax.fori_loop(0, span // width, step, 0)
+
+
+def code_kernel(design_far, code_far, design, code, arrived, left, *, width, stages):
+    span = design.shape[1] // stages
+
+    def load(stage):
+        at = pl.ds(stage * span, span)
+        return pltpu.make_async_copy(design_far.at[:, at], design.at[:, at], arrived.at[stage])
+
+    def save(stage):
+        at = pl.ds(stage * span, span)
+        return pltpu.make_async_copy(code.at[:, at], code_far.at[:, at], left.at[stage])
+
+    for stage in range(stages):
+        load(stage).start()
+    for stage in range(stages):
+        load(stage).wait()
+
+        def step(c, none):
+            at = cols(stage * (span // width) + c, width)
+            code[:, at] = to_i16(design[:, at] * DESIGN_STEPS)
+            return none
+
+        lax.fori_loop(0, span // width, step, 0)
+        save(stage).start()
+    for stage in range(stages):
+        save(stage).wait()
 
 
 def element_kernel(
@@ -239,7 +270,7 @@
     for stage in reversed(range(stages)):
         for copy in copies(stage):
             copy.wait()
-        carries = lax.fori_loop(0, count, functools.partial(step, stage), carries)
+        carries = lax.fori_loop(0, count, functools.partial(step, stage), carries, unroll=2)
         for copy in results(stage):
             copy.start()
     for stage in reversed(range(stages)):
@@ -247,10 +278,17 @@
             copy.wait()
 
 
-def partial_kernel(*refs, stages):
-    sources, out_far, kept = refs[:7], refs[7], refs[8:15]
-    rowed, spread, blocks, out, arrived, left = refs[15:]
-    design, above, below, passive, elastic, inertia, inverse = kept
+def tap_sums(before, after):
+    near = jnp.maximum(RADIUS - before, 0)
+    far = jnp.maximum(RADIUS - after, 0)
+    missing = near * (near + 1) + far * (far + 1)
+    return float((RADIUS + 1) ** 2) - 0.5 * missing.astype(f32)
+
+
+def partial_kernel(top, *refs, stages, whole_rows):
+    sources, out_far, kept = refs[:6], refs[6], refs[7:13]
+    rowed, spread, blocks, out, arrived, left = refs[13:]
+    design, above, below, passive, elastic, inertia = kept
     peers = out.shape[0]
     piece = design.shape[1] // peers
     narrow = 2048
@@ -263,7 +301,7 @@
             for k in range(3)
         ]
 
-    late = [pltpu.make_async_copy(sources[k], kept[k], arrived.at[0, k]) for k in range(3, 7)]
+    late = [pltpu.make_async_copy(sources[k], kept[k], arrived.at[0, k]) for k in range(3, 6)]
     for stage in range(stages):
         for copy in early(stage):
             copy.start()
@@ -287,9 +325,18 @@
     for copy in late:
         copy.wait()
 
+    row = top[0] + row_ids(LANES)
+    lane = lax.broadcasted_iota(jnp.int32, (8, LANES), 1)
+    full = float((RADIUS + 1) ** 2)
+    inside = 1.0 / (full * tap_sums(row, whole_rows - 1 - row))
+    left_end = full / tap_sums(lane, RADIUS)
+    right_end = full / tap_sums(RADIUS, LANES - 1 - lane)
+
     def scale(c, none):
         at = cols(c, piece)
-        weights = inverse[:, at]
+        first = inside * jnp.where(c == 0, left_end, 1.0)
+        last = inside * jnp.where(c == peers - 1, right_end, 1.0)
+        weights = jnp.concatenate([first] + [inside] * (piece // LANES - 2) + [last], axis=1)
         tilde = col_filter(rowed[:, padded_cols(c, piece)])[:, LANES : LANES + piece] * weights
         steep = jnp.tanh(SHARPNESS * (tilde - THRESHOLD))
         solid = passive[:, at] > 0
@@ -304,7 +351,7 @@
     def send(peer, none):
         block = col_filter(spread[:, padded_cols(peer, piece)])[:, LANES : LANES + piece]
         blocks[...] = block
-        encode(blocks, folded_max(jnp.abs(block)), [out.at[peer]], narrow)
+        encode(blocks, folded_max(block), [out.at[peer]], narrow)
         pltpu.make_async_copy(out.at[peer], out_far.at[peer], left.at[peer]).start()
         return none
 
@@ -331,55 +378,56 @@
 
 def back_kernel(above, here, below, out, blocks, *, width):
     piece = here.shape[1]
-
-    def step(c, largest):
+    zeros = jnp.zeros((8, LANES), f32)
+
+    def step(c, carry):
+        largest, squares = carry
         at = cols(c, width)
         block = row_filter(above[:, at], here[:, at], below[:, at])
         blocks[:, at] = block
-        return jnp.maximum(largest, folded_max(jnp.abs(block)))
-
-    largest = lax.fori_loop(0, piece // width, step, jnp.zeros((8, LANES), f32))
+        return jnp.maximum(largest, folded_max(block)), squares + folded(block * block, jnp.add)
+
+    largest, squares = lax.fori_loop(0, piece // width, step, (zeros, zeros))
     encode(blocks, largest, [out.at[peer] for peer in range(out.shape[0])], width)
-
-
-def decode_kernel(coded, out, squares, *, width):
+    code = scale_code(squares).astype(jnp.int32).astype(i16)
+    values = to_i16(squares / decode_scale(code))
+    for peer in range(out.shape[0]):
+        out[peer, :, piece + LANES : piece + 2 * LANES] = code
+        out[peer, :, piece + 2 * LANES :] = values
+
+
+def squares_kernel(coded, squares):
+    piece = coded.shape[2] - 3 * LANES
+    total = jnp.zeros((8, LANES), f32)
+    for peer in range(coded.shape[0]):
+        values = coded[peer, :, piece + 2 * LANES :].astype(jnp.int32).astype(f32)
+        total = total + values * decode_scale(coded[peer, :, piece + LANES : piece + 2 * LANES])
+    squares[...] = jnp.broadcast_to(total[None], squares.shape)
+
+
+def result_kernel(coded, squares, out_far, out, left, *, width, elements):
     peers = coded.shape[0]
     piece = out.shape[1] // peers
-    total = jnp.zeros((8, LANES), f32)
-    for peer in range(peers):
-        scale = wide(decode_scale(coded[peer, :, piece:]), width)
-
-        def step(c, total):
-            block = coded[peer, :, cols(c, width)].astype(jnp.int32).astype(f32) * scale
-            out[:, cols(peer * (piece // width) + c, width)] = block
-            square = block * block
-            parts = [square[:, i : i + LANES] for i in range(0, width, LANES)]
-            while len(parts) > 1:
-                parts = [a + b for a, b in zip(parts[::2], parts[1::2])]
-            return total + parts[0]
-
-        total = lax.fori_loop(0, piece // width, step, total)
-    squares[...] = jnp.broadcast_to(total[None], squares.shape)
-
-
-def scale_kernel(back, squares, out, *, width, elements):
     mean = jnp.sum(jnp.sum(squares[...], axis=0), keepdims=True) * (1.0 / elements) + EPSILON
     root = lax.rsqrt(mean)
     root = root * (1.5 - 0.5 * mean * root * root)
 
-    def step(c, none):
-        at = cols(c, width)
-        out[:, at] = back[:, at] * root
-        return none
-
-    lax.fori_loop(0, out.shape[1] // width, step, 0)
-
-
-def edge_weights(positions, whole):
-    near = jnp.maximum(RADIUS - positions, 0)
-    far = jnp.maximum(RADIUS - (whole - 1 - positions), 0)
-    missing = near * (near + 1) // 2 + far * (far + 1) // 2
-    return ((RADIUS + 1) ** 2 - missing).astype(f32)
+    def finished(peer):
+        at = pl.ds(peer * piece, piece)
+        return pltpu.make_async_copy(out.at[:, at], out_far.at[:, at], left.at[peer])
+
+    for peer in range(peers):
+        scale = wide(decode_scale(coded[peer, :, piece : piece + LANES]) * root, width)
+
+        def step(c, none):
+            block = coded[peer, :, cols(c, width)].astype(jnp.int32).astype(f32) * scale
+            out[:, cols(peer * (piece // width) + c, width)] = block
+            return none
+
+        lax.fori_loop(0, piece // width, step, 0)
+        finished(peer).start()
+    for peer in range(peers):
+        finished(peer).wait()
 
 
 def layer(design, passive, state, adjoint, omega_sq, assign):
@@ -410,15 +458,24 @@
         name="edge",
     )(state, adjoint)
     edge_below = lax.ppermute(edge, "rows", down)
-    code = jnp.round(design * DESIGN_STEPS).astype(i16)
+    code = pl.pallas_call(
+        functools.partial(code_kernel, width=2048, stages=stages),
+        out_shape=jax.ShapeDtypeStruct((slab_rows, width), i16),
+        in_specs=[in_place],
+        out_specs=in_place,
+        scratch_shapes=[
+            pltpu.VMEM((slab_rows, width), f32),
+            pltpu.VMEM((slab_rows, width), i16),
+            pltpu.SemaphoreType.DMA((stages,)),
+            pltpu.SemaphoreType.DMA((stages,)),
+        ],
+        compiler_params=params(63),
+        name="code",
+    )(design)
     code_below = lax.ppermute(code, "rows", down)
     code_above = lax.ppermute(code, "rows", up)
 
-    top = lax.axis_index("rows") * slab_rows
-    inverse = 1.0 / (
-        edge_weights(top + jnp.arange(slab_rows, dtype=jnp.int32), whole_rows)[:, None]
-        * edge_weights(jnp.arange(width, dtype=jnp.int32), width)[None, :]
-    )
+    top = (lax.axis_index("rows") * slab_rows).astype(jnp.int32).reshape(1)
 
     slab = jax.ShapeDtypeStruct((slab_rows, width), f32)
     elastic, inertia = pl.pallas_call(
@@ -436,11 +493,11 @@
     )(omega_sq, assign, state, adjoint, edge_below)
 
     coded = jax.ShapeDtypeStruct((peers, slab_rows, piece + LANES), i16)
-    operands = (design, code_above, code_below, passive, elastic, inertia, inverse)
+    operands = (design, code_above, code_below, passive, elastic, inertia)
     sent = pl.pallas_call(
-        functools.partial(partial_kernel, stages=stages),
+        functools.partial(partial_kernel, stages=stages, whole_rows=whole_rows),
         out_shape=coded,
-        in_specs=[in_place] * len(operands),
+        in_specs=[smem] + [in_place] * len(operands),
         out_specs=in_place,
         scratch_shapes=[pltpu.VMEM(operand.shape, operand.dtype) for operand in operands]
         + [
@@ -454,7 +511,7 @@
         compiler_params=params(63),
         cost_estimate=cost(150 * slab_rows * width, 14 * 1024 * 1024),
         name="partial",
-    )(*operands)
+    )(top, *operands)
 
     received = lax.all_to_all(sent, "freq", 0, 0, tiled=True)
 
@@ -469,9 +526,10 @@
     spread_below = lax.ppermute(spread, "rows", down)
     spread_above = lax.ppermute(spread, "rows", up)
 
+    wide_coded = jax.ShapeDtypeStruct((peers, slab_rows, piece + 3 * LANES), i16)
     result = pl.pallas_call(
         functools.partial(back_kernel, width=1024),
-        out_shape=coded,
+        out_shape=wide_coded,
         in_specs=vmem(3),
         out_specs=vmem(1)[0],
         scratch_shapes=[pltpu.VMEM((slab_rows, piece), f32)],
@@ -481,27 +539,25 @@
 
     pieces = lax.all_to_all(result, "freq", 0, 0, tiled=True)
 
-    back, squares = pl.pallas_call(
-        functools.partial(decode_kernel, width=1024),
-        out_shape=[slab, jax.ShapeDtypeStruct((rows, 8, LANES), f32)],
+    squares = pl.pallas_call(
+        squares_kernel,
+        out_shape=jax.ShapeDtypeStruct((rows, 8, LANES), f32),
         in_specs=vmem(1),
-        out_specs=vmem(2),
-        compiler_params=params(16),
-        name="decode",
+        out_specs=vmem(1)[0],
+        compiler_params=params(8),
+        name="squares",
     )(pieces)
     squares = lax.all_to_all(squares, "rows", 0, 0, tiled=True)
 
-    out_width = 16384
-    out_block = pl.BlockSpec((slab_rows, out_width), lambda c: (0, c))
     return pl.pallas_call(
-        functools.partial(scale_kernel, width=2048, elements=float(whole_rows * width)),
-        grid=(width // out_width,),
+        functools.partial(result_kernel, width=2048, elements=float(whole_rows * width)),
         out_shape=slab,
-        in_specs=[out_block, pl.BlockSpec((rows, 8, LANES), lambda c: (0, 0, 0))],
-        out_specs=out_block,
+        in_specs=vmem(2),
+        out_specs=in_place,
+        scratch_shapes=[pltpu.VMEM((slab_rows, width), f32), pltpu.SemaphoreType.DMA((peers,))],
         compiler_params=params(16),
-        name="scale",
-    )(back, squares)
+        name="result",
+    )(pieces, squares)
 
 
 def solution(mesh):

time: 134 us -> 131 us (0.978)
  other arithmetic: 4.62 us -> 0 us
  waiting for transfers between devices: 10.4 us -> 12.2 us
    convert_element_type x3 -> x0, other arithmetic: 2.93 us -> none  [the longest x1 2.89 us: layer(): code = jnp.round(design * DESIGN_STEPS).astype(i16)]
    ppermute x1, waiting for transfers between devices: 7.13 us -> 8.89 us  [layer(): edge_below = lax.ppermute(edge, 'rows', down)]
    div x1 -> x0, other arithmetic: 1.69 us -> none  [layer(): 1.0 / (edge_weights(top + jnp.arange(slab_rows, dtype=jnp.int32), whole_r...]
    pallas_call x4 -> x5, Pallas kernels: 21.8 us -> 22.7 us  [the longest x1 18.1 us: layer(): pl.pallas_call(functools.partial(partial_kernel, stages=stages, whole_row...]
  transfers between devices with their start and end apart: 5 -> 5, of which waited for: 3 -> 3; matrix products, arithmetic and copies ran while one was open for 1% -> 0% of each run, Pallas kernels for 11% -> 11%
where the time goes in v4:
time: 131 us; the launch traced here: 130 us
  blocking collectives  59.2 us (45%)
  Pallas kernels  37 us (28%)
  starting transfers between devices  20.4 us (16%)
  waiting for transfers between devices  12.2 us (9%)
    all_to_all x1, blocking collectives, layer(): squares = lax.all_to_all(squares, 'rows', 0, 0, tiled=True)  24.3 us
    all_to_all x1, blocking collectives, layer(): received = lax.all_to_all(sent, 'freq', 0, 0, tiled=True)  18.8 us
    pallas_call x1, Pallas kernels, layer(): pl.pallas_call(functools.partial(partial_kernel, stages=stages, whole_row...  18.1 us
    all_to_all x1, blocking collectives, layer(): pieces = lax.all_to_all(result, 'freq', 0, 0, tiled=True)  16 us
    pallas_call x1, Pallas kernels, layer(): pl.pallas_call(functools.partial(element_kernel, width=2048, stages=stage...  10.8 us
    ppermute x1, waiting for transfers between devices, layer(): edge_below = lax.ppermute(edge, 'rows', down)  8.89 us
    ppermute x1, starting transfers between devices, layer(): spread_above = lax.ppermute(spread, 'rows', up)  8.1 us
    ppermute x1, starting transfers between devices, layer(): code_below = lax.ppermute(code, 'rows', down)  5.11 us
  transfers between devices with their start and end apart: 5, of which 3 were waited for; matrix products, arithmetic and copies ran while one was open for 0% of the time, Pallas kernels for 11%

profile of v4, /device:TPU:1, one launch (start us, length us, event | category | flops | bytes accessed | tf_op | source)
XLA Modules:
  0.0 130.4 jit_solution(14054362112324495970)
XLA Ops:
  0.0 2.4 %code.1 = s16[8,65536]{1,0:T(8,128)(2,1)} custom-call(f32[8,65536]{1,0:T(8,128)} %refs_0_.1), custom_call_target="tpu_custom_call" | custom-call | tf_op jit(solution)/shard_map/code/pallas_call | solution.py:461
  2.4 5.1 %collective-permute-start.1 = (s16[8,65536]{1,0:T(8,128)(2,1)}, s16[8,65536]{1,0:T(8,128)(2,1)}, u32[]{:S(2)}, u32[]{:S(2)}) collective-permute-start(s16[8,65536]{1,0:T(8,128)(2,1)} %code.1), channel_id=1, source_target_pairs={{8,0},{16,8},{24,16},{32,24},{40,32},{48,40},{56,48},{64,56},{72,6... | collective-permute-start | bytes 3145736 | tf_op jit(solution)/shard_map/ppermute | solution.py:475
  7.5 1.9 %collective-permute-start = (s16[8,65536]{1,0:T(8,128)(2,1)}, s16[8,65536]{1,0:T(8,128)(2,1)}, u32[]{:S(2)}, u32[]{:S(2)}) collective-permute-start(s16[8,65536]{1,0:T(8,128)(2,1)} %code.1), channel_id=1, source_target_pairs={{0,8},{8,16},{16,24},{24,32},{32,40},{40,48},{48,56},{56,64},{64,7... | collective-permute-start | bytes 3145736 | tf_op jit(solution)/shard_map/ppermute | solution.py:476
  9.4 3.3 %edge.1 = bf16[4,65536]{1,0:T(4,128)(2,1)} custom-call(bf16[2,1,8,65536]{3,2,1,0:T(8,128)(2,1)} %state_far.3, bf16[2,1,8,65536]{3,2,1,0:T(8,128)(2,1)} %adjoint_far.3), custom_call_target="tpu_custom_call" | custom-call | flops 4194304 | bytes 4194304 | tf_op jit(solution)/shard_map/edge/pallas_call | solution.py:450
  12.7 3.4 %collective-permute-start.2 = (bf16[4,65536]{1,0:T(4,128)(2,1)}, bf16[4,65536]{1,0:T(4,128)(2,1)S(1)}, u32[]{:S(2)}, u32[]{:S(2)}) collective-permute-start(bf16[4,65536]{1,0:T(4,128)(2,1)} %edge.1), channel_id=1, source_target_pairs={{8,0},{16,8},{24,16},{32,24},{40,32},{48,40},{56,48},{64,56},{72,6... | collective-permute-start | bytes 1572872 | tf_op jit(solution)/shard_map/ppermute | solution.py:460
  16.7 8.9 %collective-permute-done.2.edge_far = bf16[4,65536]{1,0:T(4,128)(2,1)S(1)} collective-permute-done((bf16[4,65536]{1,0:T(4,128)(2,1)}, bf16[4,65536]{1,0:T(4,128)(2,1)S(1)}, u32[]{:S(2)}, u32[]{:S(2)}) %collective-permute-start.2) | collective-permute-done | bytes 524320 | tf_op jit(solution)/shard_map/ppermute | solution.py:460
  25.6 0.0 copy-start
  25.6 0.8 copy-done
  26.4 10.8 %element.1 = (f32[8,65536]{1,0:T(8,128)}, f32[8,65536]{1,0:T(8,128)}) custom-call(f32[8]{0:T(128)} %omega_sq.1, s32[1]{0:T(128)S(6)} %copy.7.assign, bf16[2,1,8,65536]{3,2,1,0:T(8,128)(2,1)} %state_far.3, bf16[2,1,8,65536]{3,2,1,0:T(8,128)(2,1)} %adjoint_far.3, bf16[4,65536]{1,0:T(4,128)(2,1)} %copy-done), custom_call_target="tpu_custom_call" | custom-call | flops 41943040 | bytes 8388608 | tf_op jit(solution)/shard_map/element/pallas_call | solution.py:481
  37.2 0.0 collective-permute-done.1.refs_2_
  37.2 0.0 collective-permute-done.refs_1_
  37.2 18.1 %partial.1 = s16[8,8,8320]{2,1,0:T(8,128)(2,1)} custom-call(s32[1]{0:T(128)} %bitcast.top, f32[8,65536]{1,0:T(8,128)} %refs_0_.1, s16[8,65536]{1,0:T(8,128)(2,1)} %collective-permute-done.refs_1_, s16[8,65536]{1,0:T(8,128)(2,1)} %collective-permute-done.1.refs_2_, s32[8,65536]{1,0:T(8,128)} %refs_3_.1, f32[8,65536]{1,0:T(8,128)} %get-tuple-element.7.refs_4_, ...), custom_call_target="tpu_custom_call" | custom-call | flops 78643200 | bytes 14680064 | tf_op jit(solution)/shard_map/partial/pallas_call | solution.py:497
  55.3 18.8 %all_to_all.15.coded = s16[8,8,8320]{2,1,0:T(8,128)(2,1)S(1)} all-to-all(s16[8,8,8320]{2,1,0:T(8,128)(2,1)} %partial.1), channel_id=1, replica_groups=mesh['rows'=32,'freq'=8] {'freq'}, dimensions={0} | all-to-all | bytes 2129920 | tf_op jit(solution)/shard_map/all_to_all | solution.py:516
  74.1 0.3 total.1.here
  74.5 1.9 %collective-permute-start.4 = (f32[8,8192]{1,0:T(8,128)S(1)}, f32[8,8192]{1,0:T(8,128)S(1)}, u32[]{:S(2)}, u32[]{:S(2)}) collective-permute-start(f32[8,8192]{1,0:T(8,128)S(1)} %total.1.here), channel_id=1, source_target_pairs={{8,0},{16,8},{24,16},{32,24},{40,32},{48,40},{56,48},{64,56},{72,6... | collective-permute-start | bytes 786440 | tf_op jit(solution)/shard_map/ppermute | solution.py:526
  76.4 8.1 %collective-permute-start.3 = (f32[8,8192]{1,0:T(8,128)S(1)}, f32[8,8192]{1,0:T(8,128)S(1)}, u32[]{:S(2)}, u32[]{:S(2)}) collective-permute-start(f32[8,8192]{1,0:T(8,128)S(1)} %total.1.here), channel_id=1, source_target_pairs={{0,8},{8,16},{16,24},{24,32},{32,40},{40,48},{48,56},{56,64},{64,7... | collective-permute-start | bytes 786440 | tf_op jit(solution)/shard_map/ppermute | solution.py:527
  84.5 2.2 %collective-permute-done.4.below = f32[8,8192]{1,0:T(8,128)S(1)} collective-permute-done((f32[8,8192]{1,0:T(8,128)S(1)}, f32[8,8192]{1,0:T(8,128)S(1)}, u32[]{:S(2)}, u32[]{:S(2)}) %collective-permute-start.4) | collective-permute-done | bytes 262176 | tf_op jit(solution)/shard_map/ppermute | solution.py:526
  86.7 1.1 collective-permute-done.3.above
  87.8 0.6 back.1
  88.5 16.0 %all_to_all.16.coded = s16[8,8,8576]{2,1,0:T(8,128)(2,1)S(1)} all-to-all(s16[8,8,8576]{2,1,0:T(8,128)(2,1)S(1)} %back.1), channel_id=1, replica_groups=mesh['rows'=32,'freq'=8] {'freq'}, dimensions={0} | all-to-all | bytes 2195456 | tf_op jit(solution)/shard_map/all_to_all | solution.py:540
  104.5 24.3 %all_to_all.17.squares = f32[32,8,128]{2,1,0:T(8,128)S(1)} all-to-all(f32[32,8,128]{2,1,0:T(8,128)S(1)} %squares.1), channel_id=1, replica_groups=mesh['rows'=32,'freq'=8] {'rows'}, dimensions={0} | all-to-all | bytes 262144 | tf_op jit(solution)/shard_map/all_to_all | solution.py:550
  128.8 1.6 %result.1 = f32[8,65536]{1,0:T(8,128)} custom-call(s16[8,8,8576]{2,1,0:T(8,128)(2,1)S(1)} %all_to_all.16.coded, f32[32,8,128]{2,1,0:T(8,128)S(1)} %all_to_all.17.squares), custom_call_target="tpu_custom_call" | custom-call | tf_op jit(solution)/shard_map/result/pallas_call | solution.py:552
  (1 shorter events, 0.0 us)
Async XLA Ops:
  2.4 34.8 %collective-permute-start.1 = (s16[8,65536]{1,0:T(8,128)(2,1)}, s16[8,65536]{1,0:T(8,128)(2,1)}, u32[]{:S(2)}, u32[]{:S(2)}) collective-permute-start(s16[8,65536]{1,0:T(8,128)(2,1)} %code.1), channel_id=1, source_target_pairs={{8,0},{16,8},{24,16},{32,24},{40,32},{48,40},{56,48},{64,56},{72,6... | collective-permute-start | bytes 3145736 | tf_op jit(solution)/shard_map/ppermute | solution.py:475
  7.5 29.7 %collective-permute-start = (s16[8,65536]{1,0:T(8,128)(2,1)}, s16[8,65536]{1,0:T(8,128)(2,1)}, u32[]{:S(2)}, u32[]{:S(2)}) collective-permute-start(s16[8,65536]{1,0:T(8,128)(2,1)} %code.1), channel_id=1, source_target_pairs={{0,8},{8,16},{16,24},{24,32},{32,40},{40,48},{48,56},{56,64},{64,7... | collective-permute-start | bytes 3145736 | tf_op jit(solution)/shard_map/ppermute | solution.py:476
  12.7 12.9 %collective-permute-start.2 = (bf16[4,65536]{1,0:T(4,128)(2,1)}, bf16[4,65536]{1,0:T(4,128)(2,1)S(1)}, u32[]{:S(2)}, u32[]{:S(2)}) collective-permute-start(bf16[4,65536]{1,0:T(4,128)(2,1)} %edge.1), channel_id=1, source_target_pairs={{8,0},{16,8},{24,16},{32,24},{40,32},{48,40},{56,48},{64,56},{72,6... | collective-permute-start | bytes 1572872 | tf_op jit(solution)/shard_map/ppermute | solution.py:460
  25.6 0.8 copy-start
  74.5 12.3 %collective-permute-start.4 = (f32[8,8192]{1,0:T(8,128)S(1)}, f32[8,8192]{1,0:T(8,128)S(1)}, u32[]{:S(2)}, u32[]{:S(2)}) collective-permute-start(f32[8,8192]{1,0:T(8,128)S(1)} %total.1.here), channel_id=1, source_target_pairs={{8,0},{16,8},{24,16},{32,24},{40,32},{48,40},{56,48},{64,56},{72,6... | collective-permute-start | bytes 786440 | tf_op jit(solution)/shard_map/ppermute | solution.py:526
  76.4 11.4 %collective-permute-start.3 = (f32[8,8192]{1,0:T(8,128)S(1)}, f32[8,8192]{1,0:T(8,128)S(1)}, u32[]{:S(2)}, u32[]{:S(2)}) collective-permute-start(f32[8,8192]{1,0:T(8,128)S(1)} %total.1.here), channel_id=1, source_target_pairs={{0,8},{8,16},{16,24},{24,32},{32,40},{40,48},{48,56},{56,64},{64,7... | collective-permute-start | bytes 786440 | tf_op jit(solution)/shard_map/ppermute | solution.py:527

commit v5 on v4

--- a/solution.py
+++ b/solution.py
@@ -19,6 +19,7 @@
 TANH_HALF = 0.999329299739067
 DESIGN_STEPS = 32767.0
 CODE_STEPS = 32700.0
+SUM_STAGES = ((8, 16), (32, 64), (128, 1), (2, 4))
 
 f32 = jnp.float32
 i16 = jnp.int16
@@ -376,7 +377,7 @@
     lax.fori_loop(0, piece // width, step, 0)
 
 
-def back_kernel(above, here, below, out, blocks, *, width):
+def back_kernel(above, here, below, out, shared, blocks, *, width):
     piece = here.shape[1]
     zeros = jnp.zeros((8, LANES), f32)
 
@@ -389,26 +390,17 @@
 
     largest, squares = lax.fori_loop(0, piece // width, step, (zeros, zeros))
     encode(blocks, largest, [out.at[peer] for peer in range(out.shape[0])], width)
-    code = scale_code(squares).astype(jnp.int32).astype(i16)
-    values = to_i16(squares / decode_scale(code))
-    for peer in range(out.shape[0]):
-        out[peer, :, piece + LANES : piece + 2 * LANES] = code
-        out[peer, :, piece + 2 * LANES :] = values
-
-
-def squares_kernel(coded, squares):
-    piece = coded.shape[2] - 3 * LANES
-    total = jnp.zeros((8, LANES), f32)
-    for peer in range(coded.shape[0]):
-        values = coded[peer, :, piece + 2 * LANES :].astype(jnp.int32).astype(f32)
-        total = total + values * decode_scale(coded[peer, :, piece + LANES : piece + 2 * LANES])
-    squares[...] = jnp.broadcast_to(total[None], squares.shape)
+    shared[...] = squares
+
+
+def fold_kernel(own, first, second, both, total):
+    total[...] = (own[...] + first[...]) + (second[...] + both[...])
 
 
 def result_kernel(coded, squares, out_far, out, left, *, width, elements):
     peers = coded.shape[0]
     piece = out.shape[1] // peers
-    mean = jnp.sum(jnp.sum(squares[...], axis=0), keepdims=True) * (1.0 / elements) + EPSILON
+    mean = jnp.sum(squares[...], keepdims=True) * (1.0 / elements) + EPSILON
     root = lax.rsqrt(mean)
     root = root * (1.5 - 0.5 * mean * root * root)
 
@@ -417,7 +409,7 @@
         return pltpu.make_async_copy(out.at[:, at], out_far.at[:, at], left.at[peer])
 
     for peer in range(peers):
-        scale = wide(decode_scale(coded[peer, :, piece : piece + LANES]) * root, width)
+        scale = wide(decode_scale(coded[peer, :, piece:]) * root, width)
 
         def step(c, none):
             block = coded[peer, :, cols(c, width)].astype(jnp.int32).astype(f32) * scale
@@ -526,12 +518,12 @@
     spread_below = lax.ppermute(spread, "rows", down)
     spread_above = lax.ppermute(spread, "rows", up)
 
-    wide_coded = jax.ShapeDtypeStruct((peers, slab_rows, piece + 3 * LANES), i16)
-    result = pl.pallas_call(
+    tile = jax.ShapeDtypeStruct((8, LANES), f32)
+    result, squares = pl.pallas_call(
         functools.partial(back_kernel, width=1024),
-        out_shape=wide_coded,
+        out_shape=[coded, tile],
         in_specs=vmem(3),
-        out_specs=vmem(1)[0],
+        out_specs=vmem(2),
         scratch_shapes=[pltpu.VMEM((slab_rows, piece), f32)],
         compiler_params=params(8),
         name="back",
@@ -539,15 +531,20 @@
 
     pieces = lax.all_to_all(result, "freq", 0, 0, tiled=True)
 
-    squares = pl.pallas_call(
-        squares_kernel,
-        out_shape=jax.ShapeDtypeStruct((rows, 8, LANES), f32),
-        in_specs=vmem(1),
-        out_specs=vmem(1)[0],
-        compiler_params=params(8),
-        name="squares",
-    )(pieces)
-    squares = lax.all_to_all(squares, "rows", 0, 0, tiled=True)
+    everyone = ("rows", "freq")
+    for first, second in SUM_STAGES:
+        heard = [
+            lax.ppermute(squares, everyone, [(i, i ^ mask) for i in range(rows * peers)])
+            for mask in (first, second, first | second)
+        ]
+        squares = pl.pallas_call(
+            fold_kernel,
+            out_shape=tile,
+            in_specs=vmem(4),
+            out_specs=vmem(1)[0],
+            compiler_params=params(4),
+            cost_estimate=cost(1 << 20, 1 << 18),
+        )(squares, *heard)
 
     return pl.pallas_call(
         functools.partial(result_kernel, width=2048, elements=float(whole_rows * width)),

time: 131 us -> 132 us (level)
  the two profiles are of different devices: /device:TPU:1 before, /device:TPU:64 now
where the time goes in v5:
time: 132 us; the launch traced here: 131 us
  Pallas kernels  38 us (29%)
  starting transfers between devices  36.6 us (28%)
  waiting for transfers between devices  30 us (23%)
  blocking collectives  25.1 us (19%)
    all_to_all x1, blocking collectives, layer(): received = lax.all_to_all(sent, 'freq', 0, 0, tiled=True)  25.1 us
    ppermute x12, starting transfers between devices, layer(): lax.ppermute(squares, everyone, [(i, i ^ mask) for i in range(rows * peer...  21.1 us
    pallas_call x1, Pallas kernels, layer(): pl.pallas_call(functools.partial(partial_kernel, stages=stages, whole_row...  18.1 us
    ppermute x12, waiting for transfers between devices, layer(): lax.ppermute(squares, everyone, [(i, i ^ mask) for i in range(rows * peer...  15.8 us
    pallas_call x1, Pallas kernels, layer(): pl.pallas_call(functools.partial(element_kernel, width=2048, stages=stage...  10.8 us
    ppermute x1, waiting for transfers between devices, layer(): edge_below = lax.ppermute(edge, 'rows', down)  8.74 us
    ppermute x1, waiting for transfers between devices, layer(): spread_above = lax.ppermute(spread, 'rows', up)  3.82 us
    all_to_all x1, starting transfers between devices, layer(): pieces = lax.all_to_all(result, 'freq', 0, 0, tiled=True)  3.56 us
  transfers between devices with their start and end apart: 18, of which 10 were waited for; matrix products, arithmetic and copies ran while one was open for 0% of the time, Pallas kernels for 11%

profile of v5, /device:TPU:64, one launch (start us, length us, event | category | flops | bytes accessed | tf_op | source)
XLA Modules:
  0.0 131.3 jit_solution(11055582745845448608)
XLA Ops:
  0.0 2.4 %code.1 = s16[8,65536]{1,0:T(8,128)(2,1)} custom-call(f32[8,65536]{1,0:T(8,128)} %refs_0_.1), custom_call_target="tpu_custom_call" | custom-call | tf_op jit(solution)/shard_map/code/pallas_call | solution.py:453
  2.4 1.9 %collective-permute-start.1 = (s16[8,65536]{1,0:T(8,128)(2,1)}, s16[8,65536]{1,0:T(8,128)(2,1)}, u32[]{:S(2)}, u32[]{:S(2)}) collective-permute-start(s16[8,65536]{1,0:T(8,128)(2,1)} %code.1), channel_id=1, source_target_pairs={{8,0},{16,8},{24,16},{32,24},{40,32},{48,40},{56,48},{64,56},{72,6... | collective-permute-start | bytes 3145736 | tf_op jit(solution)/shard_map/ppermute | solution.py:467
  4.3 2.4 %collective-permute-start = (s16[8,65536]{1,0:T(8,128)(2,1)}, s16[8,65536]{1,0:T(8,128)(2,1)}, u32[]{:S(2)}, u32[]{:S(2)}) collective-permute-start(s16[8,65536]{1,0:T(8,128)(2,1)} %code.1), channel_id=1, source_target_pairs={{0,8},{8,16},{16,24},{24,32},{32,40},{40,48},{48,56},{56,64},{64,7... | collective-permute-start | bytes 3145736 | tf_op jit(solution)/shard_map/ppermute | solution.py:468
  6.7 3.3 %edge.1 = bf16[4,65536]{1,0:T(4,128)(2,1)} custom-call(bf16[2,1,8,65536]{3,2,1,0:T(8,128)(2,1)} %state_far.3, bf16[2,1,8,65536]{3,2,1,0:T(8,128)(2,1)} %adjoint_far.3), custom_call_target="tpu_custom_call" | custom-call | flops 4194304 | bytes 4194304 | tf_op jit(solution)/shard_map/edge/pallas_call | solution.py:442
  10.0 3.2 %collective-permute-start.2 = (bf16[4,65536]{1,0:T(4,128)(2,1)}, bf16[4,65536]{1,0:T(4,128)(2,1)S(1)}, u32[]{:S(2)}, u32[]{:S(2)}) collective-permute-start(bf16[4,65536]{1,0:T(4,128)(2,1)} %edge.1), channel_id=1, source_target_pairs={{8,0},{16,8},{24,16},{32,24},{40,32},{48,40},{56,48},{64,56},{72,6... | collective-permute-start | bytes 1572872 | tf_op jit(solution)/shard_map/ppermute | solution.py:452
  13.8 8.7 %collective-permute-done.2.edge_far = bf16[4,65536]{1,0:T(4,128)(2,1)S(1)} collective-permute-done((bf16[4,65536]{1,0:T(4,128)(2,1)}, bf16[4,65536]{1,0:T(4,128)(2,1)S(1)}, u32[]{:S(2)}, u32[]{:S(2)}) %collective-permute-start.2) | collective-permute-done | bytes 524320 | tf_op jit(solution)/shard_map/ppermute | solution.py:452
  23.3 10.8 %element.1 = (f32[8,65536]{1,0:T(8,128)}, f32[8,65536]{1,0:T(8,128)}) custom-call(f32[8]{0:T(128)} %omega_sq.1, s32[1]{0:T(128)S(6)} %copy.7.assign, bf16[2,1,8,65536]{3,2,1,0:T(8,128)(2,1)} %state_far.3, bf16[2,1,8,65536]{3,2,1,0:T(8,128)(2,1)} %adjoint_far.3, bf16[4,65536]{1,0:T(4,128)(2,1)} %copy-done), custom_call_target="tpu_custom_call" | custom-call | flops 41943040 | bytes 8388608 | tf_op jit(solution)/shard_map/element/pallas_call | solution.py:473
  34.1 18.1 %partial.1 = s16[8,8,8320]{2,1,0:T(8,128)(2,1)} custom-call(s32[1]{0:T(128)} %bitcast.top, f32[8,65536]{1,0:T(8,128)} %refs_0_.1, s16[8,65536]{1,0:T(8,128)(2,1)} %collective-permute-done.refs_1_, s16[8,65536]{1,0:T(8,128)(2,1)} %collective-permute-done.1.refs_2_, s32[8,65536]{1,0:T(8,128)} %refs_3_.1, f32[8,65536]{1,0:T(8,128)} %get-tuple-element.9.refs_4_, ...), custom_call_target="tpu_custom_call" | custom-call | flops 78643200 | bytes 14680064 | tf_op jit(solution)/shard_map/partial/pallas_call | solution.py:489
  52.2 25.1 %all_to_all.10.coded = s16[8,8,8320]{2,1,0:T(8,128)(2,1)S(1)} all-to-all(s16[8,8,8320]{2,1,0:T(8,128)(2,1)} %partial.1), channel_id=1, replica_groups=mesh['rows'=32,'freq'=8] {'freq'}, dimensions={0} | all-to-all | bytes 2129920 | tf_op jit(solution)/shard_map/all_to_all | solution.py:508
  77.6 2.3 %collective-permute-start.4 = (f32[8,8192]{1,0:T(8,128)S(1)}, f32[8,8192]{1,0:T(8,128)S(1)}, u32[]{:S(2)}, u32[]{:S(2)}) collective-permute-start(f32[8,8192]{1,0:T(8,128)S(1)} %total.1.here), channel_id=1, source_target_pairs={{8,0},{16,8},{24,16},{32,24},{40,32},{48,40},{56,48},{64,56},{72,6... | collective-permute-start | bytes 786440 | tf_op jit(solution)/shard_map/ppermute | solution.py:518
  80.0 2.2 %collective-permute-start.3 = (f32[8,8192]{1,0:T(8,128)S(1)}, f32[8,8192]{1,0:T(8,128)S(1)}, u32[]{:S(2)}, u32[]{:S(2)}) collective-permute-start(f32[8,8192]{1,0:T(8,128)S(1)} %total.1.here), channel_id=1, source_target_pairs={{0,8},{8,16},{16,24},{24,32},{32,40},{40,48},{48,56},{56,64},{64,7... | collective-permute-start | bytes 786440 | tf_op jit(solution)/shard_map/ppermute | solution.py:519
  82.2 1.7 %collective-permute-done.4.below = f32[8,8192]{1,0:T(8,128)S(1)} collective-permute-done((f32[8,8192]{1,0:T(8,128)S(1)}, f32[8,8192]{1,0:T(8,128)S(1)}, u32[]{:S(2)}, u32[]{:S(2)}) %collective-permute-start.4) | collective-permute-done | bytes 262176 | tf_op jit(solution)/shard_map/ppermute | solution.py:518
  83.8 3.8 %collective-permute-done.3.above = f32[8,8192]{1,0:T(8,128)S(1)} collective-permute-done((f32[8,8192]{1,0:T(8,128)S(1)}, f32[8,8192]{1,0:T(8,128)S(1)}, u32[]{:S(2)}, u32[]{:S(2)}) %collective-permute-start.3) | collective-permute-done | bytes 262176 | tf_op jit(solution)/shard_map/ppermute | solution.py:519
  87.7 1.6 %back.1 = (s16[8,8,8320]{2,1,0:T(8,128)(2,1)}, f32[8,128]{1,0:T(8,128)S(1)}) custom-call(f32[8,8192]{1,0:T(8,128)S(1)} %collective-permute-done.3.above, f32[8,8192]{1,0:T(8,128)S(1)} %total.1.here, f32[8,8192]{1,0:T(8,128)S(1)} %collective-permute-done.4.below), custom_call_target="tpu_custom_call" | custom-call | tf_op jit(solution)/shard_map/back/pallas_call | solution.py:522
  89.3 3.6 %all-to-all-start.1 = ((s16[8,8,8320]{2,1,0:T(8,128)(2,1)}), s16[8,8,8320]{2,1,0:T(8,128)(2,1)S(1)}, u32[]{:S(2)}, u32[]{:S(2)}) async-start(s16[8,8,8320]{2,1,0:T(8,128)(2,1)} %get-tuple-element.11), calls=%async_computation.1 | async-start | bytes 2129920 | tf_op jit(solution)/shard_map/all_to_all | solution.py:532
  92.8 2.4 %collective-permute-start.7 = (f32[8,128]{1,0:T(8,128)S(1)}, f32[8,128]{1,0:T(8,128)S(1)}, u32[]{:S(2)}, u32[]{:S(2)}) collective-permute-start(f32[8,128]{1,0:T(8,128)S(1)} %get-tuple-element.12.own), channel_id=1, source_target_pairs={{0,24},{1,25},{2,26},{3,27},{4,28},{5,29},{6,30},{7,31},{8,16},{9,... | collective-permute-start | bytes 12296 | tf_op jit(solution)/shard_map/ppermute | solution.py:537
  96.6 2.3 %collective-permute-done.6.second = f32[8,128]{1,0:T(8,128)S(1)} collective-permute-done((f32[8,128]{1,0:T(8,128)S(1)}, f32[8,128]{1,0:T(8,128)S(1)}, u32[]{:S(2)}, u32[]{:S(2)}) %collective-permute-start.6) | collective-permute-done | bytes 4128 | tf_op jit(solution)/shard_map/ppermute | solution.py:537
  98.9 3.6 %collective-permute-start.10 = (f32[8,128]{1,0:T(8,128)S(1)}, f32[8,128]{1,0:T(8,128)S(1)}, u32[]{:S(2)}, u32[]{:S(2)}) collective-permute-start(f32[8,128]{1,0:T(8,128)S(1)} %shard_map.64.own), channel_id=1, source_target_pairs={{0,96},{1,97},{2,98},{3,99},{4,100},{5,101},{6,102},{7,103},{8,104... | collective-permute-start | bytes 12296 | tf_op jit(solution)/shard_map/ppermute | solution.py:537
  102.5 2.3 %collective-permute-start.9 = (f32[8,128]{1,0:T(8,128)S(1)}, f32[8,128]{1,0:T(8,128)S(1)}, u32[]{:S(2)}, u32[]{:S(2)}) collective-permute-start(f32[8,128]{1,0:T(8,128)S(1)} %shard_map.64.own), channel_id=1, source_target_pairs={{0,64},{1,65},{2,66},{3,67},{4,68},{5,69},{6,70},{7,71},{8,72},{9,... | collective-permute-start | bytes 12296 | tf_op jit(solution)/shard_map/ppermute | solution.py:537
  105.5 4.5 %collective-permute-done.9.second = f32[8,128]{1,0:T(8,128)S(1)} collective-permute-done((f32[8,128]{1,0:T(8,128)S(1)}, f32[8,128]{1,0:T(8,128)S(1)}, u32[]{:S(2)}, u32[]{:S(2)}) %collective-permute-start.9) | collective-permute-done | bytes 4128 | tf_op jit(solution)/shard_map/ppermute | solution.py:537
  110.0 6.7 %collective-permute-start.13 = (f32[8,128]{1,0:T(8,128)S(1)}, f32[8,128]{1,0:T(8,128)S(1)}, u32[]{:S(2)}, u32[]{:S(2)}) collective-permute-start(f32[8,128]{1,0:T(8,128)S(1)} %shard_map.65.own), channel_id=1, source_target_pairs={{0,129},{1,128},{2,131},{3,130},{4,133},{5,132},{6,135},{7,134},{8... | collective-permute-start | bytes 12296 | tf_op jit(solution)/shard_map/ppermute | solution.py:537
  118.3 3.5 %collective-permute-done.12.second = f32[8,128]{1,0:T(8,128)S(1)} collective-permute-done((f32[8,128]{1,0:T(8,128)S(1)}, f32[8,128]{1,0:T(8,128)S(1)}, u32[]{:S(2)}, u32[]{:S(2)}) %collective-permute-start.12) | collective-permute-done | bytes 4128 | tf_op jit(solution)/shard_map/ppermute | solution.py:537
  121.8 2.8 %collective-permute-start.16 = (f32[8,128]{1,0:T(8,128)S(1)}, f32[8,128]{1,0:T(8,128)S(1)}, u32[]{:S(2)}, u32[]{:S(2)}) collective-permute-start(f32[8,128]{1,0:T(8,128)S(1)} %shard_map.66.own), channel_id=1, source_target_pairs={{0,6},{1,7},{2,4},{3,5},{4,2},{5,3},{6,0},{7,1},{8,14},{9,15},{10,... | collective-permute-start | bytes 12296 | tf_op jit(solution)/shard_map/ppermute | solution.py:537
  126.7 3.0 %collective-permute-done.15.second = f32[8,128]{1,0:T(8,128)S(1)} collective-permute-done((f32[8,128]{1,0:T(8,128)S(1)}, f32[8,128]{1,0:T(8,128)S(1)}, u32[]{:S(2)}, u32[]{:S(2)}) %collective-permute-start.15) | collective-permute-done | bytes 4128 | tf_op jit(solution)/shard_map/ppermute | solution.py:537
  (26 shorter events, 8.4 us)
Async XLA Ops:
  2.4 31.7 %collective-permute-start.1 = (s16[8,65536]{1,0:T(8,128)(2,1)}, s16[8,65536]{1,0:T(8,128)(2,1)}, u32[]{:S(2)}, u32[]{:S(2)}) collective-permute-start(s16[8,65536]{1,0:T(8,128)(2,1)} %code.1), channel_id=1, source_target_pairs={{8,0},{16,8},{24,16},{32,24},{40,32},{48,40},{56,48},{64,56},{72,6... | collective-permute-start | bytes 3145736 | tf_op jit(solution)/shard_map/ppermute | solution.py:467
  4.3 29.8 %collective-permute-start = (s16[8,65536]{1,0:T(8,128)(2,1)}, s16[8,65536]{1,0:T(8,128)(2,1)}, u32[]{:S(2)}, u32[]{:S(2)}) collective-permute-start(s16[8,65536]{1,0:T(8,128)(2,1)} %code.1), channel_id=1, source_target_pairs={{0,8},{8,16},{16,24},{24,32},{32,40},{40,48},{48,56},{56,64},{64,7... | collective-permute-start | bytes 3145736 | tf_op jit(solution)/shard_map/ppermute | solution.py:468
  10.0 12.6 %collective-permute-start.2 = (bf16[4,65536]{1,0:T(4,128)(2,1)}, bf16[4,65536]{1,0:T(4,128)(2,1)S(1)}, u32[]{:S(2)}, u32[]{:S(2)}) collective-permute-start(bf16[4,65536]{1,0:T(4,128)(2,1)} %edge.1), channel_id=1, source_target_pairs={{8,0},{16,8},{24,16},{32,24},{40,32},{48,40},{56,48},{64,56},{72,6... | collective-permute-start | bytes 1572872 | tf_op jit(solution)/shard_map/ppermute | solution.py:452
  22.5 0.8 copy-start
  77.6 6.2 %collective-permute-start.4 = (f32[8,8192]{1,0:T(8,128)S(1)}, f32[8,8192]{1,0:T(8,128)S(1)}, u32[]{:S(2)}, u32[]{:S(2)}) collective-permute-start(f32[8,8192]{1,0:T(8,128)S(1)} %total.1.here), channel_id=1, source_target_pairs={{8,0},{16,8},{24,16},{32,24},{40,32},{48,40},{56,48},{64,56},{72,6... | collective-permute-start | bytes 786440 | tf_op jit(solution)/shard_map/ppermute | solution.py:518
  80.0 7.7 %collective-permute-start.3 = (f32[8,8192]{1,0:T(8,128)S(1)}, f32[8,8192]{1,0:T(8,128)S(1)}, u32[]{:S(2)}, u32[]{:S(2)}) collective-permute-start(f32[8,8192]{1,0:T(8,128)S(1)} %total.1.here), channel_id=1, source_target_pairs={{0,8},{8,16},{16,24},{24,32},{32,40},{40,48},{48,56},{56,64},{64,7... | collective-permute-start | bytes 786440 | tf_op jit(solution)/shard_map/ppermute | solution.py:519
  89.3 40.5 %all-to-all-start.1 = ((s16[8,8,8320]{2,1,0:T(8,128)(2,1)}), s16[8,8,8320]{2,1,0:T(8,128)(2,1)S(1)}, u32[]{:S(2)}, u32[]{:S(2)}) async-start(s16[8,8,8320]{2,1,0:T(8,128)(2,1)} %get-tuple-element.11), calls=%async_computation.1 | async-start | bytes 2129920 | tf_op jit(solution)/shard_map/all_to_all | solution.py:532
  92.8 3.8 %collective-permute-start.7 = (f32[8,128]{1,0:T(8,128)S(1)}, f32[8,128]{1,0:T(8,128)S(1)}, u32[]{:S(2)}, u32[]{:S(2)}) collective-permute-start(f32[8,128]{1,0:T(8,128)S(1)} %get-tuple-element.12.own), channel_id=1, source_target_pairs={{0,24},{1,25},{2,26},{3,27},{4,28},{5,29},{6,30},{7,31},{8,16},{9,... | collective-permute-start | bytes 12296 | tf_op jit(solution)/shard_map/ppermute | solution.py:537
  95.3 3.6 %collective-permute-start.6 = (f32[8,128]{1,0:T(8,128)S(1)}, f32[8,128]{1,0:T(8,128)S(1)}, u32[]{:S(2)}, u32[]{:S(2)}) collective-permute-start(f32[8,128]{1,0:T(8,128)S(1)} %get-tuple-element.12.own), channel_id=1, source_target_pairs={{0,16},{1,17},{2,18},{3,19},{4,20},{5,21},{6,22},{7,23},{8,24},{9,... | collective-permute-start | bytes 12296 | tf_op jit(solution)/shard_map/ppermute | solution.py:537
  95.3 3.6 %collective-permute-start.5 = (f32[8,128]{1,0:T(8,128)S(1)}, f32[8,128]{1,0:T(8,128)S(1)}, u32[]{:S(2)}, u32[]{:S(2)}) collective-permute-start(f32[8,128]{1,0:T(8,128)S(1)} %get-tuple-element.12.own), channel_id=1, source_target_pairs={{0,8},{1,9},{2,10},{3,11},{4,12},{5,13},{6,14},{7,15},{8,0},{9,1},... | collective-permute-start | bytes 12296 | tf_op jit(solution)/shard_map/ppermute | solution.py:537
  98.9 6.6 %collective-permute-start.10 = (f32[8,128]{1,0:T(8,128)S(1)}, f32[8,128]{1,0:T(8,128)S(1)}, u32[]{:S(2)}, u32[]{:S(2)}) collective-permute-start(f32[8,128]{1,0:T(8,128)S(1)} %shard_map.64.own), channel_id=1, source_target_pairs={{0,96},{1,97},{2,98},{3,99},{4,100},{5,101},{6,102},{7,103},{8,104... | collective-permute-start | bytes 12296 | tf_op jit(solution)/shard_map/ppermute | solution.py:537
  102.5 7.5 %collective-permute-start.9 = (f32[8,128]{1,0:T(8,128)S(1)}, f32[8,128]{1,0:T(8,128)S(1)}, u32[]{:S(2)}, u32[]{:S(2)}) collective-permute-start(f32[8,128]{1,0:T(8,128)S(1)} %shard_map.64.own), channel_id=1, source_target_pairs={{0,64},{1,65},{2,66},{3,67},{4,68},{5,69},{6,70},{7,71},{8,72},{9,... | collective-permute-start | bytes 12296 | tf_op jit(solution)/shard_map/ppermute | solution.py:537
  104.9 5.2 %collective-permute-start.8 = (f32[8,128]{1,0:T(8,128)S(1)}, f32[8,128]{1,0:T(8,128)S(1)}, u32[]{:S(2)}, u32[]{:S(2)}) collective-permute-start(f32[8,128]{1,0:T(8,128)S(1)} %shard_map.64.own), channel_id=1, source_target_pairs={{0,32},{1,33},{2,34},{3,35},{4,36},{5,37},{6,38},{7,39},{8,40},{9,... | collective-permute-start | bytes 12296 | tf_op jit(solution)/shard_map/ppermute | solution.py:537
  110.0 8.3 %collective-permute-start.13 = (f32[8,128]{1,0:T(8,128)S(1)}, f32[8,128]{1,0:T(8,128)S(1)}, u32[]{:S(2)}, u32[]{:S(2)}) collective-permute-start(f32[8,128]{1,0:T(8,128)S(1)} %shard_map.65.own), channel_id=1, source_target_pairs={{0,129},{1,128},{2,131},{3,130},{4,133},{5,132},{6,135},{7,134},{8... | collective-permute-start | bytes 12296 | tf_op jit(solution)/shard_map/ppermute | solution.py:537
  116.7 5.1 %collective-permute-start.12 = (f32[8,128]{1,0:T(8,128)S(1)}, f32[8,128]{1,0:T(8,128)S(1)}, u32[]{:S(2)}, u32[]{:S(2)}) collective-permute-start(f32[8,128]{1,0:T(8,128)S(1)} %shard_map.65.own), channel_id=1, source_target_pairs={{0,1},{1,0},{2,3},{3,2},{4,5},{5,4},{6,7},{7,6},{8,9},{9,8},{10,11... | collective-permute-start | bytes 12296 | tf_op jit(solution)/shard_map/ppermute | solution.py:537
  116.7 5.1 %collective-permute-start.11 = (f32[8,128]{1,0:T(8,128)S(1)}, f32[8,128]{1,0:T(8,128)S(1)}, u32[]{:S(2)}, u32[]{:S(2)}) collective-permute-start(f32[8,128]{1,0:T(8,128)S(1)} %shard_map.65.own), channel_id=1, source_target_pairs={{0,128},{1,129},{2,130},{3,131},{4,132},{5,133},{6,134},{7,135},{8... | collective-permute-start | bytes 12296 | tf_op jit(solution)/shard_map/ppermute | solution.py:537
  121.8 4.9 %collective-permute-start.16 = (f32[8,128]{1,0:T(8,128)S(1)}, f32[8,128]{1,0:T(8,128)S(1)}, u32[]{:S(2)}, u32[]{:S(2)}) collective-permute-start(f32[8,128]{1,0:T(8,128)S(1)} %shard_map.66.own), channel_id=1, source_target_pairs={{0,6},{1,7},{2,4},{3,5},{4,2},{5,3},{6,0},{7,1},{8,14},{9,15},{10,... | collective-permute-start | bytes 12296 | tf_op jit(solution)/shard_map/ppermute | solution.py:537
  124.6 5.1 %collective-permute-start.15 = (f32[8,128]{1,0:T(8,128)S(1)}, f32[8,128]{1,0:T(8,128)S(1)}, u32[]{:S(2)}, u32[]{:S(2)}) collective-permute-start(f32[8,128]{1,0:T(8,128)S(1)} %shard_map.66.own), channel_id=1, source_target_pairs={{0,4},{1,5},{2,6},{3,7},{4,0},{5,1},{6,2},{7,3},{8,12},{9,13},{10,... | collective-permute-start | bytes 12296 | tf_op jit(solution)/shard_map/ppermute | solution.py:537
  125.5 4.3 %collective-permute-start.14 = (f32[8,128]{1,0:T(8,128)S(1)}, f32[8,128]{1,0:T(8,128)S(1)}, u32[]{:S(2)}, u32[]{:S(2)}) collective-permute-start(f32[8,128]{1,0:T(8,128)S(1)} %shard_map.66.own), channel_id=1, source_target_pairs={{0,2},{1,3},{2,0},{3,1},{4,6},{5,7},{6,4},{7,5},{8,10},{9,11},{10,... | collective-permute-start | bytes 12296 | tf_op jit(solution)/shard_map/ppermute | solution.py:537

commit v6 on v4

--- a/solution.py
+++ b/solution.py
@@ -71,12 +71,37 @@
     return pltpu.roll(block, (width - count) % width, 1)
 
 
-def col_filter(block):
-    for step in (1, 3):
-        near = moved(block, step) + moved(block, -step)
-        far = moved(block, 2 * step) + moved(block, -2 * step)
-        block = 3.0 * block + 2.0 * near + far
-    return block
+def band():
+    shape = (3 * LANES, LANES)
+    source = lax.broadcasted_iota(jnp.int32, shape, 0) - LANES
+    target = lax.broadcasted_iota(jnp.int32, shape, 1)
+    taps = jnp.maximum(RADIUS + 1 - jnp.abs(source - target), 0)
+    return taps.astype(f32).astype(jnp.bfloat16)
+
+
+def col_filter(window, taps):
+    count = window.shape[1] // LANES - 2
+    half = count // 2
+    tiles = [window[:, i * LANES : (i + 1) * LANES] for i in range(count + 2)]
+    stacked = jnp.concatenate(
+        [tiles[i + side] for i in range(half + 2) for side in (0, half)], axis=0
+    )
+    coarse = stacked.astype(jnp.bfloat16)
+    fine = (stacked - coarse.astype(f32)).astype(jnp.bfloat16)
+    left, here, right = (slice(start, start + 16 * half) for start in (0, 16, 32))
+
+    def product(first, second, weights):
+        return jnp.dot(
+            jnp.concatenate([first, second], axis=1), weights, preferred_element_type=f32
+        )
+
+    near, far = taps[: 2 * LANES], taps[2 * LANES :]
+    total = product(coarse[left], coarse[here], near) + product(fine[left], fine[here], near)
+    total = total + product(coarse[right], fine[right], jnp.concatenate([far, far], axis=0))
+    halves = [
+        [total[16 * i + 8 * side : 16 * i + 8 * side + 8] for i in range(half)] for side in (0, 1)
+    ]
+    return jnp.concatenate(halves[0] + halves[1], axis=1)
 
 
 def padded_cols(index, width):
@@ -325,6 +350,7 @@
     for copy in late:
         copy.wait()
 
+    taps = band()
     row = top[0] + row_ids(LANES)
     lane = lax.broadcasted_iota(jnp.int32, (8, LANES), 1)
     full = float((RADIUS + 1) ** 2)
@@ -337,7 +363,7 @@
         first = inside * jnp.where(c == 0, left_end, 1.0)
         last = inside * jnp.where(c == peers - 1, right_end, 1.0)
         weights = jnp.concatenate([first] + [inside] * (piece // LANES - 2) + [last], axis=1)
-        tilde = col_filter(rowed[:, padded_cols(c, piece)])[:, LANES : LANES + piece] * weights
+        tilde = col_filter(rowed[:, padded_cols(c, piece)], taps) * weights
         steep = jnp.tanh(SHARPNESS * (tilde - THRESHOLD))
         solid = passive[:, at] > 0
         density = jnp.where(solid, 1.0, (TANH_HALF + steep) * (0.5 / TANH_HALF))
@@ -349,7 +375,7 @@
     lax.fori_loop(0, peers, scale, 0)
 
     def send(peer, none):
-        block = col_filter(spread[:, padded_cols(peer, piece)])[:, LANES : LANES + piece]
+        block = col_filter(spread[:, padded_cols(peer, piece)], taps)
         blocks[...] = block
         encode(blocks, folded_max(block), [out.at[peer]], narrow)
         pltpu.make_async_copy(out.at[peer], out_far.at[peer], left.at[peer]).start()

time: 131 us -> 126 us (0.962)
  Pallas kernels: 37 us -> 32.1 us
    pallas_call x1, Pallas kernels: 18.1 us -> 13.1 us  [layer(): pl.pallas_call(functools.partial(partial_kernel, stages=stages, whole_row...]
where the time goes in v6:
time: 126 us; the launch traced here: 125 us
  blocking collectives  59.2 us (47%)
  Pallas kernels  32.1 us (25%)
  starting transfers between devices  20.4 us (16%)
  waiting for transfers between devices  12.2 us (10%)
    all_to_all x1, blocking collectives, layer(): squares = lax.all_to_all(squares, 'rows', 0, 0, tiled=True)  24.3 us
    all_to_all x1, blocking collectives, layer(): received = lax.all_to_all(sent, 'freq', 0, 0, tiled=True)  18.8 us
    all_to_all x1, blocking collectives, layer(): pieces = lax.all_to_all(result, 'freq', 0, 0, tiled=True)  16 us
    pallas_call x1, Pallas kernels, layer(): pl.pallas_call(functools.partial(partial_kernel, stages=stages, whole_row...  13.1 us
    pallas_call x1, Pallas kernels, layer(): pl.pallas_call(functools.partial(element_kernel, width=2048, stages=stage...  10.8 us
    ppermute x1, waiting for transfers between devices, layer(): edge_below = lax.ppermute(edge, 'rows', down)  8.89 us
    ppermute x1, starting transfers between devices, layer(): spread_above = lax.ppermute(spread, 'rows', up)  8.1 us
    ppermute x1, starting transfers between devices, layer(): code_below = lax.ppermute(code, 'rows', down)  5.11 us
  transfers between devices with their start and end apart: 5, of which 3 were waited for; matrix products, arithmetic and copies ran while one was open for 0% of the time, Pallas kernels for 11%

profile of v6, /device:TPU:1, one launch (start us, length us, event | category | flops | bytes accessed | tf_op | source)
XLA Modules:
  0.0 125.4 jit_solution(17675902175331224335)
XLA Ops:
  0.0 2.4 %code.1 = s16[8,65536]{1,0:T(8,128)(2,1)} custom-call(f32[8,65536]{1,0:T(8,128)} %refs_0_.1), custom_call_target="tpu_custom_call" | custom-call | tf_op jit(solution)/shard_map/code/pallas_call | solution.py:487
  2.4 5.1 %collective-permute-start.1 = (s16[8,65536]{1,0:T(8,128)(2,1)}, s16[8,65536]{1,0:T(8,128)(2,1)}, u32[]{:S(2)}, u32[]{:S(2)}) collective-permute-start(s16[8,65536]{1,0:T(8,128)(2,1)} %code.1), channel_id=1, source_target_pairs={{8,0},{16,8},{24,16},{32,24},{40,32},{48,40},{56,48},{64,56},{72,6... | collective-permute-start | bytes 3145736 | tf_op jit(solution)/shard_map/ppermute | solution.py:501
  7.5 1.9 %collective-permute-start = (s16[8,65536]{1,0:T(8,128)(2,1)}, s16[8,65536]{1,0:T(8,128)(2,1)}, u32[]{:S(2)}, u32[]{:S(2)}) collective-permute-start(s16[8,65536]{1,0:T(8,128)(2,1)} %code.1), channel_id=1, source_target_pairs={{0,8},{8,16},{16,24},{24,32},{32,40},{40,48},{48,56},{56,64},{64,7... | collective-permute-start | bytes 3145736 | tf_op jit(solution)/shard_map/ppermute | solution.py:502
  9.4 3.3 %edge.1 = bf16[4,65536]{1,0:T(4,128)(2,1)} custom-call(bf16[2,1,8,65536]{3,2,1,0:T(8,128)(2,1)} %state_far.3, bf16[2,1,8,65536]{3,2,1,0:T(8,128)(2,1)} %adjoint_far.3), custom_call_target="tpu_custom_call" | custom-call | flops 4194304 | bytes 4194304 | tf_op jit(solution)/shard_map/edge/pallas_call | solution.py:476
  12.7 3.4 %collective-permute-start.2 = (bf16[4,65536]{1,0:T(4,128)(2,1)}, bf16[4,65536]{1,0:T(4,128)(2,1)S(1)}, u32[]{:S(2)}, u32[]{:S(2)}) collective-permute-start(bf16[4,65536]{1,0:T(4,128)(2,1)} %edge.1), channel_id=1, source_target_pairs={{8,0},{16,8},{24,16},{32,24},{40,32},{48,40},{56,48},{64,56},{72,6... | collective-permute-start | bytes 1572872 | tf_op jit(solution)/shard_map/ppermute | solution.py:486
  16.7 8.9 %collective-permute-done.2.edge_far = bf16[4,65536]{1,0:T(4,128)(2,1)S(1)} collective-permute-done((bf16[4,65536]{1,0:T(4,128)(2,1)}, bf16[4,65536]{1,0:T(4,128)(2,1)S(1)}, u32[]{:S(2)}, u32[]{:S(2)}) %collective-permute-start.2) | collective-permute-done | bytes 524320 | tf_op jit(solution)/shard_map/ppermute | solution.py:486
  25.6 0.0 copy-start
  25.6 0.8 copy-done
  26.4 10.8 %element.1 = (f32[8,65536]{1,0:T(8,128)}, f32[8,65536]{1,0:T(8,128)}) custom-call(f32[8]{0:T(128)} %omega_sq.1, s32[1]{0:T(128)S(6)} %copy.7.assign, bf16[2,1,8,65536]{3,2,1,0:T(8,128)(2,1)} %state_far.3, bf16[2,1,8,65536]{3,2,1,0:T(8,128)(2,1)} %adjoint_far.3, bf16[4,65536]{1,0:T(4,128)(2,1)} %copy-done), custom_call_target="tpu_custom_call" | custom-call | flops 41943040 | bytes 8388608 | tf_op jit(solution)/shard_map/element/pallas_call | solution.py:507
  37.2 0.0 collective-permute-done.1.refs_2_
  37.2 0.0 collective-permute-done.refs_1_
  37.2 13.1 %partial.1 = s16[8,8,8320]{2,1,0:T(8,128)(2,1)} custom-call(s32[1]{0:T(128)} %bitcast.top, f32[8,65536]{1,0:T(8,128)} %refs_0_.1, s16[8,65536]{1,0:T(8,128)(2,1)} %collective-permute-done.refs_1_, s16[8,65536]{1,0:T(8,128)(2,1)} %collective-permute-done.1.refs_2_, s32[8,65536]{1,0:T(8,128)} %refs_3_.1, f32[8,65536]{1,0:T(8,128)} %get-tuple-element.7.refs_4_, ...), custom_call_target="tpu_custom_call" | custom-call | flops 78643200 | bytes 14680064 | tf_op jit(solution)/shard_map/partial/pallas_call | solution.py:523
  50.4 18.8 %all_to_all.15.coded = s16[8,8,8320]{2,1,0:T(8,128)(2,1)S(1)} all-to-all(s16[8,8,8320]{2,1,0:T(8,128)(2,1)} %partial.1), channel_id=1, replica_groups=mesh['rows'=32,'freq'=8] {'freq'}, dimensions={0} | all-to-all | bytes 2129920 | tf_op jit(solution)/shard_map/all_to_all | solution.py:542
  69.2 0.3 total.1.here
  69.5 1.9 %collective-permute-start.4 = (f32[8,8192]{1,0:T(8,128)S(1)}, f32[8,8192]{1,0:T(8,128)S(1)}, u32[]{:S(2)}, u32[]{:S(2)}) collective-permute-start(f32[8,8192]{1,0:T(8,128)S(1)} %total.1.here), channel_id=1, source_target_pairs={{8,0},{16,8},{24,16},{32,24},{40,32},{48,40},{56,48},{64,56},{72,6... | collective-permute-start | bytes 786440 | tf_op jit(solution)/shard_map/ppermute | solution.py:552
  71.5 8.1 %collective-permute-start.3 = (f32[8,8192]{1,0:T(8,128)S(1)}, f32[8,8192]{1,0:T(8,128)S(1)}, u32[]{:S(2)}, u32[]{:S(2)}) collective-permute-start(f32[8,8192]{1,0:T(8,128)S(1)} %total.1.here), channel_id=1, source_target_pairs={{0,8},{8,16},{16,24},{24,32},{32,40},{40,48},{48,56},{56,64},{64,7... | collective-permute-start | bytes 786440 | tf_op jit(solution)/shard_map/ppermute | solution.py:553
  79.6 2.2 %collective-permute-done.4.below = f32[8,8192]{1,0:T(8,128)S(1)} collective-permute-done((f32[8,8192]{1,0:T(8,128)S(1)}, f32[8,8192]{1,0:T(8,128)S(1)}, u32[]{:S(2)}, u32[]{:S(2)}) %collective-permute-start.4) | collective-permute-done | bytes 262176 | tf_op jit(solution)/shard_map/ppermute | solution.py:552
  81.8 1.1 collective-permute-done.3.above
  82.9 0.6 back.1
  83.5 16.0 %all_to_all.16.coded = s16[8,8,8576]{2,1,0:T(8,128)(2,1)S(1)} all-to-all(s16[8,8,8576]{2,1,0:T(8,128)(2,1)S(1)} %back.1), channel_id=1, replica_groups=mesh['rows'=32,'freq'=8] {'freq'}, dimensions={0} | all-to-all | bytes 2195456 | tf_op jit(solution)/shard_map/all_to_all | solution.py:566
  99.5 24.3 %all_to_all.17.squares = f32[32,8,128]{2,1,0:T(8,128)S(1)} all-to-all(f32[32,8,128]{2,1,0:T(8,128)S(1)} %squares.1), channel_id=1, replica_groups=mesh['rows'=32,'freq'=8] {'rows'}, dimensions={0} | all-to-all | bytes 262144 | tf_op jit(solution)/shard_map/all_to_all | solution.py:576
  123.9 1.6 %result.1 = f32[8,65536]{1,0:T(8,128)} custom-call(s16[8,8,8576]{2,1,0:T(8,128)(2,1)S(1)} %all_to_all.16.coded, f32[32,8,128]{2,1,0:T(8,128)S(1)} %all_to_all.17.squares), custom_call_target="tpu_custom_call" | custom-call | tf_op jit(solution)/shard_map/result/pallas_call | solution.py:578
  (1 shorter events, 0.0 us)
Async XLA Ops:
  2.4 34.8 %collective-permute-start.1 = (s16[8,65536]{1,0:T(8,128)(2,1)}, s16[8,65536]{1,0:T(8,128)(2,1)}, u32[]{:S(2)}, u32[]{:S(2)}) collective-permute-start(s16[8,65536]{1,0:T(8,128)(2,1)} %code.1), channel_id=1, source_target_pairs={{8,0},{16,8},{24,16},{32,24},{40,32},{48,40},{56,48},{64,56},{72,6... | collective-permute-start | bytes 3145736 | tf_op jit(solution)/shard_map/ppermute | solution.py:501
  7.5 29.7 %collective-permute-start = (s16[8,65536]{1,0:T(8,128)(2,1)}, s16[8,65536]{1,0:T(8,128)(2,1)}, u32[]{:S(2)}, u32[]{:S(2)}) collective-permute-start(s16[8,65536]{1,0:T(8,128)(2,1)} %code.1), channel_id=1, source_target_pairs={{0,8},{8,16},{16,24},{24,32},{32,40},{40,48},{48,56},{56,64},{64,7... | collective-permute-start | bytes 3145736 | tf_op jit(solution)/shard_map/ppermute | solution.py:502
  12.7 12.9 %collective-permute-start.2 = (bf16[4,65536]{1,0:T(4,128)(2,1)}, bf16[4,65536]{1,0:T(4,128)(2,1)S(1)}, u32[]{:S(2)}, u32[]{:S(2)}) collective-permute-start(bf16[4,65536]{1,0:T(4,128)(2,1)} %edge.1), channel_id=1, source_target_pairs={{8,0},{16,8},{24,16},{32,24},{40,32},{48,40},{56,48},{64,56},{72,6... | collective-permute-start | bytes 1572872 | tf_op jit(solution)/shard_map/ppermute | solution.py:486
  25.6 0.8 copy-start
  69.5 12.3 %collective-permute-start.4 = (f32[8,8192]{1,0:T(8,128)S(1)}, f32[8,8192]{1,0:T(8,128)S(1)}, u32[]{:S(2)}, u32[]{:S(2)}) collective-permute-start(f32[8,8192]{1,0:T(8,128)S(1)} %total.1.here), channel_id=1, source_target_pairs={{8,0},{16,8},{24,16},{32,24},{40,32},{48,40},{56,48},{64,56},{72,6... | collective-permute-start | bytes 786440 | tf_op jit(solution)/shard_map/ppermute | solution.py:552
  71.5 11.4 %collective-permute-start.3 = (f32[8,8192]{1,0:T(8,128)S(1)}, f32[8,8192]{1,0:T(8,128)S(1)}, u32[]{:S(2)}, u32[]{:S(2)}) collective-permute-start(f32[8,8192]{1,0:T(8,128)S(1)} %total.1.here), channel_id=1, source_target_pairs={{0,8},{8,16},{16,24},{24,32},{32,40},{40,48},{48,56},{56,64},{64,7... | collective-permute-start | bytes 786440 | tf_op jit(solution)/shard_map/ppermute | solution.py:553

commit v7 on v6

--- a/solution.py
+++ b/solution.py
@@ -171,22 +171,61 @@
     ]
 
 
-def edge_kernel(state_far, adjoint_far, edge, state, adjoint, arrived, *, width, stages):
+def prepare_kernel(
+    state_far,
+    adjoint_far,
+    design_far,
+    edge,
+    code_far,
+    state,
+    adjoint,
+    design,
+    code,
+    arrived,
+    design_arrived,
+    left,
+    *,
+    width,
+    stages,
+):
     ids = row_ids(width)
     span = edge.shape[1] // stages
+    steps = span // width
     copies = functools.partial(
         field_copies, (state_far, adjoint_far), (state, adjoint), arrived, span=span
     )
+
+    def load(stage):
+        at = pl.ds(stage * span, span)
+        return pltpu.make_async_copy(design_far.at[:, at], design.at[:, at], design_arrived.at[stage])
+
+    def save(stage):
+        at = pl.ds(stage * span, span)
+        return pltpu.make_async_copy(code.at[:, at], code_far.at[:, at], left.at[stage])
+
+    for stage in range(stages):
+        load(stage).start()
     for stage in range(stages):
         for copy in copies(stage):
             copy.start()
 
     for stage in range(stages):
+        load(stage).wait()
+
+        def encode_rows(c, none):
+            at = cols(stage * steps + c, width)
+            code[:, at] = to_i16(design[:, at] * DESIGN_STEPS)
+            return none
+
+        lax.fori_loop(0, steps, encode_rows, 0)
+        save(stage).start()
+
+    for stage in range(stages):
         for copy in copies(stage):
             copy.wait()
 
-        def step(c, none):
-            at = cols(stage * (span // width) + c, width)
+        def pick_rows(c, none):
+            at = cols(stage * steps + c, width)
             first = state[0, 0, :, at].astype(f32)
             rows = [state[1, 0, :, at], adjoint[0, 0, :, at], adjoint[1, 0, :, at]]
             for place, row in enumerate(rows):
@@ -194,32 +233,7 @@
             edge[:, at] = first[:4].astype(jnp.bfloat16)
             return none
 
-        lax.fori_loop(0, span // width, step, 0)
-
-
-def code_kernel(design_far, code_far, design, code, arrived, left, *, width, stages):
-    span = design.shape[1] // stages
-
-    def load(stage):
-        at = pl.ds(stage * span, span)
-        return pltpu.make_async_copy(design_far.at[:, at], design.at[:, at], arrived.at[stage])
-
-    def save(stage):
-        at = pl.ds(stage * span, span)
-        return pltpu.make_async_copy(code.at[:, at], code_far.at[:, at], left.at[stage])
-
-    for stage in range(stages):
-        load(stage).start()
-    for stage in range(stages):
-        load(stage).wait()
-
-        def step(c, none):
-            at = cols(stage * (span // width) + c, width)
-            code[:, at] = to_i16(design[:, at] * DESIGN_STEPS)
-            return none
-
-        lax.fori_loop(0, span // width, step, 0)
-        save(stage).start()
+        lax.fori_loop(0, steps, pick_rows, 0)
     for stage in range(stages):
         save(stage).wait()
 
@@ -468,36 +482,33 @@
 
     in_place = pl.BlockSpec(memory_space=pltpu.HBM)
     stages = 4
+    element_stages = 8
     field_scratch = [
         pltpu.VMEM(state.shape, state.dtype),
         pltpu.VMEM(adjoint.shape, adjoint.dtype),
         pltpu.SemaphoreType.DMA((stages, 2)),
     ]
-    edge = pl.pallas_call(
-        functools.partial(edge_kernel, width=2048, stages=stages),
-        out_shape=jax.ShapeDtypeStruct((4, width), jnp.bfloat16),
-        in_specs=[in_place, in_place],
-        out_specs=vmem(1)[0],
-        scratch_shapes=field_scratch,
+    design_scratch = [
+        pltpu.VMEM((slab_rows, width), f32),
+        pltpu.VMEM((slab_rows, width), i16),
+    ]
+    edge, code = pl.pallas_call(
+        functools.partial(prepare_kernel, width=2048, stages=stages),
+        out_shape=[
+            jax.ShapeDtypeStruct((4, width), jnp.bfloat16),
+            jax.ShapeDtypeStruct((slab_rows, width), i16),
+        ],
+        in_specs=[in_place] * 3,
+        out_specs=vmem(1) + [in_place],
+        scratch_shapes=field_scratch[:2]
+        + design_scratch
+        + [field_scratch[2]]
+        + [pltpu.SemaphoreType.DMA((stages,))] * 2,
         compiler_params=params(63),
-        cost_estimate=cost(8 * slab_rows * width, 4 * 1024 * 1024),
-        name="edge",
-    )(state, adjoint)
+        cost_estimate=cost(8 * slab_rows * width, 7 * 1024 * 1024),
+        name="prepare",
+    )(state, adjoint, design)
     edge_below = lax.ppermute(edge, "rows", down)
-    code = pl.pallas_call(
-        functools.partial(code_kernel, width=2048, stages=stages),
-        out_shape=jax.ShapeDtypeStruct((slab_rows, width), i16),
-        in_specs=[in_place],
-        out_specs=in_place,
-        scratch_shapes=[
-            pltpu.VMEM((slab_rows, width), f32),
-            pltpu.VMEM((slab_rows, width), i16),
-            pltpu.SemaphoreType.DMA((stages,)),
-            pltpu.SemaphoreType.DMA((stages,)),
-        ],
-        compiler_params=params(63),
-        name="code",
-    )(design)
     code_below = lax.ppermute(code, "rows", down)
     code_above = lax.ppermute(code, "rows", up)
 
@@ -505,15 +516,15 @@
 
     slab = jax.ShapeDtypeStruct((slab_rows, width), f32)
     elastic, inertia = pl.pallas_call(
-        functools.partial(element_kernel, width=2048, stages=stages),
+        functools.partial(element_kernel, width=2048, stages=element_stages),
         out_shape=[slab, slab],
         in_specs=[smem, smem] + [in_place] * 3,
         out_specs=[in_place, in_place],
         scratch_shapes=field_scratch[:2]
         + [pltpu.VMEM(edge.shape, edge.dtype)]
         + [pltpu.VMEM((slab_rows, width), f32)] * 2
-        + [pltpu.SemaphoreType.DMA((stages, 3)), pltpu.SemaphoreType.DMA((stages, 2))],
-        compiler_params=params(63),
+        + [pltpu.SemaphoreType.DMA((element_stages, count)) for count in (3, 2)],
+        compiler_params=params(53),
         cost_estimate=cost(80 * slab_rows * width, 8 * 1024 * 1024),
         name="element",
     )(omega_sq, assign, state, adjoint, edge_below)

time: 126 us -> 127 us (level)
  waiting for transfers between devices: 12.2 us -> 15.4 us
  Pallas kernels: 32.1 us -> 30.8 us
    ppermute x1, waiting for transfers between devices: 8.89 us -> 12.2 us  [layer(): edge_below = lax.ppermute(edge, 'rows', down)]
    pallas_call x3 -> x2, Pallas kernels: 16.4 us -> 15.1 us  [the longest x1 10.5 us: layer(): pl.pallas_call(functools.partial(element_kernel, width=2048, stages=eleme...]
  transfers between devices with their start and end apart: 5 -> 5, of which waited for: 3 -> 3; matrix products, arithmetic and copies ran while one was open for 0% -> 0% of each run, Pallas kernels for 11% -> 8%
where the time goes in v7:
time: 127 us
  blocking collectives  59.2 us (47%)
  Pallas kernels  30.8 us (24%)
  starting transfers between devices  20.4 us (16%)
  waiting for transfers between devices  15.4 us (12%)
    all_to_all x1, blocking collectives, layer(): squares = lax.all_to_all(squares, 'rows', 0, 0, tiled=True)  24.3 us
    all_to_all x1, blocking collectives, layer(): received = lax.all_to_all(sent, 'freq', 0, 0, tiled=True)  18.8 us
    all_to_all x1, blocking collectives, layer(): pieces = lax.all_to_all(result, 'freq', 0, 0, tiled=True)  16 us
    pallas_call x1, Pallas kernels, layer(): pl.pallas_call(functools.partial(partial_kernel, stages=stages, whole_row...  13.1 us
    ppermute x1, waiting for transfers between devices, layer(): edge_below = lax.ppermute(edge, 'rows', down)  12.2 us
    pallas_call x1, Pallas kernels, layer(): pl.pallas_call(functools.partial(element_kernel, width=2048, stages=eleme...  10.5 us
    ppermute x1, starting transfers between devices, layer(): spread_above = lax.ppermute(spread, 'rows', up)  8.1 us
    ppermute x1, starting transfers between devices, layer(): code_below = lax.ppermute(code, 'rows', down)  5.11 us
  transfers between devices with their start and end apart: 5, of which 3 were waited for; matrix products, arithmetic and copies ran while one was open for 0% of the time, Pallas kernels for 8%

profile of v7, /device:TPU:1, one launch (start us, length us, event | category | flops | bytes accessed | tf_op | source)
XLA Modules:
  0.0 126.6 jit_solution(12699948986200948684)
XLA Ops:
  0.0 0.0 copy-start
  0.0 4.6 %prepare.1 = (bf16[4,65536]{1,0:T(4,128)(2,1)}, s16[8,65536]{1,0:T(8,128)(2,1)}) custom-call(bf16[2,1,8,65536]{3,2,1,0:T(8,128)(2,1)} %state_far.3, bf16[2,1,8,65536]{3,2,1,0:T(8,128)(2,1)} %adjoint_far.3, f32[8,65536]{1,0:T(8,128)} %refs_0_.1), custom_call_target="tpu_custom_call" | custom-call | flops 4194304 | bytes 7340032 | tf_op jit(solution)/shard_map/prepare/pallas_call | solution.py:495
  4.6 5.1 %collective-permute-start.1 = (s16[8,65536]{1,0:T(8,128)(2,1)}, s16[8,65536]{1,0:T(8,128)(2,1)}, u32[]{:S(2)}, u32[]{:S(2)}) collective-permute-start(s16[8,65536]{1,0:T(8,128)(2,1)} %get-tuple-element.9), channel_id=1, source_target_pairs={{8,0},{16,8},{24,16},{32,24},{40,32},{48,40},{56,48},{64,56},{72,6... | collective-permute-start | bytes 3145736 | tf_op jit(solution)/shard_map/ppermute | solution.py:512
  9.8 1.9 %collective-permute-start = (s16[8,65536]{1,0:T(8,128)(2,1)}, s16[8,65536]{1,0:T(8,128)(2,1)}, u32[]{:S(2)}, u32[]{:S(2)}) collective-permute-start(s16[8,65536]{1,0:T(8,128)(2,1)} %get-tuple-element.9), channel_id=1, source_target_pairs={{0,8},{8,16},{16,24},{24,32},{32,40},{40,48},{48,56},{56,64},{64,7... | collective-permute-start | bytes 3145736 | tf_op jit(solution)/shard_map/ppermute | solution.py:513
  11.7 3.4 %collective-permute-start.2 = (bf16[4,65536]{1,0:T(4,128)(2,1)}, bf16[4,65536]{1,0:T(4,128)(2,1)S(1)}, u32[]{:S(2)}, u32[]{:S(2)}) collective-permute-start(bf16[4,65536]{1,0:T(4,128)(2,1)} %get-tuple-element.10), channel_id=1, source_target_pairs={{8,0},{16,8},{24,16},{32,24},{40,32},{48,40},{56,48},{64,56},{72,6... | collective-permute-start | bytes 1572872 | tf_op jit(solution)/shard_map/ppermute | solution.py:511
  15.7 12.2 %collective-permute-done.2.edge_far = bf16[4,65536]{1,0:T(4,128)(2,1)S(1)} collective-permute-done((bf16[4,65536]{1,0:T(4,128)(2,1)}, bf16[4,65536]{1,0:T(4,128)(2,1)S(1)}, u32[]{:S(2)}, u32[]{:S(2)}) %collective-permute-start.2) | collective-permute-done | bytes 524320 | tf_op jit(solution)/shard_map/ppermute | solution.py:511
  27.9 0.0 copy-done
  27.9 10.5 %element.1 = (f32[8,65536]{1,0:T(8,128)}, f32[8,65536]{1,0:T(8,128)}) custom-call(f32[8]{0:T(128)S(1)} %copy-done, s32[1]{0:T(128)S(6)} %copy.7.assign, bf16[2,1,8,65536]{3,2,1,0:T(8,128)(2,1)} %state_far.3, bf16[2,1,8,65536]{3,2,1,0:T(8,128)(2,1)} %adjoint_far.3, bf16[4,65536]{1,0:T(4,128)(2,1)S(1)} %collective-permute-done.2.edge_far), custom_call_target="tpu_custom_call" | custom-call | flops 41943040 | bytes 8388608 | tf_op jit(solution)/shard_map/element/pallas_call | solution.py:518
  38.4 0.0 collective-permute-done.1.refs_2_
  38.4 0.0 collective-permute-done.refs_1_
  38.4 13.1 %partial.1 = s16[8,8,8320]{2,1,0:T(8,128)(2,1)} custom-call(s32[1]{0:T(128)} %bitcast.top, f32[8,65536]{1,0:T(8,128)} %refs_0_.1, s16[8,65536]{1,0:T(8,128)(2,1)} %collective-permute-done.refs_1_, s16[8,65536]{1,0:T(8,128)(2,1)} %collective-permute-done.1.refs_2_, s32[8,65536]{1,0:T(8,128)} %refs_3_.1, f32[8,65536]{1,0:T(8,128)} %get-tuple-element.11.refs_4_, ...), custom_call_target="tpu_custom_call" | custom-call | flops 78643200 | bytes 14680064 | tf_op jit(solution)/shard_map/partial/pallas_call | solution.py:534
  51.5 18.8 %all_to_all.15.coded = s16[8,8,8320]{2,1,0:T(8,128)(2,1)S(1)} all-to-all(s16[8,8,8320]{2,1,0:T(8,128)(2,1)} %partial.1), channel_id=1, replica_groups=mesh['rows'=32,'freq'=8] {'freq'}, dimensions={0} | all-to-all | bytes 2129920 | tf_op jit(solution)/shard_map/all_to_all | solution.py:553
  70.4 0.3 total.1.here
  70.7 1.9 %collective-permute-start.4 = (f32[8,8192]{1,0:T(8,128)S(1)}, f32[8,8192]{1,0:T(8,128)S(1)}, u32[]{:S(2)}, u32[]{:S(2)}) collective-permute-start(f32[8,8192]{1,0:T(8,128)S(1)} %total.1.here), channel_id=1, source_target_pairs={{8,0},{16,8},{24,16},{32,24},{40,32},{48,40},{56,48},{64,56},{72,6... | collective-permute-start | bytes 786440 | tf_op jit(solution)/shard_map/ppermute | solution.py:563
  72.6 8.1 %collective-permute-start.3 = (f32[8,8192]{1,0:T(8,128)S(1)}, f32[8,8192]{1,0:T(8,128)S(1)}, u32[]{:S(2)}, u32[]{:S(2)}) collective-permute-start(f32[8,8192]{1,0:T(8,128)S(1)} %total.1.here), channel_id=1, source_target_pairs={{0,8},{8,16},{16,24},{24,32},{32,40},{40,48},{48,56},{56,64},{64,7... | collective-permute-start | bytes 786440 | tf_op jit(solution)/shard_map/ppermute | solution.py:564
  80.8 2.2 %collective-permute-done.4.below = f32[8,8192]{1,0:T(8,128)S(1)} collective-permute-done((f32[8,8192]{1,0:T(8,128)S(1)}, f32[8,8192]{1,0:T(8,128)S(1)}, u32[]{:S(2)}, u32[]{:S(2)}) %collective-permute-start.4) | collective-permute-done | bytes 262176 | tf_op jit(solution)/shard_map/ppermute | solution.py:563
  83.0 1.1 collective-permute-done.3.above
  84.1 0.6 back.1
  84.7 16.0 %all_to_all.16.coded = s16[8,8,8576]{2,1,0:T(8,128)(2,1)S(1)} all-to-all(s16[8,8,8576]{2,1,0:T(8,128)(2,1)S(1)} %back.1), channel_id=1, replica_groups=mesh['rows'=32,'freq'=8] {'freq'}, dimensions={0} | all-to-all | bytes 2195456 | tf_op jit(solution)/shard_map/all_to_all | solution.py:577
  100.7 24.3 %all_to_all.17.squares = f32[32,8,128]{2,1,0:T(8,128)S(1)} all-to-all(f32[32,8,128]{2,1,0:T(8,128)S(1)} %squares.1), channel_id=1, replica_groups=mesh['rows'=32,'freq'=8] {'rows'}, dimensions={0} | all-to-all | bytes 262144 | tf_op jit(solution)/shard_map/all_to_all | solution.py:587
  125.0 1.6 %result.1 = f32[8,65536]{1,0:T(8,128)} custom-call(s16[8,8,8576]{2,1,0:T(8,128)(2,1)S(1)} %all_to_all.16.coded, f32[32,8,128]{2,1,0:T(8,128)S(1)} %all_to_all.17.squares), custom_call_target="tpu_custom_call" | custom-call | tf_op jit(solution)/shard_map/result/pallas_call | solution.py:589
  (1 shorter events, 0.0 us)
Async XLA Ops:
  0.0 27.9 %copy-start = (f32[8]{0:T(128)S(1)}, f32[8]{0:T(128)}, u32[]{:S(2)}) copy-start(f32[8]{0:T(128)} %omega_sq.1) | copy-start | bytes 100
  4.6 33.7 %collective-permute-start.1 = (s16[8,65536]{1,0:T(8,128)(2,1)}, s16[8,65536]{1,0:T(8,128)(2,1)}, u32[]{:S(2)}, u32[]{:S(2)}) collective-permute-start(s16[8,65536]{1,0:T(8,128)(2,1)} %get-tuple-element.9), channel_id=1, source_target_pairs={{8,0},{16,8},{24,16},{32,24},{40,32},{48,40},{56,48},{64,56},{72,6... | collective-permute-start | bytes 3145736 | tf_op jit(solution)/shard_map/ppermute | solution.py:512
  9.8 28.6 %collective-permute-start = (s16[8,65536]{1,0:T(8,128)(2,1)}, s16[8,65536]{1,0:T(8,128)(2,1)}, u32[]{:S(2)}, u32[]{:S(2)}) collective-permute-start(s16[8,65536]{1,0:T(8,128)(2,1)} %get-tuple-element.9), channel_id=1, source_target_pairs={{0,8},{8,16},{16,24},{24,32},{32,40},{40,48},{48,56},{56,64},{64,7... | collective-permute-start | bytes 3145736 | tf_op jit(solution)/shard_map/ppermute | solution.py:513
  11.7 16.2 %collective-permute-start.2 = (bf16[4,65536]{1,0:T(4,128)(2,1)}, bf16[4,65536]{1,0:T(4,128)(2,1)S(1)}, u32[]{:S(2)}, u32[]{:S(2)}) collective-permute-start(bf16[4,65536]{1,0:T(4,128)(2,1)} %get-tuple-element.10), channel_id=1, source_target_pairs={{8,0},{16,8},{24,16},{32,24},{40,32},{48,40},{56,48},{64,56},{72,6... | collective-permute-start | bytes 1572872 | tf_op jit(solution)/shard_map/ppermute | solution.py:511
  70.7 12.3 %collective-permute-start.4 = (f32[8,8192]{1,0:T(8,128)S(1)}, f32[8,8192]{1,0:T(8,128)S(1)}, u32[]{:S(2)}, u32[]{:S(2)}) collective-permute-start(f32[8,8192]{1,0:T(8,128)S(1)} %total.1.here), channel_id=1, source_target_pairs={{8,0},{16,8},{24,16},{32,24},{40,32},{48,40},{56,48},{64,56},{72,6... | collective-permute-start | bytes 786440 | tf_op jit(solution)/shard_map/ppermute | solution.py:563
  72.6 11.4 %collective-permute-start.3 = (f32[8,8192]{1,0:T(8,128)S(1)}, f32[8,8192]{1,0:T(8,128)S(1)}, u32[]{:S(2)}, u32[]{:S(2)}) collective-permute-start(f32[8,8192]{1,0:T(8,128)S(1)} %total.1.here), channel_id=1, source_target_pairs={{0,8},{8,16},{16,24},{24,32},{32,40},{40,48},{48,56},{56,64},{64,7... | collective-permute-start | bytes 786440 | tf_op jit(solution)/shard_map/ppermute | solution.py:564

commit v8 on v7

--- a/solution.py
+++ b/solution.py
@@ -188,12 +188,16 @@
     width,
     stages,
 ):
-    ids = row_ids(width)
     span = edge.shape[1] // stages
     steps = span // width
-    copies = functools.partial(
-        field_copies, (state_far, adjoint_far), (state, adjoint), arrived, span=span
-    )
+    sent = lax.broadcasted_iota(jnp.int32, (4, width), 0)
+
+    def copies(stage):
+        at = pl.ds(stage * span, span)
+        return [
+            pltpu.make_async_copy(source.at[:, :, 0:2, at], target.at[:, :, :, at], arrived.at[stage, place])
+            for place, (source, target) in enumerate(((state_far, state), (adjoint_far, adjoint)))
+        ]
 
     def load(stage):
         at = pl.ds(stage * span, span)
@@ -204,10 +208,26 @@
         return pltpu.make_async_copy(code.at[:, at], code_far.at[:, at], left.at[stage])
 
     for stage in range(stages):
+        for copy in copies(stage):
+            copy.start()
+    for stage in range(stages):
         load(stage).start()
+
     for stage in range(stages):
         for copy in copies(stage):
-            copy.start()
+            copy.wait()
+
+        def pick_rows(c, none):
+            at = cols(stage * steps + c, width)
+            fields = [state[0, 0, :, at], state[1, 0, :, at], adjoint[0, 0, :, at], adjoint[1, 0, :, at]]
+            picked = jnp.zeros((4, width), f32)
+            for place, field in enumerate(fields):
+                row = jnp.broadcast_to(field.astype(f32)[:1], picked.shape)
+                picked = jnp.where(sent == place, row, picked)
+            edge[:, at] = picked.astype(jnp.bfloat16)
+            return none
+
+        lax.fori_loop(0, steps, pick_rows, 0)
 
     for stage in range(stages):
         load(stage).wait()
@@ -219,21 +239,6 @@
 
         lax.fori_loop(0, steps, encode_rows, 0)
         save(stage).start()
-
-    for stage in range(stages):
-        for copy in copies(stage):
-            copy.wait()
-
-        def pick_rows(c, none):
-            at = cols(stage * steps + c, width)
-            first = state[0, 0, :, at].astype(f32)
-            rows = [state[1, 0, :, at], adjoint[0, 0, :, at], adjoint[1, 0, :, at]]
-            for place, row in enumerate(rows):
-                first = jnp.where(ids == place + 1, pltpu.roll(row.astype(f32), place + 1, 0), first)
-            edge[:, at] = first[:4].astype(jnp.bfloat16)
-            return none
-
-        lax.fori_loop(0, steps, pick_rows, 0)
     for stage in range(stages):
         save(stage).wait()
 
@@ -500,7 +505,10 @@
         ],
         in_specs=[in_place] * 3,
         out_specs=vmem(1) + [in_place],
-        scratch_shapes=field_scratch[:2]
+        scratch_shapes=[
+            pltpu.VMEM((2, 1, 2, width), state.dtype),
+            pltpu.VMEM((2, 1, 2, width), adjoint.dtype),
+        ]
         + design_scratch
         + [field_scratch[2]]
         + [pltpu.SemaphoreType.DMA((stages,))] * 2,
@@ -509,8 +517,8 @@
         name="prepare",
     )(state, adjoint, design)
     edge_below = lax.ppermute(edge, "rows", down)
+    code_above = lax.ppermute(code, "rows", up)
     code_below = lax.ppermute(code, "rows", down)
-    code_above = lax.ppermute(code, "rows", up)
 
     top = (lax.axis_index("rows") * slab_rows).astype(jnp.int32).reshape(1)
 

time: 127 us -> 127 us (level)
  no operation moved by 1% of the time
where the time goes in v8:
time: 127 us; the launch traced here: 126 us
  blocking collectives  59.2 us (47%)
  Pallas kernels  30.4 us (24%)
  starting transfers between devices  20.4 us (16%)
  waiting for transfers between devices  15.4 us (12%)
    all_to_all x1, blocking collectives, layer(): squares = lax.all_to_all(squares, 'rows', 0, 0, tiled=True)  24.3 us
    all_to_all x1, blocking collectives, layer(): received = lax.all_to_all(sent, 'freq', 0, 0, tiled=True)  18.8 us
    all_to_all x1, blocking collectives, layer(): pieces = lax.all_to_all(result, 'freq', 0, 0, tiled=True)  16 us
    pallas_call x1, Pallas kernels, layer(): pl.pallas_call(functools.partial(partial_kernel, stages=stages, whole_row...  13.1 us
    ppermute x1, waiting for transfers between devices, layer(): edge_below = lax.ppermute(edge, 'rows', down)  12.2 us
    pallas_call x1, Pallas kernels, layer(): pl.pallas_call(functools.partial(element_kernel, width=2048, stages=eleme...  10.5 us
    ppermute x1, starting transfers between devices, layer(): spread_above = lax.ppermute(spread, 'rows', up)  8.1 us
    ppermute x1, starting transfers between devices, layer(): code_below = lax.ppermute(code, 'rows', down)  5.11 us
  transfers between devices with their start and end apart: 5, of which 3 were waited for; matrix products, arithmetic and copies ran while one was open for 0% of the time, Pallas kernels for 8%

profile of v8, /device:TPU:1, one launch (start us, length us, event | category | flops | bytes accessed | tf_op | source)
XLA Modules:
  0.0 126.2 jit_solution(4947742416364364709)
XLA Ops:
  0.0 0.0 copy-start
  0.0 4.2 %prepare.1 = (bf16[4,65536]{1,0:T(4,128)(2,1)}, s16[8,65536]{1,0:T(8,128)(2,1)}) custom-call(bf16[2,1,8,65536]{3,2,1,0:T(8,128)(2,1)} %state_far.3, bf16[2,1,8,65536]{3,2,1,0:T(8,128)(2,1)} %adjoint_far.3, f32[8,65536]{1,0:T(8,128)} %refs_0_.1), custom_call_target="tpu_custom_call" | custom-call | flops 4194304 | bytes 7340032 | tf_op jit(solution)/shard_map/prepare/pallas_call | solution.py:500
  4.2 5.1 %collective-permute-start.1 = (s16[8,65536]{1,0:T(8,128)(2,1)}, s16[8,65536]{1,0:T(8,128)(2,1)}, u32[]{:S(2)}, u32[]{:S(2)}) collective-permute-start(s16[8,65536]{1,0:T(8,128)(2,1)} %get-tuple-element.9), channel_id=1, source_target_pairs={{8,0},{16,8},{24,16},{32,24},{40,32},{48,40},{56,48},{64,56},{72,6... | collective-permute-start | bytes 3145736 | tf_op jit(solution)/shard_map/ppermute | solution.py:521
  9.3 1.9 %collective-permute-start = (s16[8,65536]{1,0:T(8,128)(2,1)}, s16[8,65536]{1,0:T(8,128)(2,1)}, u32[]{:S(2)}, u32[]{:S(2)}) collective-permute-start(s16[8,65536]{1,0:T(8,128)(2,1)} %get-tuple-element.9), channel_id=1, source_target_pairs={{0,8},{8,16},{16,24},{24,32},{32,40},{40,48},{48,56},{56,64},{64,7... | collective-permute-start | bytes 3145736 | tf_op jit(solution)/shard_map/ppermute | solution.py:520
  11.3 3.4 %collective-permute-start.2 = (bf16[4,65536]{1,0:T(4,128)(2,1)}, bf16[4,65536]{1,0:T(4,128)(2,1)S(1)}, u32[]{:S(2)}, u32[]{:S(2)}) collective-permute-start(bf16[4,65536]{1,0:T(4,128)(2,1)} %get-tuple-element.10), channel_id=1, source_target_pairs={{8,0},{16,8},{24,16},{32,24},{40,32},{48,40},{56,48},{64,56},{72,6... | collective-permute-start | bytes 1572872 | tf_op jit(solution)/shard_map/ppermute | solution.py:519
  15.3 12.2 %collective-permute-done.2.edge_far = bf16[4,65536]{1,0:T(4,128)(2,1)S(1)} collective-permute-done((bf16[4,65536]{1,0:T(4,128)(2,1)}, bf16[4,65536]{1,0:T(4,128)(2,1)S(1)}, u32[]{:S(2)}, u32[]{:S(2)}) %collective-permute-start.2) | collective-permute-done | bytes 524320 | tf_op jit(solution)/shard_map/ppermute | solution.py:519
  27.4 0.0 copy-done
  27.4 10.5 %element.1 = (f32[8,65536]{1,0:T(8,128)}, f32[8,65536]{1,0:T(8,128)}) custom-call(f32[8]{0:T(128)S(1)} %copy-done, s32[1]{0:T(128)S(6)} %copy.7.assign, bf16[2,1,8,65536]{3,2,1,0:T(8,128)(2,1)} %state_far.3, bf16[2,1,8,65536]{3,2,1,0:T(8,128)(2,1)} %adjoint_far.3, bf16[4,65536]{1,0:T(4,128)(2,1)S(1)} %collective-permute-done.2.edge_far), custom_call_target="tpu_custom_call" | custom-call | flops 41943040 | bytes 8388608 | tf_op jit(solution)/shard_map/element/pallas_call | solution.py:526
  37.9 0.0 collective-permute-done.1.refs_2_
  38.0 0.0 collective-permute-done.refs_1_
  38.0 13.1 %partial.1 = s16[8,8,8320]{2,1,0:T(8,128)(2,1)} custom-call(s32[1]{0:T(128)} %bitcast.top, f32[8,65536]{1,0:T(8,128)} %refs_0_.1, s16[8,65536]{1,0:T(8,128)(2,1)} %collective-permute-done.refs_1_, s16[8,65536]{1,0:T(8,128)(2,1)} %collective-permute-done.1.refs_2_, s32[8,65536]{1,0:T(8,128)} %refs_3_.1, f32[8,65536]{1,0:T(8,128)} %get-tuple-element.11.refs_4_, ...), custom_call_target="tpu_custom_call" | custom-call | flops 78643200 | bytes 14680064 | tf_op jit(solution)/shard_map/partial/pallas_call | solution.py:542
  51.1 18.8 %all_to_all.15.coded = s16[8,8,8320]{2,1,0:T(8,128)(2,1)S(1)} all-to-all(s16[8,8,8320]{2,1,0:T(8,128)(2,1)} %partial.1), channel_id=1, replica_groups=mesh['rows'=32,'freq'=8] {'freq'}, dimensions={0} | all-to-all | bytes 2129920 | tf_op jit(solution)/shard_map/all_to_all | solution.py:561
  69.9 0.3 total.1.here
  70.3 1.9 %collective-permute-start.4 = (f32[8,8192]{1,0:T(8,128)S(1)}, f32[8,8192]{1,0:T(8,128)S(1)}, u32[]{:S(2)}, u32[]{:S(2)}) collective-permute-start(f32[8,8192]{1,0:T(8,128)S(1)} %total.1.here), channel_id=1, source_target_pairs={{8,0},{16,8},{24,16},{32,24},{40,32},{48,40},{56,48},{64,56},{72,6... | collective-permute-start | bytes 786440 | tf_op jit(solution)/shard_map/ppermute | solution.py:571
  72.2 8.1 %collective-permute-start.3 = (f32[8,8192]{1,0:T(8,128)S(1)}, f32[8,8192]{1,0:T(8,128)S(1)}, u32[]{:S(2)}, u32[]{:S(2)}) collective-permute-start(f32[8,8192]{1,0:T(8,128)S(1)} %total.1.here), channel_id=1, source_target_pairs={{0,8},{8,16},{16,24},{24,32},{32,40},{40,48},{48,56},{56,64},{64,7... | collective-permute-start | bytes 786440 | tf_op jit(solution)/shard_map/ppermute | solution.py:572
  80.3 2.2 %collective-permute-done.4.below = f32[8,8192]{1,0:T(8,128)S(1)} collective-permute-done((f32[8,8192]{1,0:T(8,128)S(1)}, f32[8,8192]{1,0:T(8,128)S(1)}, u32[]{:S(2)}, u32[]{:S(2)}) %collective-permute-start.4) | collective-permute-done | bytes 262176 | tf_op jit(solution)/shard_map/ppermute | solution.py:571
  82.5 1.1 collective-permute-done.3.above
  83.6 0.6 back.1
  84.3 16.0 %all_to_all.16.coded = s16[8,8,8576]{2,1,0:T(8,128)(2,1)S(1)} all-to-all(s16[8,8,8576]{2,1,0:T(8,128)(2,1)S(1)} %back.1), channel_id=1, replica_groups=mesh['rows'=32,'freq'=8] {'freq'}, dimensions={0} | all-to-all | bytes 2195456 | tf_op jit(solution)/shard_map/all_to_all | solution.py:585
  100.3 24.3 %all_to_all.17.squares = f32[32,8,128]{2,1,0:T(8,128)S(1)} all-to-all(f32[32,8,128]{2,1,0:T(8,128)S(1)} %squares.1), channel_id=1, replica_groups=mesh['rows'=32,'freq'=8] {'rows'}, dimensions={0} | all-to-all | bytes 262144 | tf_op jit(solution)/shard_map/all_to_all | solution.py:595
  124.6 1.6 %result.1 = f32[8,65536]{1,0:T(8,128)} custom-call(s16[8,8,8576]{2,1,0:T(8,128)(2,1)S(1)} %all_to_all.16.coded, f32[32,8,128]{2,1,0:T(8,128)S(1)} %all_to_all.17.squares), custom_call_target="tpu_custom_call" | custom-call | tf_op jit(solution)/shard_map/result/pallas_call | solution.py:597
  (1 shorter events, 0.0 us)
Async XLA Ops:
  0.0 27.4 %copy-start = (f32[8]{0:T(128)S(1)}, f32[8]{0:T(128)}, u32[]{:S(2)}) copy-start(f32[8]{0:T(128)} %omega_sq.1) | copy-start | bytes 100
  4.2 33.7 %collective-permute-start.1 = (s16[8,65536]{1,0:T(8,128)(2,1)}, s16[8,65536]{1,0:T(8,128)(2,1)}, u32[]{:S(2)}, u32[]{:S(2)}) collective-permute-start(s16[8,65536]{1,0:T(8,128)(2,1)} %get-tuple-element.9), channel_id=1, source_target_pairs={{8,0},{16,8},{24,16},{32,24},{40,32},{48,40},{56,48},{64,56},{72,6... | collective-permute-start | bytes 3145736 | tf_op jit(solution)/shard_map/ppermute | solution.py:521
  9.3 28.6 %collective-permute-start = (s16[8,65536]{1,0:T(8,128)(2,1)}, s16[8,65536]{1,0:T(8,128)(2,1)}, u32[]{:S(2)}, u32[]{:S(2)}) collective-permute-start(s16[8,65536]{1,0:T(8,128)(2,1)} %get-tuple-element.9), channel_id=1, source_target_pairs={{0,8},{8,16},{16,24},{24,32},{32,40},{40,48},{48,56},{56,64},{64,7... | collective-permute-start | bytes 3145736 | tf_op jit(solution)/shard_map/ppermute | solution.py:520
  11.3 16.2 %collective-permute-start.2 = (bf16[4,65536]{1,0:T(4,128)(2,1)}, bf16[4,65536]{1,0:T(4,128)(2,1)S(1)}, u32[]{:S(2)}, u32[]{:S(2)}) collective-permute-start(bf16[4,65536]{1,0:T(4,128)(2,1)} %get-tuple-element.10), channel_id=1, source_target_pairs={{8,0},{16,8},{24,16},{32,24},{40,32},{48,40},{56,48},{64,56},{72,6... | collective-permute-start | bytes 1572872 | tf_op jit(solution)/shard_map/ppermute | solution.py:519
  70.3 12.3 %collective-permute-start.4 = (f32[8,8192]{1,0:T(8,128)S(1)}, f32[8,8192]{1,0:T(8,128)S(1)}, u32[]{:S(2)}, u32[]{:S(2)}) collective-permute-start(f32[8,8192]{1,0:T(8,128)S(1)} %total.1.here), channel_id=1, source_target_pairs={{8,0},{16,8},{24,16},{32,24},{40,32},{48,40},{56,48},{64,56},{72,6... | collective-permute-start | bytes 786440 | tf_op jit(solution)/shard_map/ppermute | solution.py:571
  72.2 11.4 %collective-permute-start.3 = (f32[8,8192]{1,0:T(8,128)S(1)}, f32[8,8192]{1,0:T(8,128)S(1)}, u32[]{:S(2)}, u32[]{:S(2)}) collective-permute-start(f32[8,8192]{1,0:T(8,128)S(1)} %total.1.here), channel_id=1, source_target_pairs={{0,8},{8,16},{16,24},{24,32},{32,40},{40,48},{48,56},{56,64},{64,7... | collective-permute-start | bytes 786440 | tf_op jit(solution)/shard_map/ppermute | solution.py:572

commit v9 on v6

--- a/solution.py
+++ b/solution.py
@@ -172,33 +172,40 @@
 
 
 def edge_kernel(state_far, adjoint_far, edge, state, adjoint, arrived, *, width, stages):
-    ids = row_ids(width)
     span = edge.shape[1] // stages
-    copies = functools.partial(
-        field_copies, (state_far, adjoint_far), (state, adjoint), arrived, span=span
-    )
+    steps = span // width
+    sent = lax.broadcasted_iota(jnp.int32, (4, width), 0)
+
+    def copies(stage):
+        at = pl.ds(stage * span, span)
+        return [
+            pltpu.make_async_copy(source.at[:, :, 0:2, at], target.at[:, :, :, at], arrived.at[stage, place])
+            for place, (source, target) in enumerate(((state_far, state), (adjoint_far, adjoint)))
+        ]
+
     for stage in range(stages):
         for copy in copies(stage):
             copy.start()
-
     for stage in range(stages):
         for copy in copies(stage):
             copy.wait()
 
-        def step(c, none):
-            at = cols(stage * (span // width) + c, width)
-            first = state[0, 0, :, at].astype(f32)
-            rows = [state[1, 0, :, at], adjoint[0, 0, :, at], adjoint[1, 0, :, at]]
-            for place, row in enumerate(rows):
-                first = jnp.where(ids == place + 1, pltpu.roll(row.astype(f32), place + 1, 0), first)
-            edge[:, at] = first[:4].astype(jnp.bfloat16)
+        def pick_rows(c, none):
+            at = cols(stage * steps + c, width)
+            fields = [state[0, 0, :, at], state[1, 0, :, at], adjoint[0, 0, :, at], adjoint[1, 0, :, at]]
+            picked = jnp.zeros((4, width), f32)
+            for place, field in enumerate(fields):
+                row = jnp.broadcast_to(field.astype(f32)[:1], picked.shape)
+                picked = jnp.where(sent == place, row, picked)
+            edge[:, at] = picked.astype(jnp.bfloat16)
             return none
 
-        lax.fori_loop(0, span // width, step, 0)
+        lax.fori_loop(0, steps, pick_rows, 0)
 
 
 def code_kernel(design_far, code_far, design, code, arrived, left, *, width, stages):
     span = design.shape[1] // stages
+    steps = span // width
 
     def load(stage):
         at = pl.ds(stage * span, span)
@@ -213,12 +220,12 @@
     for stage in range(stages):
         load(stage).wait()
 
-        def step(c, none):
-            at = cols(stage * (span // width) + c, width)
+        def encode_rows(c, none):
+            at = cols(stage * steps + c, width)
             code[:, at] = to_i16(design[:, at] * DESIGN_STEPS)
             return none
 
-        lax.fori_loop(0, span // width, step, 0)
+        lax.fori_loop(0, steps, encode_rows, 0)
         save(stage).start()
     for stage in range(stages):
         save(stage).wait()
@@ -386,30 +393,36 @@
         pltpu.make_async_copy(out.at[peer], out_far.at[peer], left.at[peer]).wait()
 
 
-def sum_kernel(coded, out, *, width):
+def sum_kernel(coded, out, sent, *, width):
     peers, piece = coded.shape[0], out.shape[1]
     scales = [wide(decode_scale(coded[peer, :, piece:]), width) for peer in range(peers)]
 
-    def step(c, none):
+    def step(c, largest):
         at = cols(c, width)
         total = None
         for peer in range(peers):
             term = coded[peer, :, at].astype(jnp.int32).astype(f32) * scales[peer]
             total = term if total is None else total + term
         out[:, at] = total
-        return none
-
-    lax.fori_loop(0, piece // width, step, 0)
+        return jnp.maximum(largest, folded_max(total))
+
+    largest = lax.fori_loop(0, piece // width, step, jnp.zeros((8, LANES), f32))
+    encode(out, largest, [sent], width)
 
 
 def back_kernel(above, here, below, out, blocks, *, width):
     piece = here.shape[1]
     zeros = jnp.zeros((8, LANES), f32)
+    above_scale, below_scale = (
+        wide(decode_scale(ref[:, piece:]), width) for ref in (above, below)
+    )
 
     def step(c, carry):
         largest, squares = carry
         at = cols(c, width)
-        block = row_filter(above[:, at], here[:, at], below[:, at])
+        upper = above[:, at].astype(jnp.int32).astype(f32) * above_scale
+        lower = below[:, at].astype(jnp.int32).astype(f32) * below_scale
+        block = row_filter(upper, here[:, at], lower)
         blocks[:, at] = block
         return jnp.maximum(largest, folded_max(block)), squares + folded(block * block, jnp.add)
 
@@ -468,6 +481,7 @@
 
     in_place = pl.BlockSpec(memory_space=pltpu.HBM)
     stages = 4
+    element_stages = 8
     field_scratch = [
         pltpu.VMEM(state.shape, state.dtype),
         pltpu.VMEM(adjoint.shape, adjoint.dtype),
@@ -476,11 +490,15 @@
     edge = pl.pallas_call(
         functools.partial(edge_kernel, width=2048, stages=stages),
         out_shape=jax.ShapeDtypeStruct((4, width), jnp.bfloat16),
-        in_specs=[in_place, in_place],
+        in_specs=[in_place] * 2,
         out_specs=vmem(1)[0],
-        scratch_shapes=field_scratch,
+        scratch_shapes=[
+            pltpu.VMEM((2, 1, 2, width), state.dtype),
+            pltpu.VMEM((2, 1, 2, width), adjoint.dtype),
+            field_scratch[2],
+        ],
         compiler_params=params(63),
-        cost_estimate=cost(8 * slab_rows * width, 4 * 1024 * 1024),
+        cost_estimate=cost(4 * slab_rows * width, 2 * 1024 * 1024),
         name="edge",
     )(state, adjoint)
     edge_below = lax.ppermute(edge, "rows", down)
@@ -492,28 +510,27 @@
         scratch_shapes=[
             pltpu.VMEM((slab_rows, width), f32),
             pltpu.VMEM((slab_rows, width), i16),
-            pltpu.SemaphoreType.DMA((stages,)),
-            pltpu.SemaphoreType.DMA((stages,)),
-        ],
+        ]
+        + [pltpu.SemaphoreType.DMA((stages,))] * 2,
         compiler_params=params(63),
         name="code",
     )(design)
+    code_above = lax.ppermute(code, "rows", up)
     code_below = lax.ppermute(code, "rows", down)
-    code_above = lax.ppermute(code, "rows", up)
 
     top = (lax.axis_index("rows") * slab_rows).astype(jnp.int32).reshape(1)
 
     slab = jax.ShapeDtypeStruct((slab_rows, width), f32)
     elastic, inertia = pl.pallas_call(
-        functools.partial(element_kernel, width=2048, stages=stages),
+        functools.partial(element_kernel, width=2048, stages=element_stages),
         out_shape=[slab, slab],
         in_specs=[smem, smem] + [in_place] * 3,
         out_specs=[in_place, in_place],
         scratch_shapes=field_scratch[:2]
         + [pltpu.VMEM(edge.shape, edge.dtype)]
         + [pltpu.VMEM((slab_rows, width), f32)] * 2
-        + [pltpu.SemaphoreType.DMA((stages, 3)), pltpu.SemaphoreType.DMA((stages, 2))],
-        compiler_params=params(63),
+        + [pltpu.SemaphoreType.DMA((element_stages, count)) for count in (3, 2)],
+        compiler_params=params(53),
         cost_estimate=cost(80 * slab_rows * width, 8 * 1024 * 1024),
         name="element",
     )(omega_sq, assign, state, adjoint, edge_below)
@@ -541,16 +558,19 @@
 
     received = lax.all_to_all(sent, "freq", 0, 0, tiled=True)
 
-    spread = pl.pallas_call(
+    spread, sent = pl.pallas_call(
         functools.partial(sum_kernel, width=1024),
-        out_shape=jax.ShapeDtypeStruct((slab_rows, piece), f32),
+        out_shape=[
+            jax.ShapeDtypeStruct((slab_rows, piece), f32),
+            jax.ShapeDtypeStruct((slab_rows, piece + LANES), i16),
+        ],
         in_specs=vmem(1),
-        out_specs=vmem(1)[0],
+        out_specs=vmem(2),
         compiler_params=params(8),
         name="total",
     )(received)
-    spread_below = lax.ppermute(spread, "rows", down)
-    spread_above = lax.ppermute(spread, "rows", up)
+    spread_below = lax.ppermute(sent, "rows", down)
+    spread_above = lax.ppermute(sent, "rows", up)
 
     wide_coded = jax.ShapeDtypeStruct((peers, slab_rows, piece + 3 * LANES), i16)
     result = pl.pallas_call(

time: 126 us -> 124 us (0.984)
    ppermute x2, waiting for transfers between devices: 3.29 us -> 1.94 us  [the longest x1 1.21 us: layer(): spread_above = lax.ppermute(sent, 'rows', up)]
where the time goes in v9:
time: 124 us; the launch traced here: 123 us
  blocking collectives  59.1 us (48%)
  Pallas kernels  31.8 us (26%)
  starting transfers between devices  20.4 us (16%)
  waiting for transfers between devices  11 us (9%)
    all_to_all x1, blocking collectives, layer(): squares = lax.all_to_all(squares, 'rows', 0, 0, tiled=True)  24.5 us
    all_to_all x1, blocking collectives, layer(): received = lax.all_to_all(sent, 'freq', 0, 0, tiled=True)  18.8 us
    all_to_all x1, blocking collectives, layer(): pieces = lax.all_to_all(result, 'freq', 0, 0, tiled=True)  15.8 us
    pallas_call x1, Pallas kernels, layer(): pl.pallas_call(functools.partial(partial_kernel, stages=stages, whole_row...  13.1 us
    pallas_call x1, Pallas kernels, layer(): pl.pallas_call(functools.partial(element_kernel, width=2048, stages=eleme...  10.5 us
    ppermute x1, waiting for transfers between devices, layer(): edge_below = lax.ppermute(edge, 'rows', down)  9.08 us
    ppermute x1, starting transfers between devices, layer(): spread_above = lax.ppermute(sent, 'rows', up)  8.1 us
    ppermute x1, starting transfers between devices, layer(): code_below = lax.ppermute(code, 'rows', down)  5.11 us
  transfers between devices with their start and end apart: 5, of which 3 were waited for; matrix products, arithmetic and copies ran while one was open for 0% of the time, Pallas kernels for 11%

profile of v9, /device:TPU:1, one launch (start us, length us, event | category | flops | bytes accessed | tf_op | source)
XLA Modules:
  0.0 123.1 jit_solution(10789174683582402620)
XLA Ops:
  0.0 2.4 %code.1 = s16[8,65536]{1,0:T(8,128)(2,1)} custom-call(f32[8,65536]{1,0:T(8,128)} %refs_0_.1), custom_call_target="tpu_custom_call" | custom-call | tf_op jit(solution)/shard_map/code/pallas_call | solution.py:505
  2.4 0.0 copy-start
  2.4 5.1 %collective-permute-start.1 = (s16[8,65536]{1,0:T(8,128)(2,1)}, s16[8,65536]{1,0:T(8,128)(2,1)}, u32[]{:S(2)}, u32[]{:S(2)}) collective-permute-start(s16[8,65536]{1,0:T(8,128)(2,1)} %code.1), channel_id=1, source_target_pairs={{8,0},{16,8},{24,16},{32,24},{40,32},{48,40},{56,48},{64,56},{72,6... | collective-permute-start | bytes 3145736 | tf_op jit(solution)/shard_map/ppermute | solution.py:519
  7.5 1.9 %collective-permute-start = (s16[8,65536]{1,0:T(8,128)(2,1)}, s16[8,65536]{1,0:T(8,128)(2,1)}, u32[]{:S(2)}, u32[]{:S(2)}) collective-permute-start(s16[8,65536]{1,0:T(8,128)(2,1)} %code.1), channel_id=1, source_target_pairs={{0,8},{8,16},{16,24},{24,32},{32,40},{40,48},{48,56},{56,64},{64,7... | collective-permute-start | bytes 3145736 | tf_op jit(solution)/shard_map/ppermute | solution.py:518
  9.4 3.1 %edge.1 = bf16[4,65536]{1,0:T(4,128)(2,1)} custom-call(bf16[2,1,8,65536]{3,2,1,0:T(8,128)(2,1)} %state_far.3, bf16[2,1,8,65536]{3,2,1,0:T(8,128)(2,1)} %adjoint_far.3), custom_call_target="tpu_custom_call" | custom-call | flops 2097152 | bytes 2097152 | tf_op jit(solution)/shard_map/edge/pallas_call | solution.py:490
  12.5 3.4 %collective-permute-start.2 = (bf16[4,65536]{1,0:T(4,128)(2,1)}, bf16[4,65536]{1,0:T(4,128)(2,1)S(1)}, u32[]{:S(2)}, u32[]{:S(2)}) collective-permute-start(bf16[4,65536]{1,0:T(4,128)(2,1)} %edge.1), channel_id=1, source_target_pairs={{8,0},{16,8},{24,16},{32,24},{40,32},{48,40},{56,48},{64,56},{72,6... | collective-permute-start | bytes 1572872 | tf_op jit(solution)/shard_map/ppermute | solution.py:504
  16.5 9.1 %collective-permute-done.2.edge_far = bf16[4,65536]{1,0:T(4,128)(2,1)S(1)} collective-permute-done((bf16[4,65536]{1,0:T(4,128)(2,1)}, bf16[4,65536]{1,0:T(4,128)(2,1)S(1)}, u32[]{:S(2)}, u32[]{:S(2)}) %collective-permute-start.2) | collective-permute-done | bytes 524320 | tf_op jit(solution)/shard_map/ppermute | solution.py:504
  25.6 0.0 copy-done
  25.6 10.5 %element.1 = (f32[8,65536]{1,0:T(8,128)}, f32[8,65536]{1,0:T(8,128)}) custom-call(f32[8]{0:T(128)S(1)} %copy-done, s32[1]{0:T(128)S(6)} %copy.7.assign, bf16[2,1,8,65536]{3,2,1,0:T(8,128)(2,1)} %state_far.3, bf16[2,1,8,65536]{3,2,1,0:T(8,128)(2,1)} %adjoint_far.3, bf16[4,65536]{1,0:T(4,128)(2,1)S(1)} %collective-permute-done.2.edge_far), custom_call_target="tpu_custom_call" | custom-call | flops 41943040 | bytes 8388608 | tf_op jit(solution)/shard_map/element/pallas_call | solution.py:524
  36.1 0.0 collective-permute-done.1.refs_2_
  36.1 0.0 collective-permute-done.refs_1_
  36.1 13.1 %partial.1 = s16[8,8,8320]{2,1,0:T(8,128)(2,1)} custom-call(s32[1]{0:T(128)} %bitcast.top, f32[8,65536]{1,0:T(8,128)} %refs_0_.1, s16[8,65536]{1,0:T(8,128)(2,1)} %collective-permute-done.refs_1_, s16[8,65536]{1,0:T(8,128)(2,1)} %collective-permute-done.1.refs_2_, s32[8,65536]{1,0:T(8,128)} %refs_3_.1, f32[8,65536]{1,0:T(8,128)} %get-tuple-element.9.refs_4_, ...), custom_call_target="tpu_custom_call" | custom-call | flops 78643200 | bytes 14680064 | tf_op jit(solution)/shard_map/partial/pallas_call | solution.py:540
  49.3 18.8 %all_to_all.15.coded = s16[8,8,8320]{2,1,0:T(8,128)(2,1)S(1)} all-to-all(s16[8,8,8320]{2,1,0:T(8,128)(2,1)} %partial.1), channel_id=1, replica_groups=mesh['rows'=32,'freq'=8] {'freq'}, dimensions={0} | all-to-all | bytes 2129920 | tf_op jit(solution)/shard_map/all_to_all | solution.py:559
  68.1 0.4 total.1
  68.5 1.9 %collective-permute-start.4 = (s16[8,8320]{1,0:T(8,128)(2,1)S(1)}, s16[8,8320]{1,0:T(8,128)(2,1)S(1)}, u32[]{:S(2)}, u32[]{:S(2)}) collective-permute-start(s16[8,8320]{1,0:T(8,128)(2,1)S(1)} %get-tuple-element.11), channel_id=1, source_target_pairs={{8,0},{16,8},{24,16},{32,24},{40,32},{48,40},{56,48},{64,56},{72,6... | collective-permute-start | bytes 399368 | tf_op jit(solution)/shard_map/ppermute | solution.py:572
  70.5 8.1 %collective-permute-start.3 = (s16[8,8320]{1,0:T(8,128)(2,1)S(1)}, s16[8,8320]{1,0:T(8,128)(2,1)S(1)}, u32[]{:S(2)}, u32[]{:S(2)}) collective-permute-start(s16[8,8320]{1,0:T(8,128)(2,1)S(1)} %get-tuple-element.11), channel_id=1, source_target_pairs={{0,8},{8,16},{16,24},{24,32},{32,40},{40,48},{48,56},{56,64},{64,7... | collective-permute-start | bytes 399368 | tf_op jit(solution)/shard_map/ppermute | solution.py:573
  78.6 0.7 collective-permute-done.4.below
  79.3 1.2 collective-permute-done.3.above
  80.5 0.7 back.1
  81.2 15.8 %all_to_all.16.coded = s16[8,8,8576]{2,1,0:T(8,128)(2,1)S(1)} all-to-all(s16[8,8,8576]{2,1,0:T(8,128)(2,1)S(1)} %back.1), channel_id=1, replica_groups=mesh['rows'=32,'freq'=8] {'freq'}, dimensions={0} | all-to-all | bytes 2195456 | tf_op jit(solution)/shard_map/all_to_all | solution.py:586
  97.0 24.5 %all_to_all.17.squares = f32[32,8,128]{2,1,0:T(8,128)S(1)} all-to-all(f32[32,8,128]{2,1,0:T(8,128)S(1)} %squares.1), channel_id=1, replica_groups=mesh['rows'=32,'freq'=8] {'rows'}, dimensions={0} | all-to-all | bytes 262144 | tf_op jit(solution)/shard_map/all_to_all | solution.py:596
  121.5 1.6 %result.1 = f32[8,65536]{1,0:T(8,128)} custom-call(s16[8,8,8576]{2,1,0:T(8,128)(2,1)S(1)} %all_to_all.16.coded, f32[32,8,128]{2,1,0:T(8,128)S(1)} %all_to_all.17.squares), custom_call_target="tpu_custom_call" | custom-call | tf_op jit(solution)/shard_map/result/pallas_call | solution.py:598
  (1 shorter events, 0.0 us)
Async XLA Ops:
  2.4 23.2 %copy-start = (f32[8]{0:T(128)S(1)}, f32[8]{0:T(128)}, u32[]{:S(2)}) copy-start(f32[8]{0:T(128)} %omega_sq.1) | copy-start | bytes 100
  2.4 33.7 %collective-permute-start.1 = (s16[8,65536]{1,0:T(8,128)(2,1)}, s16[8,65536]{1,0:T(8,128)(2,1)}, u32[]{:S(2)}, u32[]{:S(2)}) collective-permute-start(s16[8,65536]{1,0:T(8,128)(2,1)} %code.1), channel_id=1, source_target_pairs={{8,0},{16,8},{24,16},{32,24},{40,32},{48,40},{56,48},{64,56},{72,6... | collective-permute-start | bytes 3145736 | tf_op jit(solution)/shard_map/ppermute | solution.py:519
  7.5 28.6 %collective-permute-start = (s16[8,65536]{1,0:T(8,128)(2,1)}, s16[8,65536]{1,0:T(8,128)(2,1)}, u32[]{:S(2)}, u32[]{:S(2)}) collective-permute-start(s16[8,65536]{1,0:T(8,128)(2,1)} %code.1), channel_id=1, source_target_pairs={{0,8},{8,16},{16,24},{24,32},{32,40},{40,48},{48,56},{56,64},{64,7... | collective-permute-start | bytes 3145736 | tf_op jit(solution)/shard_map/ppermute | solution.py:518
  12.5 13.1 %collective-permute-start.2 = (bf16[4,65536]{1,0:T(4,128)(2,1)}, bf16[4,65536]{1,0:T(4,128)(2,1)S(1)}, u32[]{:S(2)}, u32[]{:S(2)}) collective-permute-start(bf16[4,65536]{1,0:T(4,128)(2,1)} %edge.1), channel_id=1, source_target_pairs={{8,0},{16,8},{24,16},{32,24},{40,32},{48,40},{56,48},{64,56},{72,6... | collective-permute-start | bytes 1572872 | tf_op jit(solution)/shard_map/ppermute | solution.py:504
  68.5 10.8 %collective-permute-start.4 = (s16[8,8320]{1,0:T(8,128)(2,1)S(1)}, s16[8,8320]{1,0:T(8,128)(2,1)S(1)}, u32[]{:S(2)}, u32[]{:S(2)}) collective-permute-start(s16[8,8320]{1,0:T(8,128)(2,1)S(1)} %get-tuple-element.11), channel_id=1, source_target_pairs={{8,0},{16,8},{24,16},{32,24},{40,32},{48,40},{56,48},{64,56},{72,6... | collective-permute-start | bytes 399368 | tf_op jit(solution)/shard_map/ppermute | solution.py:572
  70.5 10.1 %collective-permute-start.3 = (s16[8,8320]{1,0:T(8,128)(2,1)S(1)}, s16[8,8320]{1,0:T(8,128)(2,1)S(1)}, u32[]{:S(2)}, u32[]{:S(2)}) collective-permute-start(s16[8,8320]{1,0:T(8,128)(2,1)S(1)} %get-tuple-element.11), channel_id=1, source_target_pairs={{0,8},{8,16},{16,24},{24,32},{32,40},{40,48},{48,56},{56,64},{64,7... | collective-permute-start | bytes 399368 | tf_op jit(solution)/shard_map/ppermute | solution.py:573

commit v10 on v7

--- a/solution.py
+++ b/solution.py
@@ -340,12 +340,19 @@
             for k in range(3)
         ]
 
-    late = [pltpu.make_async_copy(sources[k], kept[k], arrived.at[0, k]) for k in range(3, 6)]
+    def late(stage):
+        at = cols(stage, span)
+        return [
+            pltpu.make_async_copy(sources[k].at[:, at], kept[k].at[:, at], arrived.at[stage, k])
+            for k in range(3, 6)
+        ]
+
     for stage in range(stages):
         for copy in early(stage):
             copy.start()
-    for copy in late:
-        copy.start()
+    for stage in range(stages):
+        for copy in late(stage):
+            copy.start()
     clear_ends(rowed)
     clear_ends(spread)
 
@@ -361,8 +368,6 @@
             copy.wait()
         first = stage * (span // narrow)
         lax.fori_loop(first, first + span // narrow, filter_rows, 0)
-    for copy in late:
-        copy.wait()
 
     taps = band()
     row = top[0] + row_ids(LANES)
@@ -374,6 +379,8 @@
 
     def scale(c, none):
         at = cols(c, piece)
+        for copy in late(c):
+            copy.wait()
         first = inside * jnp.where(c == 0, left_end, 1.0)
         last = inside * jnp.where(c == peers - 1, right_end, 1.0)
         weights = jnp.concatenate([first] + [inside] * (piece // LANES - 2) + [last], axis=1)
@@ -400,30 +407,36 @@
         pltpu.make_async_copy(out.at[peer], out_far.at[peer], left.at[peer]).wait()
 
 
-def sum_kernel(coded, out, *, width):
+def sum_kernel(coded, out, sent, *, width):
     peers, piece = coded.shape[0], out.shape[1]
     scales = [wide(decode_scale(coded[peer, :, piece:]), width) for peer in range(peers)]
 
-    def step(c, none):
+    def step(c, largest):
         at = cols(c, width)
         total = None
         for peer in range(peers):
             term = coded[peer, :, at].astype(jnp.int32).astype(f32) * scales[peer]
             total = term if total is None else total + term
         out[:, at] = total
-        return none
-
-    lax.fori_loop(0, piece // width, step, 0)
+        return jnp.maximum(largest, folded_max(total))
+
+    largest = lax.fori_loop(0, piece // width, step, jnp.zeros((8, LANES), f32))
+    encode(out, largest, [sent], width)
 
 
 def back_kernel(above, here, below, out, blocks, *, width):
     piece = here.shape[1]
     zeros = jnp.zeros((8, LANES), f32)
+    above_scale, below_scale = (
+        wide(decode_scale(ref[:, piece:]), width) for ref in (above, below)
+    )
 
     def step(c, carry):
         largest, squares = carry
         at = cols(c, width)
-        block = row_filter(above[:, at], here[:, at], below[:, at])
+        upper = above[:, at].astype(jnp.int32).astype(f32) * above_scale
+        lower = below[:, at].astype(jnp.int32).astype(f32) * below_scale
+        block = row_filter(upper, here[:, at], lower)
         blocks[:, at] = block
         return jnp.maximum(largest, folded_max(block)), squares + folded(block * block, jnp.add)
 
@@ -532,7 +545,7 @@
     coded = jax.ShapeDtypeStruct((peers, slab_rows, piece + LANES), i16)
     operands = (design, code_above, code_below, passive, elastic, inertia)
     sent = pl.pallas_call(
-        functools.partial(partial_kernel, stages=stages, whole_rows=whole_rows),
+        functools.partial(partial_kernel, stages=peers, whole_rows=whole_rows),
         out_shape=coded,
         in_specs=[smem] + [in_place] * len(operands),
         out_specs=in_place,
@@ -542,7 +555,7 @@
             pltpu.VMEM((slab_rows, width + 2 * LANES), f32),
             pltpu.VMEM((slab_rows, piece), f32),
             pltpu.VMEM(coded.shape, coded.dtype),
-            pltpu.SemaphoreType.DMA((stages, len(operands))),
+            pltpu.SemaphoreType.DMA((peers, len(operands))),
             pltpu.SemaphoreType.DMA((peers,)),
         ],
         compiler_params=params(63),
@@ -552,16 +565,19 @@
 
     received = lax.all_to_all(sent, "freq", 0, 0, tiled=True)
 
-    spread = pl.pallas_call(
+    spread, sent = pl.pallas_call(
         functools.partial(sum_kernel, width=1024),
-        out_shape=jax.ShapeDtypeStruct((slab_rows, piece), f32),
+        out_shape=[
+            jax.ShapeDtypeStruct((slab_rows, piece), f32),
+            jax.ShapeDtypeStruct((slab_rows, piece + LANES), i16),
+        ],
         in_specs=vmem(1),
-        out_specs=vmem(1)[0],
+        out_specs=vmem(2),
         compiler_params=params(8),
         name="total",
     )(received)
-    spread_below = lax.ppermute(spread, "rows", down)
-    spread_above = lax.ppermute(spread, "rows", up)
+    spread_below = lax.ppermute(sent, "rows", down)
+    spread_above = lax.ppermute(sent, "rows", up)
 
     wide_coded = jax.ShapeDtypeStruct((peers, slab_rows, piece + 3 * LANES), i16)
     result = pl.pallas_call(

time: 127 us -> 126 us (level)
  waiting for transfers between devices: 15.4 us -> 14.1 us
    ppermute x2, waiting for transfers between devices: 3.29 us -> 1.94 us  [the longest x1 1.21 us: layer(): spread_above = lax.ppermute(sent, 'rows', up)]
where the time goes in v10:
time: 126 us; the launch traced here: 125 us
  blocking collectives  59.1 us (47%)
  Pallas kernels  31 us (25%)
  starting transfers between devices  20.4 us (16%)
  waiting for transfers between devices  14.1 us (11%)
    all_to_all x1, blocking collectives, layer(): squares = lax.all_to_all(squares, 'rows', 0, 0, tiled=True)  24.5 us
    all_to_all x1, blocking collectives, layer(): received = lax.all_to_all(sent, 'freq', 0, 0, tiled=True)  18.8 us
    all_to_all x1, blocking collectives, layer(): pieces = lax.all_to_all(result, 'freq', 0, 0, tiled=True)  15.8 us
    pallas_call x1, Pallas kernels, layer(): pl.pallas_call(functools.partial(partial_kernel, stages=peers, whole_rows...  13.2 us
    ppermute x1, waiting for transfers between devices, layer(): edge_below = lax.ppermute(edge, 'rows', down)  12.1 us
    pallas_call x1, Pallas kernels, layer(): pl.pallas_call(functools.partial(element_kernel, width=2048, stages=eleme...  10.5 us
    ppermute x1, starting transfers between devices, layer(): spread_above = lax.ppermute(sent, 'rows', up)  8.1 us
    ppermute x1, starting transfers between devices, layer(): code_below = lax.ppermute(code, 'rows', down)  5.11 us
  transfers between devices with their start and end apart: 5, of which 3 were waited for; matrix products, arithmetic and copies ran while one was open for 0% of the time, Pallas kernels for 8%

profile of v10, /device:TPU:1, one launch (start us, length us, event | category | flops | bytes accessed | tf_op | source)
XLA Modules:
  0.0 125.4 jit_solution(16033560924486727849)
XLA Ops:
  0.0 0.0 copy-start
  0.0 4.6 %prepare.1 = (bf16[4,65536]{1,0:T(4,128)(2,1)}, s16[8,65536]{1,0:T(8,128)(2,1)}) custom-call(bf16[2,1,8,65536]{3,2,1,0:T(8,128)(2,1)} %state_far.3, bf16[2,1,8,65536]{3,2,1,0:T(8,128)(2,1)} %adjoint_far.3, f32[8,65536]{1,0:T(8,128)} %refs_0_.1), custom_call_target="tpu_custom_call" | custom-call | flops 4194304 | bytes 7340032 | tf_op jit(solution)/shard_map/prepare/pallas_call | solution.py:508
  4.6 5.1 %collective-permute-start.1 = (s16[8,65536]{1,0:T(8,128)(2,1)}, s16[8,65536]{1,0:T(8,128)(2,1)}, u32[]{:S(2)}, u32[]{:S(2)}) collective-permute-start(s16[8,65536]{1,0:T(8,128)(2,1)} %get-tuple-element.11), channel_id=1, source_target_pairs={{8,0},{16,8},{24,16},{32,24},{40,32},{48,40},{56,48},{64,56},{72,6... | collective-permute-start | bytes 3145736 | tf_op jit(solution)/shard_map/ppermute | solution.py:525
  9.8 1.9 %collective-permute-start = (s16[8,65536]{1,0:T(8,128)(2,1)}, s16[8,65536]{1,0:T(8,128)(2,1)}, u32[]{:S(2)}, u32[]{:S(2)}) collective-permute-start(s16[8,65536]{1,0:T(8,128)(2,1)} %get-tuple-element.11), channel_id=1, source_target_pairs={{0,8},{8,16},{16,24},{24,32},{32,40},{40,48},{48,56},{56,64},{64,7... | collective-permute-start | bytes 3145736 | tf_op jit(solution)/shard_map/ppermute | solution.py:526
  11.7 3.4 %collective-permute-start.2 = (bf16[4,65536]{1,0:T(4,128)(2,1)}, bf16[4,65536]{1,0:T(4,128)(2,1)S(1)}, u32[]{:S(2)}, u32[]{:S(2)}) collective-permute-start(bf16[4,65536]{1,0:T(4,128)(2,1)} %get-tuple-element.12), channel_id=1, source_target_pairs={{8,0},{16,8},{24,16},{32,24},{40,32},{48,40},{56,48},{64,56},{72,6... | collective-permute-start | bytes 1572872 | tf_op jit(solution)/shard_map/ppermute | solution.py:524
  15.7 12.1 %collective-permute-done.2.edge_far = bf16[4,65536]{1,0:T(4,128)(2,1)S(1)} collective-permute-done((bf16[4,65536]{1,0:T(4,128)(2,1)}, bf16[4,65536]{1,0:T(4,128)(2,1)S(1)}, u32[]{:S(2)}, u32[]{:S(2)}) %collective-permute-start.2) | collective-permute-done | bytes 524320 | tf_op jit(solution)/shard_map/ppermute | solution.py:524
  27.9 0.0 copy-done
  27.9 10.5 %element.1 = (f32[8,65536]{1,0:T(8,128)}, f32[8,65536]{1,0:T(8,128)}) custom-call(f32[8]{0:T(128)S(1)} %copy-done, s32[1]{0:T(128)S(6)} %copy.7.assign, bf16[2,1,8,65536]{3,2,1,0:T(8,128)(2,1)} %state_far.3, bf16[2,1,8,65536]{3,2,1,0:T(8,128)(2,1)} %adjoint_far.3, bf16[4,65536]{1,0:T(4,128)(2,1)S(1)} %collective-permute-done.2.edge_far), custom_call_target="tpu_custom_call" | custom-call | flops 41943040 | bytes 8388608 | tf_op jit(solution)/shard_map/element/pallas_call | solution.py:531
  38.4 0.0 collective-permute-done.1.refs_2_
  38.4 0.0 collective-permute-done.refs_1_
  38.4 13.2 %partial.1 = s16[8,8,8320]{2,1,0:T(8,128)(2,1)} custom-call(s32[1]{0:T(128)} %bitcast.top, f32[8,65536]{1,0:T(8,128)} %refs_0_.1, s16[8,65536]{1,0:T(8,128)(2,1)} %collective-permute-done.refs_1_, s16[8,65536]{1,0:T(8,128)(2,1)} %collective-permute-done.1.refs_2_, s32[8,65536]{1,0:T(8,128)} %refs_3_.1, f32[8,65536]{1,0:T(8,128)} %get-tuple-element.13.refs_4_, ...), custom_call_target="tpu_custom_call" | custom-call | flops 78643200 | bytes 14680064 | tf_op jit(solution)/shard_map/partial/pallas_call | solution.py:547
  51.6 18.8 %all_to_all.15.coded = s16[8,8,8320]{2,1,0:T(8,128)(2,1)S(1)} all-to-all(s16[8,8,8320]{2,1,0:T(8,128)(2,1)} %partial.1), channel_id=1, replica_groups=mesh['rows'=32,'freq'=8] {'freq'}, dimensions={0} | all-to-all | bytes 2129920 | tf_op jit(solution)/shard_map/all_to_all | solution.py:566
  70.4 0.4 total.1
  70.9 1.9 %collective-permute-start.4 = (s16[8,8320]{1,0:T(8,128)(2,1)S(1)}, s16[8,8320]{1,0:T(8,128)(2,1)S(1)}, u32[]{:S(2)}, u32[]{:S(2)}) collective-permute-start(s16[8,8320]{1,0:T(8,128)(2,1)S(1)} %get-tuple-element.15), channel_id=1, source_target_pairs={{8,0},{16,8},{24,16},{32,24},{40,32},{48,40},{56,48},{64,56},{72,6... | collective-permute-start | bytes 399368 | tf_op jit(solution)/shard_map/ppermute | solution.py:579
  72.8 8.1 %collective-permute-start.3 = (s16[8,8320]{1,0:T(8,128)(2,1)S(1)}, s16[8,8320]{1,0:T(8,128)(2,1)S(1)}, u32[]{:S(2)}, u32[]{:S(2)}) collective-permute-start(s16[8,8320]{1,0:T(8,128)(2,1)S(1)} %get-tuple-element.15), channel_id=1, source_target_pairs={{0,8},{8,16},{16,24},{24,32},{32,40},{40,48},{48,56},{56,64},{64,7... | collective-permute-start | bytes 399368 | tf_op jit(solution)/shard_map/ppermute | solution.py:580
  80.9 0.7 collective-permute-done.4.below
  81.6 1.2 collective-permute-done.3.above
  82.8 0.7 back.1
  83.6 15.8 %all_to_all.16.coded = s16[8,8,8576]{2,1,0:T(8,128)(2,1)S(1)} all-to-all(s16[8,8,8576]{2,1,0:T(8,128)(2,1)S(1)} %back.1), channel_id=1, replica_groups=mesh['rows'=32,'freq'=8] {'freq'}, dimensions={0} | all-to-all | bytes 2195456 | tf_op jit(solution)/shard_map/all_to_all | solution.py:593
  99.4 24.5 %all_to_all.17.squares = f32[32,8,128]{2,1,0:T(8,128)S(1)} all-to-all(f32[32,8,128]{2,1,0:T(8,128)S(1)} %squares.1), channel_id=1, replica_groups=mesh['rows'=32,'freq'=8] {'rows'}, dimensions={0} | all-to-all | bytes 262144 | tf_op jit(solution)/shard_map/all_to_all | solution.py:603
  123.9 1.6 %result.1 = f32[8,65536]{1,0:T(8,128)} custom-call(s16[8,8,8576]{2,1,0:T(8,128)(2,1)S(1)} %all_to_all.16.coded, f32[32,8,128]{2,1,0:T(8,128)S(1)} %all_to_all.17.squares), custom_call_target="tpu_custom_call" | custom-call | tf_op jit(solution)/shard_map/result/pallas_call | solution.py:605
  (1 shorter events, 0.0 us)
Async XLA Ops:
  0.0 27.9 %copy-start = (f32[8]{0:T(128)S(1)}, f32[8]{0:T(128)}, u32[]{:S(2)}) copy-start(f32[8]{0:T(128)} %omega_sq.1) | copy-start | bytes 100
  4.6 33.7 %collective-permute-start.1 = (s16[8,65536]{1,0:T(8,128)(2,1)}, s16[8,65536]{1,0:T(8,128)(2,1)}, u32[]{:S(2)}, u32[]{:S(2)}) collective-permute-start(s16[8,65536]{1,0:T(8,128)(2,1)} %get-tuple-element.11), channel_id=1, source_target_pairs={{8,0},{16,8},{24,16},{32,24},{40,32},{48,40},{56,48},{64,56},{72,6... | collective-permute-start | bytes 3145736 | tf_op jit(solution)/shard_map/ppermute | solution.py:525
  9.8 28.6 %collective-permute-start = (s16[8,65536]{1,0:T(8,128)(2,1)}, s16[8,65536]{1,0:T(8,128)(2,1)}, u32[]{:S(2)}, u32[]{:S(2)}) collective-permute-start(s16[8,65536]{1,0:T(8,128)(2,1)} %get-tuple-element.11), channel_id=1, source_target_pairs={{0,8},{8,16},{16,24},{24,32},{32,40},{40,48},{48,56},{56,64},{64,7... | collective-permute-start | bytes 3145736 | tf_op jit(solution)/shard_map/ppermute | solution.py:526
  11.7 16.2 %collective-permute-start.2 = (bf16[4,65536]{1,0:T(4,128)(2,1)}, bf16[4,65536]{1,0:T(4,128)(2,1)S(1)}, u32[]{:S(2)}, u32[]{:S(2)}) collective-permute-start(bf16[4,65536]{1,0:T(4,128)(2,1)} %get-tuple-element.12), channel_id=1, source_target_pairs={{8,0},{16,8},{24,16},{32,24},{40,32},{48,40},{56,48},{64,56},{72,6... | collective-permute-start | bytes 1572872 | tf_op jit(solution)/shard_map/ppermute | solution.py:524
  70.9 10.8 %collective-permute-start.4 = (s16[8,8320]{1,0:T(8,128)(2,1)S(1)}, s16[8,8320]{1,0:T(8,128)(2,1)S(1)}, u32[]{:S(2)}, u32[]{:S(2)}) collective-permute-start(s16[8,8320]{1,0:T(8,128)(2,1)S(1)} %get-tuple-element.15), channel_id=1, source_target_pairs={{8,0},{16,8},{24,16},{32,24},{40,32},{48,40},{56,48},{64,56},{72,6... | collective-permute-start | bytes 399368 | tf_op jit(solution)/shard_map/ppermute | solution.py:579
  72.8 10.1 %collective-permute-start.3 = (s16[8,8320]{1,0:T(8,128)(2,1)S(1)}, s16[8,8320]{1,0:T(8,128)(2,1)S(1)}, u32[]{:S(2)}, u32[]{:S(2)}) collective-permute-start(s16[8,8320]{1,0:T(8,128)(2,1)S(1)} %get-tuple-element.15), channel_id=1, source_target_pairs={{0,8},{8,16},{16,24},{24,32},{32,40},{40,48},{48,56},{56,64},{64,7... | collective-permute-start | bytes 399368 | tf_op jit(solution)/shard_map/ppermute | solution.py:580

commit v11 on v10

--- a/solution.py
+++ b/solution.py
@@ -188,12 +188,16 @@
     width,
     stages,
 ):
-    ids = row_ids(width)
     span = edge.shape[1] // stages
     steps = span // width
-    copies = functools.partial(
-        field_copies, (state_far, adjoint_far), (state, adjoint), arrived, span=span
-    )
+    sent = lax.broadcasted_iota(jnp.int32, (4, width), 0)
+
+    def copies(stage):
+        at = pl.ds(stage * span, span)
+        return [
+            pltpu.make_async_copy(source.at[:, :, 0:2, at], target.at[:, :, :, at], arrived.at[stage, place])
+            for place, (source, target) in enumerate(((state_far, state), (adjoint_far, adjoint)))
+        ]
 
     def load(stage):
         at = pl.ds(stage * span, span)
@@ -204,10 +208,26 @@
         return pltpu.make_async_copy(code.at[:, at], code_far.at[:, at], left.at[stage])
 
     for stage in range(stages):
-        load(stage).start()
-    for stage in range(stages):
         for copy in copies(stage):
             copy.start()
+    for stage in range(stages):
+        load(stage).start()
+
+    for stage in range(stages):
+        for copy in copies(stage):
+            copy.wait()
+
+        def pick_rows(c, none):
+            at = cols(stage * steps + c, width)
+            fields = [state[0, 0, :, at], state[1, 0, :, at], adjoint[0, 0, :, at], adjoint[1, 0, :, at]]
+            picked = jnp.zeros((4, width), f32)
+            for place, field in enumerate(fields):
+                row = jnp.broadcast_to(field.astype(f32)[:1], picked.shape)
+                picked = jnp.where(sent == place, row, picked)
+            edge[:, at] = picked.astype(jnp.bfloat16)
+            return none
+
+        lax.fori_loop(0, steps, pick_rows, 0)
 
     for stage in range(stages):
         load(stage).wait()
@@ -219,21 +239,6 @@
 
         lax.fori_loop(0, steps, encode_rows, 0)
         save(stage).start()
-
-    for stage in range(stages):
-        for copy in copies(stage):
-            copy.wait()
-
-        def pick_rows(c, none):
-            at = cols(stage * steps + c, width)
-            first = state[0, 0, :, at].astype(f32)
-            rows = [state[1, 0, :, at], adjoint[0, 0, :, at], adjoint[1, 0, :, at]]
-            for place, row in enumerate(rows):
-                first = jnp.where(ids == place + 1, pltpu.roll(row.astype(f32), place + 1, 0), first)
-            edge[:, at] = first[:4].astype(jnp.bfloat16)
-            return none
-
-        lax.fori_loop(0, steps, pick_rows, 0)
     for stage in range(stages):
         save(stage).wait()
 
@@ -331,6 +336,7 @@
     peers = out.shape[0]
     piece = design.shape[1] // peers
     narrow = 2048
+    rows_width = 4096
     span = design.shape[1] // stages
 
     def early(stage):
@@ -357,17 +363,17 @@
     clear_ends(spread)
 
     def filter_rows(c, none):
-        at = cols(c, narrow)
+        at = cols(c, rows_width)
         upper = above[:, at].astype(jnp.int32).astype(f32) * (1.0 / DESIGN_STEPS)
         lower = below[:, at].astype(jnp.int32).astype(f32) * (1.0 / DESIGN_STEPS)
-        rowed[:, inner_cols(c, narrow)] = row_filter(upper, design[:, at], lower)
+        rowed[:, inner_cols(c, rows_width)] = row_filter(upper, design[:, at], lower)
         return none
 
     for stage in range(stages):
         for copy in early(stage):
             copy.wait()
-        first = stage * (span // narrow)
-        lax.fori_loop(first, first + span // narrow, filter_rows, 0)
+        first = stage * (span // rows_width)
+        lax.fori_loop(first, first + span // rows_width, filter_rows, 0)
 
     taps = band()
     row = top[0] + row_ids(LANES)
@@ -513,7 +519,10 @@
         ],
         in_specs=[in_place] * 3,
         out_specs=vmem(1) + [in_place],
-        scratch_shapes=field_scratch[:2]
+        scratch_shapes=[
+            pltpu.VMEM((2, 1, 2, width), state.dtype),
+            pltpu.VMEM((2, 1, 2, width), adjoint.dtype),
+        ]
         + design_scratch
         + [field_scratch[2]]
         + [pltpu.SemaphoreType.DMA((stages,))] * 2,

time: 126 us -> 125 us (level)
  no operation moved by 1% of the time
where the time goes in v11:
time: 125 us
  blocking collectives  59.1 us (47%)
  Pallas kernels  30.4 us (24%)
  starting transfers between devices  20.4 us (16%)
  waiting for transfers between devices  14.1 us (11%)
    all_to_all x1, blocking collectives, layer(): squares = lax.all_to_all(squares, 'rows', 0, 0, tiled=True)  24.5 us
    all_to_all x1, blocking collectives, layer(): received = lax.all_to_all(sent, 'freq', 0, 0, tiled=True)  18.8 us
    all_to_all x1, blocking collectives, layer(): pieces = lax.all_to_all(result, 'freq', 0, 0, tiled=True)  15.8 us
    pallas_call x1, Pallas kernels, layer(): pl.pallas_call(functools.partial(partial_kernel, stages=peers, whole_rows...  13 us
    ppermute x1, waiting for transfers between devices, layer(): edge_below = lax.ppermute(edge, 'rows', down)  12.1 us
    pallas_call x1, Pallas kernels, layer(): pl.pallas_call(functools.partial(element_kernel, width=2048, stages=eleme...  10.5 us
    ppermute x1, starting transfers between devices, layer(): spread_above = lax.ppermute(sent, 'rows', up)  8.1 us
    ppermute x1, starting transfers between devices, layer(): code_below = lax.ppermute(code, 'rows', down)  5.11 us
  transfers between devices with their start and end apart: 5, of which 3 were waited for; matrix products, arithmetic and copies ran while one was open for 0% of the time, Pallas kernels for 8%

profile of v11, /device:TPU:1, one launch (start us, length us, event | category | flops | bytes accessed | tf_op | source)
XLA Modules:
  0.0 124.8 jit_solution(10557904393419880853)
XLA Ops:
  0.0 0.0 copy-start
  0.0 4.2 %prepare.1 = (bf16[4,65536]{1,0:T(4,128)(2,1)}, s16[8,65536]{1,0:T(8,128)(2,1)}) custom-call(bf16[2,1,8,65536]{3,2,1,0:T(8,128)(2,1)} %state_far.3, bf16[2,1,8,65536]{3,2,1,0:T(8,128)(2,1)} %adjoint_far.3, f32[8,65536]{1,0:T(8,128)} %refs_0_.1), custom_call_target="tpu_custom_call" | custom-call | flops 4194304 | bytes 7340032 | tf_op jit(solution)/shard_map/prepare/pallas_call | solution.py:514
  4.2 5.1 %collective-permute-start.1 = (s16[8,65536]{1,0:T(8,128)(2,1)}, s16[8,65536]{1,0:T(8,128)(2,1)}, u32[]{:S(2)}, u32[]{:S(2)}) collective-permute-start(s16[8,65536]{1,0:T(8,128)(2,1)} %get-tuple-element.11), channel_id=1, source_target_pairs={{8,0},{16,8},{24,16},{32,24},{40,32},{48,40},{56,48},{64,56},{72,6... | collective-permute-start | bytes 3145736 | tf_op jit(solution)/shard_map/ppermute | solution.py:534
  9.3 1.9 %collective-permute-start = (s16[8,65536]{1,0:T(8,128)(2,1)}, s16[8,65536]{1,0:T(8,128)(2,1)}, u32[]{:S(2)}, u32[]{:S(2)}) collective-permute-start(s16[8,65536]{1,0:T(8,128)(2,1)} %get-tuple-element.11), channel_id=1, source_target_pairs={{0,8},{8,16},{16,24},{24,32},{32,40},{40,48},{48,56},{56,64},{64,7... | collective-permute-start | bytes 3145736 | tf_op jit(solution)/shard_map/ppermute | solution.py:535
  11.3 3.4 %collective-permute-start.2 = (bf16[4,65536]{1,0:T(4,128)(2,1)}, bf16[4,65536]{1,0:T(4,128)(2,1)S(1)}, u32[]{:S(2)}, u32[]{:S(2)}) collective-permute-start(bf16[4,65536]{1,0:T(4,128)(2,1)} %get-tuple-element.12), channel_id=1, source_target_pairs={{8,0},{16,8},{24,16},{32,24},{40,32},{48,40},{56,48},{64,56},{72,6... | collective-permute-start | bytes 1572872 | tf_op jit(solution)/shard_map/ppermute | solution.py:533
  15.3 12.1 %collective-permute-done.2.edge_far = bf16[4,65536]{1,0:T(4,128)(2,1)S(1)} collective-permute-done((bf16[4,65536]{1,0:T(4,128)(2,1)}, bf16[4,65536]{1,0:T(4,128)(2,1)S(1)}, u32[]{:S(2)}, u32[]{:S(2)}) %collective-permute-start.2) | collective-permute-done | bytes 524320 | tf_op jit(solution)/shard_map/ppermute | solution.py:533
  27.4 0.0 copy-done
  27.4 10.5 %element.1 = (f32[8,65536]{1,0:T(8,128)}, f32[8,65536]{1,0:T(8,128)}) custom-call(f32[8]{0:T(128)S(1)} %copy-done, s32[1]{0:T(128)S(6)} %copy.7.assign, bf16[2,1,8,65536]{3,2,1,0:T(8,128)(2,1)} %state_far.3, bf16[2,1,8,65536]{3,2,1,0:T(8,128)(2,1)} %adjoint_far.3, bf16[4,65536]{1,0:T(4,128)(2,1)S(1)} %collective-permute-done.2.edge_far), custom_call_target="tpu_custom_call" | custom-call | flops 41943040 | bytes 8388608 | tf_op jit(solution)/shard_map/element/pallas_call | solution.py:540
  37.9 0.0 collective-permute-done.1.refs_2_
  37.9 0.0 collective-permute-done.refs_1_
  38.0 13.0 %partial.1 = s16[8,8,8320]{2,1,0:T(8,128)(2,1)} custom-call(s32[1]{0:T(128)} %bitcast.top, f32[8,65536]{1,0:T(8,128)} %refs_0_.1, s16[8,65536]{1,0:T(8,128)(2,1)} %collective-permute-done.refs_1_, s16[8,65536]{1,0:T(8,128)(2,1)} %collective-permute-done.1.refs_2_, s32[8,65536]{1,0:T(8,128)} %refs_3_.1, f32[8,65536]{1,0:T(8,128)} %get-tuple-element.13.refs_4_, ...), custom_call_target="tpu_custom_call" | custom-call | flops 78643200 | bytes 14680064 | tf_op jit(solution)/shard_map/partial/pallas_call | solution.py:556
  51.0 18.8 %all_to_all.15.coded = s16[8,8,8320]{2,1,0:T(8,128)(2,1)S(1)} all-to-all(s16[8,8,8320]{2,1,0:T(8,128)(2,1)} %partial.1), channel_id=1, replica_groups=mesh['rows'=32,'freq'=8] {'freq'}, dimensions={0} | all-to-all | bytes 2129920 | tf_op jit(solution)/shard_map/all_to_all | solution.py:575
  69.8 0.4 total.1
  70.3 1.9 %collective-permute-start.4 = (s16[8,8320]{1,0:T(8,128)(2,1)S(1)}, s16[8,8320]{1,0:T(8,128)(2,1)S(1)}, u32[]{:S(2)}, u32[]{:S(2)}) collective-permute-start(s16[8,8320]{1,0:T(8,128)(2,1)S(1)} %get-tuple-element.15), channel_id=1, source_target_pairs={{8,0},{16,8},{24,16},{32,24},{40,32},{48,40},{56,48},{64,56},{72,6... | collective-permute-start | bytes 399368 | tf_op jit(solution)/shard_map/ppermute | solution.py:588
  72.2 8.1 %collective-permute-start.3 = (s16[8,8320]{1,0:T(8,128)(2,1)S(1)}, s16[8,8320]{1,0:T(8,128)(2,1)S(1)}, u32[]{:S(2)}, u32[]{:S(2)}) collective-permute-start(s16[8,8320]{1,0:T(8,128)(2,1)S(1)} %get-tuple-element.15), channel_id=1, source_target_pairs={{0,8},{8,16},{16,24},{24,32},{32,40},{40,48},{48,56},{56,64},{64,7... | collective-permute-start | bytes 399368 | tf_op jit(solution)/shard_map/ppermute | solution.py:589
  80.3 0.7 collective-permute-done.4.below
  81.0 1.2 collective-permute-done.3.above
  82.2 0.7 back.1
  82.9 15.8 %all_to_all.16.coded = s16[8,8,8576]{2,1,0:T(8,128)(2,1)S(1)} all-to-all(s16[8,8,8576]{2,1,0:T(8,128)(2,1)S(1)} %back.1), channel_id=1, replica_groups=mesh['rows'=32,'freq'=8] {'freq'}, dimensions={0} | all-to-all | bytes 2195456 | tf_op jit(solution)/shard_map/all_to_all | solution.py:602
  98.7 24.5 %all_to_all.17.squares = f32[32,8,128]{2,1,0:T(8,128)S(1)} all-to-all(f32[32,8,128]{2,1,0:T(8,128)S(1)} %squares.1), channel_id=1, replica_groups=mesh['rows'=32,'freq'=8] {'rows'}, dimensions={0} | all-to-all | bytes 262144 | tf_op jit(solution)/shard_map/all_to_all | solution.py:612
  123.2 1.6 %result.1 = f32[8,65536]{1,0:T(8,128)} custom-call(s16[8,8,8576]{2,1,0:T(8,128)(2,1)S(1)} %all_to_all.16.coded, f32[32,8,128]{2,1,0:T(8,128)S(1)} %all_to_all.17.squares), custom_call_target="tpu_custom_call" | custom-call | tf_op jit(solution)/shard_map/result/pallas_call | solution.py:614
  (1 shorter events, 0.0 us)
Async XLA Ops:
  0.0 27.4 %copy-start = (f32[8]{0:T(128)S(1)}, f32[8]{0:T(128)}, u32[]{:S(2)}) copy-start(f32[8]{0:T(128)} %omega_sq.1) | copy-start | bytes 100
  4.2 33.7 %collective-permute-start.1 = (s16[8,65536]{1,0:T(8,128)(2,1)}, s16[8,65536]{1,0:T(8,128)(2,1)}, u32[]{:S(2)}, u32[]{:S(2)}) collective-permute-start(s16[8,65536]{1,0:T(8,128)(2,1)} %get-tuple-element.11), channel_id=1, source_target_pairs={{8,0},{16,8},{24,16},{32,24},{40,32},{48,40},{56,48},{64,56},{72,6... | collective-permute-start | bytes 3145736 | tf_op jit(solution)/shard_map/ppermute | solution.py:534
  9.3 28.6 %collective-permute-start = (s16[8,65536]{1,0:T(8,128)(2,1)}, s16[8,65536]{1,0:T(8,128)(2,1)}, u32[]{:S(2)}, u32[]{:S(2)}) collective-permute-start(s16[8,65536]{1,0:T(8,128)(2,1)} %get-tuple-element.11), channel_id=1, source_target_pairs={{0,8},{8,16},{16,24},{24,32},{32,40},{40,48},{48,56},{56,64},{64,7... | collective-permute-start | bytes 3145736 | tf_op jit(solution)/shard_map/ppermute | solution.py:535
  11.3 16.2 %collective-permute-start.2 = (bf16[4,65536]{1,0:T(4,128)(2,1)}, bf16[4,65536]{1,0:T(4,128)(2,1)S(1)}, u32[]{:S(2)}, u32[]{:S(2)}) collective-permute-start(bf16[4,65536]{1,0:T(4,128)(2,1)} %get-tuple-element.12), channel_id=1, source_target_pairs={{8,0},{16,8},{24,16},{32,24},{40,32},{48,40},{56,48},{64,56},{72,6... | collective-permute-start | bytes 1572872 | tf_op jit(solution)/shard_map/ppermute | solution.py:533
  70.3 10.8 %collective-permute-start.4 = (s16[8,8320]{1,0:T(8,128)(2,1)S(1)}, s16[8,8320]{1,0:T(8,128)(2,1)S(1)}, u32[]{:S(2)}, u32[]{:S(2)}) collective-permute-start(s16[8,8320]{1,0:T(8,128)(2,1)S(1)} %get-tuple-element.15), channel_id=1, source_target_pairs={{8,0},{16,8},{24,16},{32,24},{40,32},{48,40},{56,48},{64,56},{72,6... | collective-permute-start | bytes 399368 | tf_op jit(solution)/shard_map/ppermute | solution.py:588
  72.2 10.1 %collective-permute-start.3 = (s16[8,8320]{1,0:T(8,128)(2,1)S(1)}, s16[8,8320]{1,0:T(8,128)(2,1)S(1)}, u32[]{:S(2)}, u32[]{:S(2)}) collective-permute-start(s16[8,8320]{1,0:T(8,128)(2,1)S(1)} %get-tuple-element.15), channel_id=1, source_target_pairs={{0,8},{8,16},{16,24},{24,32},{32,40},{40,48},{48,56},{56,64},{64,7... | collective-permute-start | bytes 399368 | tf_op jit(solution)/shard_map/ppermute | solution.py:589
